TPU v7x, 8 devices: a whole 2x2x1 slice. The times are simulated.
8 devices in a mesh: dp: 1 (over z), y: 2 (over y), x: 4 (over x, core).
Axes of the slice: x: 2, y: 2, z: 1, core: 2. Of those that a mesh axis runs over, the one named last changes fastest.
Arguments:
- tokens: int32 [3, 128], P(None, 'dp')
- lengths: int32 [128], P('dp')
- choices: int32 [3, 128, 2], P(None, 'dp')
- emb_table: bfloat16 [122753, 2304], P(None, 'x')
- k_cache: bfloat16 [128, 128, 36, 64], P('dp', None, 'y')
- v_cache: bfloat16 [128, 128, 36, 64], P('dp', None, 'y')
- g_attn: bfloat16 [2304], P('x')
- w_q: bfloat16 [2304, 2304], P('x', 'y')
- w_k: bfloat16 [2304, 2304], P('x', 'y')
- w_v: bfloat16 [2304, 2304], P('x', 'y')
- w_o: bfloat16 [2304, 2304], P('y', 'x')
- g_ffn: bfloat16 [2304], P('x')
- w_router: bfloat16 [2304, 8], P('x')
- w_act: bfloat16 [8, 2304, 5760], P(None, 'x', 'y')
- w_lin: bfloat16 [8, 2304, 5760], P(None, 'x', 'y')
- w_down: bfloat16 [8, 5760, 2304], P(None, 'y', 'x')
Outputs:
- output 1: bfloat16 [3, 128, 2304], P(None, 'dp', 'x')
- output 2: bfloat16 [128, 128, 36, 64], P('dp', None, 'y')
- output 3: bfloat16 [128, 128, 36, 64], P('dp', None, 'y')
All inputs are finite; a program needn't handle non-finite values.
Results may differ from a plain program's by a relative error of at most 0.012595.
Values are sent between devices in bfloat16 or wider.
A program may use at most 1.5 GiB of HBM per device.

v0:
```python
import jax
import jax.numpy as jnp
from jax import lax
from jax.sharding import PartitionSpec as P

EPS = 1e-5
ROPE_BASE = 1.0e6


def shard_norm(x_val, gain_vec, width_full):
    x_f32 = x_val.astype(jnp.float32)
    sq_total = lax.psum(jnp.sum(x_f32 * x_f32, axis=-1, keepdims=True), 'x')
    return (x_f32 * lax.rsqrt(sq_total / width_full + EPS) * gain_vec.astype(jnp.float32)).astype(jnp.bfloat16)


def rotate(vectors, positions):
    head_dim = vectors.shape[-1]
    half_dim = head_dim // 2
    inv_freq = ROPE_BASE ** (-(jnp.arange(half_dim, dtype=jnp.float32) * 2.0 / head_dim))
    angle_shape = (vectors.shape[0],) + (1,) * (vectors.ndim - 2) + (half_dim,)
    angles = (positions.astype(jnp.float32)[:, None] * inv_freq[None, :]).reshape(angle_shape)
    cosine = jnp.cos(angles)
    sine_val = jnp.sin(angles)
    first_half = vectors[..., :half_dim].astype(jnp.float32)
    second_half = vectors[..., half_dim:].astype(jnp.float32)
    return jnp.concatenate([first_half * cosine - second_half * sine_val, second_half * cosine + first_half * sine_val], axis=-1).astype(jnp.bfloat16)


def write_slot(cache_arr, new_rows, positions):
    hit_mask = (jnp.arange(cache_arr.shape[1])[None, :] == positions[:, None])[:, :, None, None]
    return jnp.where(hit_mask, new_rows[:, None], cache_arr)


def attention(queries, key_cache, val_cache, positions):
    head_dim = queries.shape[-1]
    scores = jnp.einsum('bkgh,bskh->bkgs', queries, key_cache, preferred_element_type=jnp.float32) * head_dim ** -0.5
    valid_mask = (jnp.arange(key_cache.shape[1])[None, :] <= positions[:, None])[:, None, None, :]
    scores = jnp.where(valid_mask, scores, -1.0e30)
    peak_val = jnp.max(scores, axis=-1, keepdims=True)
    weight = jnp.where(valid_mask, jnp.exp(scores - peak_val), 0.0)
    total_w = jnp.sum(weight, axis=-1, keepdims=True)
    mixed_out = jnp.einsum('bkgs,bskh->bkgh', weight.astype(jnp.bfloat16), val_cache, preferred_element_type=jnp.float32)
    return (mixed_out / total_w).astype(jnp.bfloat16)


def mixing(logits, choice_row, experts):
    gate_val = jax.nn.softmax(jnp.take_along_axis(logits, choice_row, axis=1), axis=-1)
    onehot = choice_row[:, :, None] == jnp.arange(experts)[None, None, :]
    return jnp.sum(jnp.where(onehot, gate_val[:, :, None], 0.0), axis=1)


def solution(mesh):
    x_count = mesh.shape['x']
    cache_spec = P('dp', None, 'y', None)
    in_specs = (P(None, 'dp'), P('dp'), P(None, 'dp', None), P(None, 'x'), cache_spec, cache_spec, P('x'), P('x', 'y'), P('x', 'y'), P('x', 'y'), P('y', 'x'), P('x'), P('x', None), P(None, 'x', 'y'), P(None, 'x', 'y'), P(None, 'y', 'x'))
    out_specs = (P(None, 'dp', 'x'), cache_spec, cache_spec)

    def per_device(tokens, lengths, choices, emb_table, k_cache, v_cache, g_attn, w_q, w_k, w_v, w_o, g_ffn, w_router, w_act, w_lin, w_down):
        n_batch = tokens.shape[1]
        kv_local, head_dim = k_cache.shape[2], k_cache.shape[3]
        q_cols = w_q.shape[1]
        kv_cols = w_k.shape[1]
        group_size = q_cols // head_dim // kv_local
        width_full = emb_table.shape[1] * x_count
        experts = w_act.shape[0]
        key_cache, val_cache = k_cache, v_cache
        step_outs = []
        for step_idx in range(tokens.shape[0]):
            positions = lengths + step_idx
            x_in = jnp.take(emb_table, tokens[step_idx], axis=0)
            normed = shard_norm(x_in, g_attn, width_full)
            proj_part = jnp.concatenate([jnp.dot(normed, w_q, preferred_element_type=jnp.float32), jnp.dot(normed, w_k, preferred_element_type=jnp.float32), jnp.dot(normed, w_v, preferred_element_type=jnp.float32)], axis=1).astype(jnp.bfloat16)
            proj_sum = lax.psum(proj_part, 'x')
            queries = rotate(proj_sum[:, :q_cols].reshape(n_batch, kv_local, group_size, head_dim), positions)
            new_keys = rotate(proj_sum[:, q_cols:q_cols + kv_cols].reshape(n_batch, kv_local, head_dim), positions)
            new_vals = proj_sum[:, q_cols + kv_cols:].reshape(n_batch, kv_local, head_dim)
            key_cache = write_slot(key_cache, new_keys, positions)
            val_cache = write_slot(val_cache, new_vals, positions)
            mixed = attention(queries, key_cache, val_cache, positions).reshape(n_batch, q_cols)
            attn_sum = lax.psum(jnp.dot(mixed, w_o, preferred_element_type=jnp.float32).astype(jnp.bfloat16), 'y')
            x_mid = (x_in.astype(jnp.float32) + attn_sum.astype(jnp.float32)).astype(jnp.bfloat16)
            normed2 = shard_norm(x_mid, g_ffn, width_full)
            logits = lax.psum(jnp.dot(normed2, w_router, preferred_element_type=jnp.float32), 'x')
            coef = mixing(logits, choices[step_idx], experts)
            hidden_part = jnp.stack([jnp.einsum('bd,edf->ebf', normed2, w_act, preferred_element_type=jnp.float32), jnp.einsum('bd,edf->ebf', normed2, w_lin, preferred_element_type=jnp.float32)]).astype(jnp.bfloat16)
            hidden_sum = lax.psum(hidden_part, 'x')
            unit_bf16 = (coef.T[:, :, None] * jax.nn.silu(hidden_sum[0].astype(jnp.float32)) * hidden_sum[1].astype(jnp.float32)).astype(jnp.bfloat16)
            moe_sum = lax.psum(jnp.einsum('ebf,efd->bd', unit_bf16, w_down, preferred_element_type=jnp.float32).astype(jnp.bfloat16), 'y')
            step_outs.append((x_mid.astype(jnp.float32) + moe_sum.astype(jnp.float32)).astype(jnp.bfloat16))
        return jnp.stack(step_outs), key_cache, val_cache

    return jax.shard_map(per_device, mesh=mesh, in_specs=in_specs, out_specs=out_specs, check_vma=False)
```

profile of v0, /device:TPU:0, one launch (start us, length us, event | category | flops | bytes accessed | tf_op | source)
XLA Modules:
  0.0 1474.3 jit_solution(4137206433412240630)
XLA Ops:
  8.1 173.3 %copy.85 = bf16[122753,576]{1,0:T(8,128)(2,1)} copy(bf16[122753,576]{0,1:T(8,128)(2,1)} %param.23) | data formatting | bytes 282822912 | tf_op args[3]
  181.4 2.0 gather_fusion
  183.5 2.0 gather_fusion.2
  185.7 2.0 gather_fusion.4
  188.2 8.7 all-reduce.2
  202.2 1.0 pad_maximum_fusion.3
  203.2 1.0 pad_maximum_fusion.4
  204.2 1.0 pad_maximum_fusion.5
  206.4 53.8 %all-reduce.14.cloned.1.call-done = (bf16[128,3456]{1,0:T(8,128)(2,1)}, bf16[128,3456]{1,0:T(8,128)(2,1)}, bf16[128,3456]{1,0:T(8,128)(2,1)}) async-done(((bf16[128,3456]{1,0:T(8,128)(2,1)}, bf16[128,3456]{1,0:T(8,128)(2,1)}, bf16[128,3456]{1,0:T(8,128)(2,1)}), (bf16[128,3456]{1,0:T(8,128)(2,1)}, bf16[128,3456]{1,0:T(8,128)(2,1)}, bf16[128,3456]{1,0:T(8,128)(2,1)})) %all-reduce.14.cloned.1.call-update) | async-done | bytes 2654224 | tf_op jit(solution)/shard_map/psum | solution.py:73
  260.2 1.2 fusion.199
  261.7 2.4 copy.112
  264.1 2.0 fusion.200
  267.9 24.2 %fusion.3 = f32[128,18,1,128]{3,2,1,0:T(1,128)S(1)} fusion(bf16[128,18,64,1]{2,3,1,0:T(2,128)(2,1)} %copy.112, bf16[128,128,18,64]{1,3,2,0:T(8,128)(2,1)} %param.24, pred[128,128]{1,0:T(8,128)(4,1)S(1)} %get-tuple-element.94, bf16[128,18,64]{2,1,0:T(8,128)(2,1)S(1)} %copy.89), kind=kOutput, calls=%fused_computation.15 | convolution fusion | flops 56623104 | bytes 39534592 | tf_op jit(solution)/shard_map/bkgh,bskh->bkgs/dot_general | solution.py:36
  292.5 1.0 fusion.196
  294.2 26.6 %fusion.4 = f32[128,18,1,64]{3,2,1,0:T(1,128)} fusion(bf16[128,128,18,64]{1,3,2,0:T(8,128)(2,1)} %param.25, pred[128,128]{1,0:T(8,128)(4,1)} %copy-done.16, bf16[128,18,64]{2,1,0:T(8,128)(2,1)S(1)} %copy.91, bf16[128,18,128,1]{2,0,1,3:T(8,128)(2,1)S(1)} %get-tuple-element.45), kind=kOutput, calls=%fused_computation.16 | convolution fusion | flops 56623104 | bytes 39239680 | tf_op jit(solution)/shard_map/bkgs,bskh->bkgh/dot_general | solution.py:42
  320.8 2.6 copy.115
  323.7 2.0 fusion.201
  326.9 2.2 copy.116
  329.1 0.9 pad_maximum_fusion.8
  330.5 46.5 %fusion.5 = f32[128,18,1,128]{3,2,1,0:T(1,128)S(1)} fusion(bf16[128,18,64,1]{2,3,1,0:T(2,128)(2,1)} %copy.116, pred[128,128]{1,0:T(8,128)(4,1)S(1)} %copy-done.21, bf16[128,128,18,64]{1,3,2,0:T(8,128)(2,1)} %param.24, pred[128,128]{1,0:T(8,128)(4,1)S(1)} %copy-done.17, bf16[128,18,64]{2,1,0:T(8,128)(2,1)S(1)} %copy.98, bf16[128,18,64]{2,1,0:T(8,128)(2,1)S(1)} %copy.89), kind=kOutput, calls=%fused_computation.17 | convolution fusion | flops 75497472 | bytes 39845888 | tf_op jit(solution)/shard_map/bkgh,bskh->bkgs/dot_general | solution.py:36
  377.4 1.8 fusion.197
  379.3 1.2 copy.99
  380.5 1.3 copy.100
  381.7 47.2 %fusion.6 = f32[128,18,1,64]{3,2,1,0:T(1,128)} fusion(pred[128,128]{1,0:T(8,128)(4,1)S(1)} %copy-done.22, bf16[128,128,18,64]{1,3,2,0:T(8,128)(2,1)} %param.25, pred[128,128]{1,0:T(8,128)(4,1)S(1)} %copy-done.18, bf16[128,18,64]{2,1,0:T(8,128)(2,1)} %copy.100, bf16[128,18,64]{2,1,0:T(8,128)(2,1)S(1)} %copy.91, bf16[128,18,128,1]{2,0,1,3:T(8,128)(2,1)} %get-tuple-element.47), kind=kOutput, calls=%fused_computation.18 | convolution fusion | flops 75497472 | bytes 39550976 | tf_op jit(solution)/shard_map/bkgs,bskh->bkgh/dot_general | solution.py:42
  428.9 3.6 copy.119
  433.3 1.2 convolution_convert_fusion.11
  434.5 1.1 fusion.78
  435.6 1.2 convolution_convert_fusion.10
  436.8 1.7 maximum_bitcast_fusion.2
  438.5 3.8 copy.120
  443.2 1.1 fusion.110
  444.3 1.3 copy.107
  445.8 1.3 copy.109
  447.1 128.0 %broadcast_select_fusion.1 = (bf16[128,128,18,64]{1,3,2,0:T(8,128)(2,1)}, bf16[128,128,18,64]{1,3,2,0:T(8,128)(2,1)}) fusion(pred[128,128]{1,0:T(8,128)(4,1)S(1)} %copy-done.20, bf16[128,128,18,64]{1,3,2,0:T(8,128)(2,1)} %param.24, pred[128,128]{1,0:T(8,128)(4,1)S(1)} %copy-done.18, pred[128,128]{1,0:T(8,128)(4,1)} %get-tuple-element.108, ...), kind=kLoop, calls=%fused_computation.10 | loop fusion | flops 113246208 | bytes 152813568 | tf_op jit(solution)/shard_map/jit(_where)/select_n | solution.py:31
  575.1 17.1 %fusion.203 = f32[128,18,1,128]{3,2,1,0:T(1,128)S(1)} fusion(bf16[128,18,64,1]{2,3,1,0:T(2,128)(2,1)} %copy.120, bf16[128,128,18,64]{1,3,2,0:T(8,128)(2,1)} %get-tuple-element.71), kind=kOutput, calls=%fused_computation.325 | convolution fusion | flops 37748736 | bytes 39223296 | tf_op jit(solution)/shard_map/bkgh,bskh->bkgs/dot_general | solution.py:36
  593.1 24.4 %fusion.49 = f32[128,18,1,64]{3,2,1,0:T(1,128)S(1)} fusion(bf16[128,128,18,64]{1,3,2,0:T(8,128)(2,1)} %get-tuple-element.72, bf16[128,18,128,1]{2,0,1,3:T(8,128)(2,1)S(1)} %get-tuple-element.49), kind=kOutput, calls=%fused_computation.91 | convolution fusion | flops 37748736 | bytes 38928384 | tf_op jit(solution)/shard_map/bkgs,bskh->bkgh/dot_general | solution.py:42
  617.5 1.2 copy.123
  618.8 1.2 convolution_convert_fusion.9
  620.8 20.6 %all-reduce.18.cloned.1.call-done = (bf16[128,576]{0,1:T(8,128)(2,1)}, bf16[128,576]{0,1:T(8,128)(2,1)}, bf16[128,576]{0,1:T(8,128)(2,1)}) async-done(((bf16[128,576]{0,1:T(8,128)(2,1)}, bf16[128,576]{0,1:T(8,128)(2,1)}, bf16[128,576]{0,1:T(8,128)(2,1)}), (bf16[128,576]{0,1:T(8,128)(2,1)}, bf16[128,576]{0,1:T(8,128)(2,1)}, bf16[128,576]{0,1:T(8,128)(2,1)})) %all-reduce.18.cloned.1.call-update) | async-done | bytes 442384 | tf_op jit(solution)/shard_map/psum | solution.py:80
  641.4 1.0 fusion.117
  642.4 1.0 fusion.125
  643.4 1.0 fusion.133
  644.4 6.8 all-reduce.1
  651.3 18.6 %convert_bitcast_fusion.5 = bf16[1,8,128,2880]{2,3,1,0:T(8,128)(2,1)S(1)} fusion(bf16[8,576,2880]{2,1,0:T(8,128)(2,1)} %param.33, bf16[128,576]{0,1:T(8,128)(2,1)S(1)} %get-tuple-element.33, f32[576]{0:T(1024)S(1)} %convert_element_type.270, f32[128]{0:T(128)S(1)} %rsqrt_bitcast_fusion.4), kind=kOutput, calls=%fused_computation.63 | convolution fusion | flops 3400630272 | bytes 32590592 | tf_op jit(solution)/shard_map/bd,edf->ebf/dot_general | solution.py:85
  669.9 21.3 %convert_bitcast_fusion.4 = bf16[1,8,128,2880]{2,3,1,0:T(8,128)(2,1)} fusion(bf16[8,576,2880]{2,1,0:T(8,128)(2,1)} %param.34, bf16[128,576]{0,1:T(8,128)(2,1)S(1)} %get-tuple-element.33, f32[576]{0:T(1024)S(1)} %convert_element_type.270, f32[128]{0:T(128)S(1)} %rsqrt_bitcast_fusion.4), kind=kOutput, calls=%fused_computation.62 | convolution fusion | flops 3400630272 | bytes 32590592 | tf_op jit(solution)/shard_map/bd,edf->ebf/dot_general | solution.py:85
  691.2 21.3 %convert_bitcast_fusion.3 = bf16[1,8,128,2880]{2,3,1,0:T(8,128)(2,1)} fusion(bf16[8,576,2880]{2,1,0:T(8,128)(2,1)} %param.33, bf16[128,576]{0,1:T(8,128)(2,1)S(1)} %get-tuple-element.35, f32[128]{0:T(128)S(1)} %rsqrt_bitcast_fusion.2, f32[576]{0:T(1024)S(1)} %convert_element_type.270), kind=kOutput, calls=%fused_computation.61 | convolution fusion | flops 3400630272 | bytes 32590592 | tf_op jit(solution)/shard_map/bd,edf->ebf/dot_general | solution.py:85
  712.5 21.2 %convert_bitcast_fusion.2 = bf16[1,8,128,2880]{2,3,1,0:T(8,128)(2,1)} fusion(bf16[8,576,2880]{2,1,0:T(8,128)(2,1)} %param.34, bf16[128,576]{0,1:T(8,128)(2,1)S(1)} %get-tuple-element.35, f32[128]{0:T(128)S(1)} %rsqrt_bitcast_fusion.2, f32[576]{0:T(1024)S(1)} %convert_element_type.270), kind=kOutput, calls=%fused_computation.60 | convolution fusion | flops 3400630272 | bytes 32590592 | tf_op jit(solution)/shard_map/bd,edf->ebf/dot_general | solution.py:85
  733.7 21.5 %convert_bitcast_fusion.1 = bf16[1,8,128,2880]{2,3,1,0:T(8,128)(2,1)} fusion(bf16[8,576,2880]{2,1,0:T(8,128)(2,1)} %param.33, bf16[128,576]{0,1:T(8,128)(2,1)S(1)} %get-tuple-element.37, f32[128]{0:T(128)S(1)} %rsqrt_bitcast_fusion, f32[576]{0:T(1024)S(1)} %convert_element_type.270), kind=kOutput, calls=%fused_computation.59 | convolution fusion | flops 3400630272 | bytes 32590592 | tf_op jit(solution)/shard_map/bd,edf->ebf/dot_general | solution.py:85
  755.2 21.2 %convert_bitcast_fusion = bf16[1,8,128,2880]{2,3,1,0:T(8,128)(2,1)} fusion(bf16[8,576,2880]{2,1,0:T(8,128)(2,1)} %param.34, bf16[128,576]{0,1:T(8,128)(2,1)S(1)} %get-tuple-element.37, f32[128]{0:T(128)S(1)} %rsqrt_bitcast_fusion, f32[576]{0:T(1024)S(1)} %convert_element_type.270), kind=kOutput, calls=%fused_computation.58 | convolution fusion | flops 3400630272 | bytes 32590592 | tf_op jit(solution)/shard_map/bd,edf->ebf/dot_general | solution.py:85
  776.4 10.8 pad_maximum_fusion
  787.2 8.3 pad_maximum_fusion.1
  795.6 5.1 pad_maximum_fusion.2
  802.9 11.3 all-reduce
  814.2 1.4 gather_fusion.3
  815.8 1.4 gather_fusion.5
  817.4 1.6 gather_fusion.1
  819.3 562.9 %all-reduce.12.cloned.1.call-done = (bf16[2,8,128,2880]{2,3,1,0:T(8,128)(2,1)}, bf16[2,8,128,2880]{2,3,1,0:T(8,128)(2,1)}, bf16[2,8,128,2880]{2,3,1,0:T(8,128)(2,1)}) async-done(((bf16[2,8,128,2880]{2,3,1,0:T(8,128)(2,1)}, bf16[2,8,128,2880]{2,3,1,0:T(8,128)(2,1)}, bf16[2,8,128,2880]{2,3,1,0:T(8,128)(2,1)}), (bf16[2,8,128,2880]{2,3,1,0:T(8,128)(2,1)}, bf16[2,8,128,2880]{2,3,1,0:T(8,128)(2,1)}, ...) | async-done | bytes 35389456 | tf_op jit(solution)/shard_map/psum | solution.py:86
  1382.2 20.0 %fusion.62 = bf16[128,576]{0,1:T(8,128)(2,1)} fusion(bf16[8,2880,576]{1,2,0:T(8,128)(2,1)} %param.35, bf16[2,8,128,2880]{2,3,1,0:T(8,128)(2,1)} %get-tuple-element.16, f32[8,128]{1,0:T(8,128)S(1)} %bitcast.299), kind=kOutput, calls=%fused_computation.98 | convolution fusion | flops 3424002048 | bytes 38490112 | tf_op jit(solution)/shard_map/ebf,efd->bd/dot_general | solution.py:88
  1402.2 20.2 %fusion.65 = bf16[128,576]{0,1:T(8,128)(2,1)} fusion(bf16[8,2880,576]{1,2,0:T(8,128)(2,1)} %param.35, bf16[2,8,128,2880]{2,3,1,0:T(8,128)(2,1)} %get-tuple-element.15, f32[8,128]{1,0:T(8,128)S(1)} %bitcast.300), kind=kOutput, calls=%fused_computation.99 | convolution fusion | flops 3424002048 | bytes 38490112 | tf_op jit(solution)/shard_map/ebf,efd->bd/dot_general | solution.py:88
  1422.4 20.0 %fusion.68 = bf16[128,576]{0,1:T(8,128)(2,1)} fusion(bf16[8,2880,576]{1,2,0:T(8,128)(2,1)} %param.35, bf16[2,8,128,2880]{2,3,1,0:T(8,128)(2,1)} %get-tuple-element.14, f32[8,128]{1,0:T(8,128)S(1)} %bitcast.301), kind=kOutput, calls=%fused_computation.100 | convolution fusion | flops 3424002048 | bytes 38490112 | tf_op jit(solution)/shard_map/ebf,efd->bd/dot_general | solution.py:88
  1442.4 21.5 %all-reduce.16.cloned.1.call-done = (bf16[128,576]{0,1:T(8,128)(2,1)}, bf16[128,576]{0,1:T(8,128)(2,1)}, bf16[128,576]{0,1:T(8,128)(2,1)}) async-done(((bf16[128,576]{0,1:T(8,128)(2,1)}, bf16[128,576]{0,1:T(8,128)(2,1)}, bf16[128,576]{0,1:T(8,128)(2,1)}), (bf16[128,576]{0,1:T(8,128)(2,1)}, bf16[128,576]{0,1:T(8,128)(2,1)}, bf16[128,576]{0,1:T(8,128)(2,1)})) %all-reduce.16.cloned.1.call-update) | async-done | bytes 442384 | tf_op jit(solution)/shard_map/psum | solution.py:88
  1463.9 0.9 fusion.139
  1464.9 1.0 fusion.138
  1465.8 1.0 fusion.137
  (166 shorter events, 20.8 us)
Async XLA Ops:
  7.2 189.8 %copy-start = (bf16[576,1152]{1,0:T(8,128)(2,1)S(1)}, bf16[576,1152]{1,0:T(8,128)(2,1)}, u32[]{:S(2)}) copy-start(bf16[576,1152]{1,0:T(8,128)(2,1)} %param.27) | copy-start | bytes 3981316
  7.2 253.0 %all-reduce.14.cloned.1.call-start = ((), (), s32[]{:S(2)}) async-start(), calls=%async_computation.1 | async-start | bytes 5308416 | tf_op jit(solution)/shard_map/psum | solution.py:73
  8.1 191.2 %copy-start.28 = (pred[128]{0:T(512)(128)(4,1)}, pred[128]{0:T(512)(128)(4,1)S(1)}, u32[]{:S(2)}) copy-start(pred[128]{0:T(512)(128)(4,1)S(1)} %get-tuple-element.38) | copy-start | bytes 388
  8.1 191.8 %copy-start.27 = (pred[128]{0:T(512)(128)(4,1)}, pred[128]{0:T(512)(128)(4,1)S(1)}, u32[]{:S(2)}) copy-start(pred[128]{0:T(512)(128)(4,1)S(1)} %get-tuple-element.85) | copy-start | bytes 388
  8.1 193.5 %copy-start.25 = (pred[128]{0:T(512)(128)(4,1)}, pred[128]{0:T(512)(128)(4,1)S(1)}, u32[]{:S(2)}) copy-start(pred[128]{0:T(512)(128)(4,1)S(1)} %get-tuple-element.83) | copy-start | bytes 388
  8.1 188.8 %copy-start.30 = (bf16[576]{0:T(1024)(128)(2,1)S(1)}, bf16[576]{0:T(1024)(128)(2,1)}, u32[]{:S(2)}) copy-start(bf16[576]{0:T(1024)(128)(2,1)} %param.26) | copy-start | bytes 3460
  181.4 16.2 %copy-start.4 = (bf16[576,1152]{1,0:T(8,128)(2,1)S(1)}, bf16[576,1152]{1,0:T(8,128)(2,1)}, u32[]{:S(2)}) copy-start(bf16[576,1152]{1,0:T(8,128)(2,1)} %param.28) | copy-start | bytes 3981316
  183.5 16.3 %copy-start.6 = (bf16[128,576]{0,1:T(8,128)(2,1)}, bf16[128,576]{0,1:T(8,128)(2,1)S(1)}, u32[]{:S(2)}) copy-start(bf16[128,576]{0,1:T(8,128)(2,1)S(1)} %copy.86) | copy-start | bytes 442372
  185.7 14.7 copy-start.8
  187.9 13.7 copy-start.10
  196.9 2.4 copy-start.5
  201.0 4.2 copy-start.29
  205.2 436.2 %all-reduce.18.cloned.1.call-start = ((), (), s32[]{:S(2)}) async-start(), calls=%async_computation.3 | async-start | bytes 884736 | tf_op jit(solution)/shard_map/psum | solution.py:80
  205.4 86.7 %copy-start.16 = (pred[128,128]{1,0:T(8,128)(4,1)}, pred[128,128]{1,0:T(8,128)(4,1)S(1)}, u32[]{:S(2)}) copy-start(pred[128,128]{1,0:T(8,128)(4,1)S(1)} %get-tuple-element.94) | copy-start | bytes 49156
  294.2 29.2 %copy-start.15 = (bf16[128,1152]{1,0:T(8,128)(2,1)S(1)}, bf16[128,1152]{1,0:T(8,128)(2,1)}, u32[]{:S(2)}) copy-start(bf16[128,1152]{1,0:T(8,128)(2,1)} %get-tuple-element.53) | copy-start | bytes 884740
  320.8 9.7 copy-start.17
  320.8 9.7 copy-start.21
  330.5 46.5 %copy-start.12 = (bf16[128,18,64]{2,1,0:T(8,128)(2,1)}, bf16[128,18,64]{2,1,0:T(8,128)(2,1)S(1)}, u32[]{:S(2)}) copy-start(bf16[128,18,64]{2,1,0:T(8,128)(2,1)S(1)} %copy.98) | copy-start | bytes 884740
  330.5 46.5 %copy-start.23 = (pred[128,128]{1,0:T(8,128)(4,1)S(1)}, pred[128,128]{1,0:T(8,128)(4,1)}, u32[]{:S(2)}) copy-start(pred[128,128]{1,0:T(8,128)(4,1)} %get-tuple-element.109) | copy-start | bytes 49156
  330.5 51.2 %copy-start.18 = (pred[128,128]{1,0:T(8,128)(4,1)S(1)}, pred[128,128]{1,0:T(8,128)(4,1)}, u32[]{:S(2)}) copy-start(pred[128,128]{1,0:T(8,128)(4,1)} %copy-done.16) | copy-start | bytes 49156
  330.5 51.2 %copy-start.22 = (pred[128,128]{1,0:T(8,128)(4,1)S(1)}, pred[128,128]{1,0:T(8,128)(4,1)}, u32[]{:S(2)}) copy-start(pred[128,128]{1,0:T(8,128)(4,1)} %get-tuple-element.108) | copy-start | bytes 49156
  381.7 51.5 %copy-start.3 = (bf16[1152,576]{0,1:T(8,128)(2,1)S(1)}, bf16[1152,576]{0,1:T(8,128)(2,1)}, u32[]{:S(2)}) copy-start(bf16[1152,576]{0,1:T(8,128)(2,1)} %param.30) | copy-start | bytes 3981316
  432.4 14.6 copy-start.20
  433.2 9.1 copy-start.14
  433.2 12.3 copy-start.13
  575.1 17.1 %copy-start.19 = (pred[128,128]{1,0:T(8,128)(4,1)S(1)}, pred[128,128]{1,0:T(8,128)(4,1)}, u32[]{:S(2)}) copy-start(pred[128,128]{1,0:T(8,128)(4,1)} %get-tuple-element.97) | copy-start | bytes 49156
  593.1 48.3 %copy-start.7 = (bf16[128,576]{0,1:T(8,128)(2,1)S(1)}, bf16[128,576]{0,1:T(8,128)(2,1)}, u32[]{:S(2)}) copy-start(bf16[128,576]{0,1:T(8,128)(2,1)} %copy-done.6) | copy-start | bytes 442372
  593.1 49.3 %copy-start.9 = (bf16[128,576]{0,1:T(8,128)(2,1)S(1)}, bf16[128,576]{0,1:T(8,128)(2,1)}, u32[]{:S(2)}) copy-start(bf16[128,576]{0,1:T(8,128)(2,1)} %copy-done.8) | copy-start | bytes 442372
  593.1 50.3 %copy-start.11 = (bf16[128,576]{0,1:T(8,128)(2,1)S(1)}, bf16[128,576]{0,1:T(8,128)(2,1)}, u32[]{:S(2)}) copy-start(bf16[128,576]{0,1:T(8,128)(2,1)} %copy-done.10) | copy-start | bytes 442372
  593.1 50.3 %copy-start.26 = (pred[128]{0:T(512)(128)(4,1)S(1)}, pred[128]{0:T(512)(128)(4,1)}, u32[]{:S(2)}) copy-start(pred[128]{0:T(512)(128)(4,1)} %copy-done.25) | copy-start | bytes 388
  620.0 762.2 %all-reduce.12.cloned.1.call-start = ((), (), s32[]{:S(2)}) async-start(), calls=%async_computation | async-start | bytes 70778880 | tf_op jit(solution)/shard_map/psum | solution.py:86
  776.4 10.8 copy-start.2
  776.4 19.1 %slice-start = ((s8[5898240]{0:T(1024)(128)(4,1)}), s8[4194304]{0:T(1024)(128)(4,1)S(1)}, s32[]{:S(2)}) async-start(s8[5898240]{0:T(1024)(128)(4,1)} %bitcast.283), calls=%async_computation.4 | async-start | bytes 8388608
  776.4 19.1 %slice-start.2 = ((s8[5898240]{0:T(1024)(128)(4,1)}), s8[4194304]{0:T(1024)(128)(4,1)S(1)}, s32[]{:S(2)}) async-start(s8[5898240]{0:T(1024)(128)(4,1)} %bitcast.285), calls=%async_computation.6 | async-start | bytes 8388608
  787.2 8.4 slice-start.1
  787.2 8.4 slice-start.3
  800.7 0.7 copy-start.24
  800.7 1.5 copy-start.31
  800.7 663.2 %all-reduce.16.cloned.1.call-start = ((), (), s32[]{:S(2)}) async-start(), calls=%async_computation.2 | async-start | bytes 884736 | tf_op jit(solution)/shard_map/psum | solution.py:88
  1422.4 45.2 %copy-start.1 = (bf16[576,1152]{1,0:T(8,128)(2,1)S(1)}, bf16[576,1152]{1,0:T(8,128)(2,1)}, u32[]{:S(2)}) copy-start(bf16[576,1152]{1,0:T(8,128)(2,1)} %param.27) | copy-start | bytes 3981316
Sparse Core Ops, SparseCore 0:
  205.3 54.8 all-reduce.13
  620.1 21.1 all-reduce.17
  800.8 581.3 all-reduce.11
  1442.5 21.3 all-reduce.15
where the time goes:
time: 1490 us; the launch traced here: 1470 us
  waiting for transfers between devices  659 us (44%)
  matrix products  381 us (26%)
  local copies, waits for them, and re-layouts  216 us (14%)
  other arithmetic  177 us (12%)
  blocking collectives  26.9 us (2%)
    psum x1, waiting for transfers between devices, per_device(): hidden_sum = lax.psum(hidden_part, 'x')  563 us
    unnamed x73, local copies, waits for them, and re-layouts  174 us
    select_n x1, other arithmetic, write_slot(): return jnp.where(hit_mask, new_rows[:, None], cache_arr)  128 us
    dot_general x3, matrix products, attention(): jnp.einsum('bkgs,bskh->bkgh', weight.astype(jnp.bfloat16), val_cache, pre...  98.2 us
    dot_general x3, matrix products, attention(): jnp.einsum('bkgh,bskh->bkgs', queries, key_cache, preferred_element_type=...  87.7 us
    dot_general x3, matrix products, per_device(): jnp.einsum('bd,edf->ebf', normed2, w_lin, preferred_element_type=jnp.floa...  63.7 us
    dot_general x3, matrix products, per_device(): jnp.einsum('bd,edf->ebf', normed2, w_act, preferred_element_type=jnp.floa...  61.4 us
    dot_general x3, matrix products, per_device(): jnp.einsum('ebf,efd->bd', unit_bf16, w_down, preferred_element_type=jnp.f...  60.2 us
  transfers between devices with their start and end apart: 4, of which 4 were waited for; matrix products, arithmetic and copies ran while one was open for 1% of the time, Pallas kernels for 0%

commit v1 on v0

v1 whole, which is shorter than its diff:
```python
import functools
import jax
import jax.numpy as jnp
from jax import lax
from jax.experimental import pallas as pl
from jax.experimental.pallas import tpu as pltpu
from jax.sharding import PartitionSpec as P

EPS = 1e-5
ROPE_BASE = 1.0e6
LANES = 128
GROUP = 8
SLOTS = 4
TILE = 128
VMEM_BYTES = 60 * 1024 * 1024
CORE_PERM = [(0, 1), (1, 0), (2, 3), (3, 2)]
CHIP_PERM = [(0, 2), (2, 0), (1, 3), (3, 1)]
F32 = jnp.float32
BF16 = jnp.bfloat16


def params(**kw):
    return pltpu.CompilerParams(vmem_limit_bytes=VMEM_BYTES, **kw)


def gather_rows(tokens, emb_table):
    n_tok = tokens.shape[0]
    vocab, width = emb_table.shape
    last_tile = vocab // LANES - 1
    tail_at = (last_tile + 1) * LANES
    n_tail = vocab - tail_at
    n_groups = n_tok // GROUP
    per_chunk = LANES // GROUP

    def kernel(tok_s, tokv_ref, tail_ref, emb_ref, out_ref, sq_ref, buf, acc, sems):
        def copy(g, i):
            tile = jnp.minimum(tok_s[g * GROUP + i] // LANES, last_tile)
            slot = lax.rem(g, SLOTS)
            return pltpu.make_async_copy(
                emb_ref.at[:, pl.ds(pl.multiple_of(tile * LANES, LANES), LANES)],
                buf.at[slot, :, pl.ds(i * LANES, LANES)], sems.at[slot, i])

        def start(g):
            for i in range(GROUP):
                copy(g, i).start()

        for g in range(SLOTS - 1):
            start(g)
        lane_id = lax.broadcasted_iota(jnp.int32, (LANES, LANES), 0)
        col_id = lax.broadcasted_iota(jnp.int32, (LANES, LANES), 1)

        def step(g, carry):
            @pl.when(g + SLOTS - 1 < n_groups)
            def _():
                start(g + SLOTS - 1)
            for i in range(GROUP):
                copy(g, i).wait()
            slot = lax.rem(g, SLOTS)
            chunk = g // per_chunk
            base = lax.rem(g, per_chunk) * GROUP
            picks = []
            for i in range(GROUP):
                tok = tok_s[g * GROUP + i]
                lane = jnp.where(tok < tail_at, lax.rem(tok, LANES), -1)
                picks.append(((lane_id == lane) & (col_id == base + i)).astype(F32).astype(BF16))
            part = jnp.dot(buf[slot], jnp.concatenate(picks, axis=0), preferred_element_type=F32)

            @pl.when(base == 0)
            def _():
                acc[chunk] = part

            @pl.when(base != 0)
            def _():
                acc[chunk] += part
            return carry

        lax.fori_loop(0, n_groups, step, 0)
        for c in range(n_tok // LANES):
            rows = jnp.transpose(acc[c])
            tok_col = tokv_ref[pl.ds(c * LANES, LANES), :]
            for k in range(n_tail):
                rows = jnp.where(tok_col == tail_at + k, tail_ref[pl.ds(k, 1), :].astype(F32), rows)
            out_ref[pl.ds(c * LANES, LANES), :] = rows.astype(BF16)
            sq_ref[pl.ds(c * LANES, LANES), :] = jnp.sum(rows * rows, axis=1, keepdims=True)

    return pl.pallas_call(
        kernel,
        out_shape=(jax.ShapeDtypeStruct((n_tok, width), BF16), jax.ShapeDtypeStruct((n_tok, 1), F32)),
        grid_spec=pltpu.PrefetchScalarGridSpec(
            num_scalar_prefetch=1, grid=(),
            in_specs=[pl.BlockSpec(memory_space=pltpu.VMEM), pl.BlockSpec(memory_space=pltpu.VMEM), pl.BlockSpec(memory_space=pl.ANY)],
            out_specs=[pl.BlockSpec(memory_space=pltpu.VMEM)] * 2,
            scratch_shapes=[pltpu.VMEM((SLOTS, width, GROUP * LANES), BF16), pltpu.VMEM((n_tok // LANES, width, LANES), F32), pltpu.SemaphoreType.DMA((SLOTS, GROUP))]),
        compiler_params=params(),
        cost_estimate=pl.CostEstimate(flops=2 * n_tok * width * LANES * LANES, bytes_accessed=n_tok * width * LANES * 2, transcendentals=0),
        name="gather_rows",
    )(tokens, tokens[:, None], emb_table[tail_at:], emb_table.T)


def put_columns(block, columns, pick, hit):
    new = jnp.dot(columns, pick, preferred_element_type=F32)
    return jnp.where(hit, new.astype(BF16), block)


def column_scratch(rows_ref, out_ref):
    rows = rows_ref[...].astype(F32)
    pad = jnp.zeros((LANES - rows.shape[0], rows.shape[1]), F32)
    out_ref[...] = jnp.transpose(jnp.concatenate([rows, pad], axis=0)).astype(BF16)


def slot_masks(pos, row_local, per_q, steps, shape):
    col = lax.broadcasted_iota(jnp.int32, (LANES, shape[1]), 0)
    slot = lax.broadcasted_iota(jnp.int32, (LANES, shape[1]), 1)
    t = col // per_q
    pick = ((lax.rem(col, per_q) == row_local) & (slot == pos + t) & (t < steps)).astype(F32).astype(BF16)
    lane = lax.broadcasted_iota(jnp.int32, shape, 1)
    hit = (lane >= pos) & (lane < pos + steps)
    return pick, hit


def attend_quarter(quarter, lengths, q_rows, k_rows, v_rows, k_cache, v_cache, heads, steps):
    batch, kv_width, slots = k_cache.shape
    per_q = q_rows.shape[0] // steps
    head = kv_width // heads
    h_pad = (heads + 7) // 8 * 8
    step_b = 4
    n_grid = per_q // step_b

    def kernel(qi, len_s, q_ref, kr_ref, vr_ref, kc_ref, vc_ref, o_ref, ko_ref, vo_ref, k_cols, v_cols):
        g = pl.program_id(0)

        @pl.when(g == 0)
        def _():
            column_scratch(kr_ref, k_cols)
            column_scratch(vr_ref, v_cols)
        row_h = lax.broadcasted_iota(jnp.int32, (h_pad, kv_width), 0)
        col_h = lax.broadcasted_iota(jnp.int32, (h_pad, kv_width), 1) // head
        diag = row_h == col_h
        srow_t = lax.broadcasted_iota(jnp.int32, (steps * h_pad, slots), 0) // h_pad
        scol = lax.broadcasted_iota(jnp.int32, (steps * h_pad, slots), 1)
        for i in range(step_b):
            bl = g * step_b + i
            pos = len_s[qi[0] * per_q + bl]
            pick, hit = slot_masks(pos, bl, per_q, steps, (kv_width, slots))
            keys = put_columns(kc_ref[i], k_cols[...], pick, hit)
            vals = put_columns(vc_ref[i], v_cols[...], pick, hit)
            ko_ref[i] = keys
            vo_ref[i] = vals
            wide = jnp.concatenate([jnp.where(diag, q_ref[pl.ds(t * per_q + bl, 1), :], 0.0) for t in range(steps)], axis=0).astype(BF16)
            s = jnp.dot(wide, keys, preferred_element_type=F32) * head ** -0.5
            ok = scol <= pos + srow_t
            s = jnp.where(ok, s, -1.0e30)
            e = jnp.where(ok, jnp.exp(s - jnp.max(s, axis=1, keepdims=True)), 0.0)
            total = jnp.sum(e, axis=1, keepdims=True)
            mix = lax.dot_general(e.astype(BF16), vals, (((1,), (1,)), ((), ())), preferred_element_type=F32) / total
            for t in range(steps):
                piece = jnp.where(diag, mix[t * h_pad:(t + 1) * h_pad], 0.0)
                o_ref[pl.ds(t * per_q + bl, 1), :] = jnp.sum(piece, axis=0, keepdims=True)

    cache_in = pl.BlockSpec((step_b, kv_width, slots), lambda g, qi, ln: (qi[0] * n_grid + g, 0, 0))
    whole = lambda a: pl.BlockSpec(a.shape, lambda g, qi, ln: (0, 0))
    return pl.pallas_call(
        kernel,
        out_shape=(jax.ShapeDtypeStruct(q_rows.shape, F32), jax.ShapeDtypeStruct(k_cache.shape, BF16), jax.ShapeDtypeStruct(v_cache.shape, BF16)),
        grid_spec=pltpu.PrefetchScalarGridSpec(
            num_scalar_prefetch=2, grid=(n_grid,),
            in_specs=[whole(q_rows), whole(k_rows), whole(v_rows), cache_in, cache_in],
            out_specs=[pl.BlockSpec(q_rows.shape, lambda g, qi, ln: (0, 0)), cache_in, cache_in],
            scratch_shapes=[pltpu.VMEM((kv_width, LANES), BF16)] * 2),
        compiler_params=params(),
        cost_estimate=pl.CostEstimate(flops=4 * per_q * kv_width * LANES * LANES, bytes_accessed=8 * per_q * kv_width * slots, transcendentals=0),
        name="attend_quarter",
    )(quarter, lengths, q_rows, k_rows, v_rows, k_cache, v_cache)


def copy_quarter(quarter, lengths, k_rows, v_rows, k_cache, v_cache, k_out, v_out, steps):
    batch, kv_width, slots = k_cache.shape
    per_q = k_rows.shape[0] // steps
    step_b = 4
    n_grid = per_q // step_b

    def kernel(qi, len_s, kr_ref, vr_ref, kc_ref, vc_ref, ka_ref, va_ref, ko_ref, vo_ref, k_cols, v_cols):
        g = pl.program_id(0)

        @pl.when(g == 0)
        def _():
            column_scratch(kr_ref, k_cols)
            column_scratch(vr_ref, v_cols)
        for i in range(step_b):
            bl = g * step_b + i
            pos = len_s[qi[0] * per_q + bl]
            pick, hit = slot_masks(pos, bl, per_q, steps, (kv_width, slots))
            ko_ref[i] = put_columns(kc_ref[i], k_cols[...], pick, hit)
            vo_ref[i] = put_columns(vc_ref[i], v_cols[...], pick, hit)

    cache_in = pl.BlockSpec((step_b, kv_width, slots), lambda g, qi, ln: (qi[0] * n_grid + g, 0, 0))
    whole = lambda a: pl.BlockSpec(a.shape, lambda g, qi, ln: (0, 0))
    anyspec = pl.BlockSpec(memory_space=pl.ANY)
    return pl.pallas_call(
        kernel,
        out_shape=(jax.ShapeDtypeStruct(k_cache.shape, BF16), jax.ShapeDtypeStruct(v_cache.shape, BF16)),
        grid_spec=pltpu.PrefetchScalarGridSpec(
            num_scalar_prefetch=2, grid=(n_grid,),
            in_specs=[whole(k_rows), whole(v_rows), cache_in, cache_in, anyspec, anyspec],
            out_specs=[cache_in, cache_in],
            scratch_shapes=[pltpu.VMEM((kv_width, LANES), BF16)] * 2),
        input_output_aliases={6: 0, 7: 1},
        compiler_params=params(),
        cost_estimate=pl.CostEstimate(flops=4 * per_q * kv_width * LANES * LANES, bytes_accessed=8 * per_q * kv_width * slots, transcendentals=0),
        name="copy_quarter",
    )(quarter, lengths, k_rows, v_rows, k_cache, v_cache, k_out, v_out)


def expert_tiles(off_s, e, body):
    lo, hi = off_s[e], off_s[e + 1]
    first = lo // 16 * 16
    n_tiles = jnp.where(hi > lo, (hi - first + TILE - 1) // TILE, 0)

    def step(i, carry):
        at = pl.multiple_of(first + i * TILE, 16)
        row = at + lax.broadcasted_iota(jnp.int32, (TILE, 1), 0)
        body(pl.ds(at, TILE), (row >= lo) & (row < hi))
        return carry
    lax.fori_loop(0, n_tiles, step, 0)


def up_experts(offsets, rows, w_act, w_lin, chunk, size, block):
    n_rows, depth = rows.shape
    experts = w_act.shape[0]

    def kernel(off_s, x_ref, a_ref, l_ref, out_ref):
        e = pl.program_id(0)

        def body(ds, mine):
            x = x_ref[ds, :]
            for k, w_ref in enumerate((a_ref, l_ref)):
                y = jnp.dot(x, w_ref[0, :, :size], preferred_element_type=F32)
                out_ref[k, ds, :] = jnp.where(mine, y.astype(BF16), out_ref[k, ds, :])
        expert_tiles(off_s, e, body)

    w_spec = pl.BlockSpec((1, depth, block), lambda e, off: (e, 0, chunk))
    return pl.pallas_call(
        kernel,
        out_shape=jax.ShapeDtypeStruct((2, n_rows, size), BF16),
        grid_spec=pltpu.PrefetchScalarGridSpec(
            num_scalar_prefetch=1, grid=(experts,),
            in_specs=[pl.BlockSpec(rows.shape, lambda e, off: (0, 0)), w_spec, w_spec],
            out_specs=pl.BlockSpec((2, n_rows, size), lambda e, off: (0, 0, 0))),
        compiler_params=params(),
        cost_estimate=pl.CostEstimate(flops=8 * TILE * experts * depth * size, bytes_accessed=4 * experts * depth * size, transcendentals=0),
        name="up_experts",
    )(offsets, rows, w_act, w_lin)


def down_experts(offsets, units, w_down_t, pos_a, pos_b):
    n_rows, depth = units.shape
    experts, width, _ = w_down_t.shape
    n_tok = pos_a.shape[0]

    def kernel(off_s, u_ref, w_ref, pa_ref, pb_ref, out_ref, acc):
        e = pl.program_id(0)

        @pl.when(e == 0)
        def _():
            acc[...] = jnp.zeros_like(acc)

        def body(ds, mine):
            y = lax.dot_general(u_ref[ds, :], w_ref[0], (((1,), (1,)), ((), ())), preferred_element_type=F32)
            acc[ds, :] = jnp.where(mine, y, acc[ds, :])
        expert_tiles(off_s, e, body)

        @pl.when(e == experts - 1)
        def _():
            col = lax.broadcasted_iota(jnp.int32, (n_tok, n_rows), 1)
            pick = ((col == pa_ref[...]) | (col == pb_ref[...])).astype(F32).astype(BF16)
            y = acc[...]
            high = y.astype(BF16)
            low = (y - high.astype(F32)).astype(BF16)
            out_ref[...] = (jnp.dot(pick, high, preferred_element_type=F32) + jnp.dot(pick, low, preferred_element_type=F32)).astype(BF16)

    whole = lambda a: pl.BlockSpec(a.shape, lambda e, off: (0, 0))
    return pl.pallas_call(
        kernel,
        out_shape=jax.ShapeDtypeStruct((n_tok, width), BF16),
        grid_spec=pltpu.PrefetchScalarGridSpec(
            num_scalar_prefetch=1, grid=(experts,),
            in_specs=[whole(units), pl.BlockSpec((1, width, depth), lambda e, off: (e, 0, 0)), whole(pos_a), whole(pos_b)],
            out_specs=pl.BlockSpec((n_tok, width), lambda e, off: (0, 0)),
            scratch_shapes=[pltpu.VMEM((n_rows, width), F32)]),
        compiler_params=params(),
        cost_estimate=pl.CostEstimate(flops=4 * TILE * experts * depth * width, bytes_accessed=2 * experts * depth * width, transcendentals=0),
        name="down_experts",
    )(offsets, units, w_down_t, pos_a, pos_b)


def solution(mesh):
    x_count = mesh.shape['x']
    cache_spec = P('dp', None, 'y', None)
    in_specs = (P(None, 'dp'), P('dp'), P(None, 'dp', None), P(None, 'x'), cache_spec, cache_spec, P('x'), P('x', 'y'), P('x', 'y'), P('x', 'y'), P('y', 'x'), P('x'), P('x', None), P(None, 'x', 'y'), P(None, 'x', 'y'), P(None, 'y', 'x'))
    out_specs = (P(None, 'dp', 'x'), cache_spec, cache_spec)

    def over_core(v):
        return lax.ppermute(v, 'x', CORE_PERM)

    def over_chip(v):
        return lax.ppermute(v, 'x', CHIP_PERM)

    def per_device(tokens, lengths, choices, emb_table, k_cache, v_cache, g_attn, w_q, w_k, w_v, w_o, g_ffn, w_router, w_act, w_lin, w_down):
        steps, n_batch = tokens.shape
        heads, head = k_cache.shape[2], k_cache.shape[3]
        kv_width = heads * head
        width = emb_table.shape[1]
        width_full = width * x_count
        experts, _, ff = w_act.shape
        n_tok = steps * n_batch
        per_q = n_batch // x_count
        q_rows_n = steps * per_q
        xi = lax.axis_index('x')
        core = lax.rem(xi, 2)
        chip = xi // 2
        order = jnp.array([0, 2, 1, 3], jnp.int32)
        rel = lax.bitwise_xor(order, xi)
        back = order[lax.bitwise_xor(jnp.arange(x_count, dtype=jnp.int32), xi)]

        def to_rel(a):
            a = a.reshape((steps, x_count, per_q) + a.shape[2:])
            return jnp.moveaxis(a, 1, 0)[rel].reshape((n_tok,) + a.shape[3:])

        def norm(rows, sq, gain):
            sq_abs = sq.reshape(x_count, q_rows_n)[back]
            total = lax.psum(sq_abs, 'x')[rel].reshape(n_tok, 1)
            return (rows.astype(F32) * lax.rsqrt(total / width_full + EPS) * gain.astype(F32)).astype(BF16)

        tok_rel = to_rel(tokens)
        flat = choices.reshape(n_tok * 2)
        hot = (flat[:, None] == jnp.arange(experts)[None, :])
        lower = (lax.broadcasted_iota(jnp.int32, (2 * n_tok, 2 * n_tok), 0) > lax.broadcasted_iota(jnp.int32, (2 * n_tok, 2 * n_tok), 1)).astype(BF16)
        before = jnp.dot(lower, hot.astype(BF16), preferred_element_type=F32).astype(jnp.int32)
        counts = jnp.sum(hot.astype(jnp.int32), axis=0)
        first = jnp.sum(jnp.where(jnp.arange(experts)[:, None] > jnp.arange(experts)[None, :], counts[None, :], 0), axis=1)
        offsets = jnp.concatenate([first, jnp.full((1,), 2 * n_tok, jnp.int32)])
        place = jnp.sum(jnp.where(hot, before + first[None, :], 0), axis=1).reshape(steps, n_batch, 2)
        pos_a = to_rel(place[:, :, 0])
        pos_b = to_rel(place[:, :, 1])
        choice_a = to_rel(choices[:, :, 0])
        choice_b = to_rel(choices[:, :, 1])

        x_in, sq_in = gather_rows(tok_rel, emb_table)
        h = norm(x_in, sq_in, g_attn)
        part = jnp.concatenate([jnp.dot(h, w, preferred_element_type=F32) for w in (w_q, w_k, w_v)], axis=1).astype(BF16)
        half = n_tok // 2
        got = over_core(part[half:])
        part = (part[:half].astype(F32) + got.astype(F32)).astype(BF16)
        got = over_chip(part[q_rows_n:])
        proj = (part[:q_rows_n].astype(F32) + got.astype(F32)).astype(BF16).astype(F32)
        len_q = lax.dynamic_slice(lengths, (xi * per_q,), (per_q,))
        positions = (len_q[None, :] + jnp.arange(steps)[:, None]).reshape(q_rows_n).astype(F32)
        inv_freq = ROPE_BASE ** (-(jnp.arange(head // 2, dtype=F32) * 2.0 / head))
        angles = jnp.tile(positions[:, None] * inv_freq[None, :], (1, 2 * heads))
        cosine, sine = jnp.cos(angles), jnp.sin(angles)
        low_half = (jnp.arange(kv_width) % head < head // 2)[None, :]

        def rotate(v):
            other = jnp.where(low_half, -jnp.roll(v, -(head // 2), axis=1), jnp.roll(v, head // 2, axis=1))
            return (v * cosine + other * sine).astype(BF16)

        queries = rotate(proj[:, :kv_width]).astype(F32)
        kv_new = jnp.concatenate([rotate(proj[:, kv_width:2 * kv_width]), proj[:, 2 * kv_width:].astype(BF16)], axis=1)
        k_view = k_cache.transpose(0, 2, 3, 1).reshape(n_batch, kv_width, -1)
        v_view = v_cache.transpose(0, 2, 3, 1).reshape(n_batch, kv_width, -1)
        mixed, k_out, v_out = attend_quarter(xi[None], lengths, queries, kv_new[:, :kv_width], kv_new[:, kv_width:], k_view, v_view, heads, steps)
        mixed = mixed.astype(BF16)
        mixed2 = jnp.concatenate([mixed, over_chip(mixed)], axis=0)
        mixed4 = jnp.concatenate([mixed2, over_core(mixed2)], axis=0)
        attn = jnp.dot(mixed4, w_o, preferred_element_type=F32).astype(BF16)
        attn_sum = attn.astype(F32) + lax.ppermute(attn, 'y', [(0, 1), (1, 0)]).astype(F32)
        x_mid = (x_in.astype(F32) + attn_sum).astype(BF16)

        kv_pair = jnp.stack([kv_new, over_chip(kv_new)])
        kv_far = over_core(kv_pair)

        x_mid32 = x_mid.astype(F32)
        h2 = norm(x_mid, jnp.sum(x_mid32 * x_mid32, axis=1, keepdims=True), g_ffn)
        r_part = jnp.dot(h2, w_router, preferred_element_type=F32)
        logits = lax.psum(r_part.reshape(x_count, q_rows_n, experts)[back], 'x')[rel].reshape(n_tok, experts)
        eid = jnp.arange(experts)[None, :]
        pair = jnp.stack([jnp.sum(jnp.where(choice_a[:, None] == eid, logits, 0.0), axis=1), jnp.sum(jnp.where(choice_b[:, None] == eid, logits, 0.0), axis=1)], axis=1)
        gates = jax.nn.softmax(pair, axis=-1)
        n_pair = 2 * n_tok
        quarter = n_pair // x_count
        own_row = (xi * quarter + jnp.arange(quarter))[:, None]
        coef = jnp.sum(jnp.where(pos_a[None, :] == own_row, gates[None, :, 0], 0.0) + jnp.where(pos_b[None, :] == own_row, gates[None, :, 1], 0.0), axis=1, keepdims=True)
        n_rows = n_pair + TILE
        row_id = jnp.arange(n_rows)[:, None]
        sort_rows = ((pos_a[None, :] == row_id) | (pos_b[None, :] == row_id)).astype(BF16)
        sorted_h = jnp.dot(sort_rows, h2, preferred_element_type=F32).astype(BF16)

        block = 1536
        sizes = [block, ff - block]
        units = []
        for c, size in enumerate(sizes):
            first_part = up_experts(offsets, sorted_h, w_act, w_lin, c, size, block)[:, :n_pair].reshape(2, 2, 2, quarter, size)
            keep = lax.dynamic_index_in_dim(first_part, core, 2, keepdims=False)
            send = lax.dynamic_index_in_dim(first_part, 1 - core, 2, keepdims=False)
            summed = (keep.astype(F32) + over_core(send).astype(F32)).astype(BF16)
            keep = lax.dynamic_index_in_dim(summed, chip, 1, keepdims=False)
            send = lax.dynamic_index_in_dim(summed, 1 - chip, 1, keepdims=False)
            act, lin = (v for v in (keep.astype(F32) + over_chip(send).astype(F32)).astype(BF16).astype(F32))
            unit = (coef * jax.nn.silu(act) * lin).astype(BF16)
            both = lax.dynamic_update_index_in_dim(jnp.stack([over_chip(unit)] * 2), unit, chip, 0)
            far = over_core(both)
            units.append(jnp.where(core == 0, jnp.stack([both, far], axis=1), jnp.stack([far, both], axis=1)).reshape(n_pair, size))
        unit_all = jnp.pad(jnp.concatenate(units, axis=1), ((0, TILE), (0, 0)))

        for rows, idx in ((kv_pair[1], 2), (kv_far[0], 1), (kv_far[1], 3)):
            k_out, v_out = copy_quarter(lax.bitwise_xor(xi, idx)[None], lengths, rows[:, :kv_width], rows[:, kv_width:], k_view, v_view, k_out, v_out, steps)

        moe = down_experts(offsets, unit_all, w_down.transpose(0, 2, 1), pos_a[:, None], pos_b[:, None])
        moe_sum = moe.astype(F32) + lax.ppermute(moe, 'y', [(0, 1), (1, 0)]).astype(F32)
        out = (x_mid32 + moe_sum).astype(BF16)
        out = jnp.moveaxis(out.reshape(x_count, steps, per_q, width)[back], 0, 1).reshape(steps, n_batch, width)

        def to_cache(v):
            return v.reshape(n_batch, heads, head, -1).transpose(0, 3, 1, 2)
        return out, to_cache(k_out), to_cache(v_out)

    return jax.shard_map(per_device, mesh=mesh, in_specs=in_specs, out_specs=out_specs, check_vma=False)
```

time: 1490 us -> 366 us (0.25)
  waiting for transfers between devices: 659 us -> 96 us
  matrix products: 381 us -> 8.9 us
  local copies, waits for them, and re-layouts: 216 us -> 35 us
  Pallas kernels: 0 us -> 167 us
  other arithmetic: 177 us -> 21.8 us
    psum x4 -> x0, waiting for transfers between devices: 659 us -> none  [the longest x1 563 us: per_device(): hidden_sum = lax.psum(hidden_part, 'x')]
    dot_general x30 -> x7, matrix products: 381 us -> 8.9 us  [the longest x3 3.99 us: per_device(): jnp.dot(h, w, preferred_element_type=F32)]
    unnamed x73 -> x33, local copies, waits for them, and re-layouts: 174 us -> 3.26 us
    pallas_call x0 -> x8, Pallas kernels: none -> 167 us  [the longest x3 54.3 us: copy_quarter(): pl.pallas_call(kernel, out_shape=(jax.ShapeDtypeStruct(k_cache.shape, BF1...]
    select_n x1 -> x5, other arithmetic: 128 us -> 1.57 us  [the longest x2 0.8 us: per_device(): jnp.where(core == 0, jnp.stack([both, far], axis=1), jnp.stack([far, both...]
    ppermute x0 -> x16, waiting for transfers between devices: none -> 96 us  [the longest x7 88.3 us: over_chip(): return lax.ppermute(v, 'x', CHIP_PERM)]
    another operation x9 -> x4, other arithmetic: 29.8 us -> 1.32 us  [the longest x2 1.1 us: per_device(): kv_pair = jnp.stack([kv_new, over_chip(kv_new)])]
  transfers between devices with their start and end apart: 4 -> 16, of which waited for: 4 -> 11; matrix products, arithmetic and copies ran while one was open for 1% -> 9% of each run, Pallas kernels for 0% -> 24%
where the time goes in v1:
time: 366 us; the launch traced here: 364 us
  Pallas kernels  167 us (46%)
  waiting for transfers between devices  96 us (26%)
  local copies, waits for them, and re-layouts  35 us (10%)
  blocking collectives  25.2 us (7%)
  other arithmetic  21.8 us (6%)
  starting transfers between devices  9.55 us (3%)
  matrix products  8.9 us (2%)
    ppermute x7, waiting for transfers between devices, over_chip(): return lax.ppermute(v, 'x', CHIP_PERM)  88.3 us
    pallas_call x3, Pallas kernels, copy_quarter(): pl.pallas_call(kernel, out_shape=(jax.ShapeDtypeStruct(k_cache.shape, BF1...  54.3 us
    pallas_call x2, Pallas kernels, up_experts(): pl.pallas_call(kernel, out_shape=jax.ShapeDtypeStruct((2, n_rows, size),...  34.7 us
    pallas_call x1, Pallas kernels, gather_rows(): pl.pallas_call(kernel, out_shape=(jax.ShapeDtypeStruct((n_tok, width), BF...  32.8 us
    pallas_call x1, Pallas kernels, attend_quarter(): pl.pallas_call(kernel, out_shape=(jax.ShapeDtypeStruct(q_rows.shape, F32)...  23.8 us
    pallas_call x1, Pallas kernels, down_experts(): pl.pallas_call(kernel, out_shape=jax.ShapeDtypeStruct((n_tok, width), BF1...  21.2 us
    psum x2, blocking collectives, norm(): total = lax.psum(sq_abs, 'x')[rel].reshape(n_tok, 1)  14.7 us
    psum x1, blocking collectives, per_device(): lax.psum(r_part.reshape(x_count, q_rows_n, experts)[back], 'x')[rel]  10.5 us
  transfers between devices with their start and end apart: 16, of which 11 were waited for; matrix products, arithmetic and copies ran while one was open for 9% of the time, Pallas kernels for 24%

profile of v1, /device:TPU:0, one launch (start us, length us, event | category | flops | bytes accessed | tf_op | source)
XLA Modules:
  0.0 364.2 jit_solution(2971617356601457392)
XLA Ops:
  0.7 0.8 compare_select_fusion.2
  1.4 0.8 reshape.249
  3.4 0.9 broadcast_in_dim_reshape.9.tokv_ref
  4.3 1.3 gather_fusion.1
  5.6 0.7 convert_element_type.167
  6.3 0.9 slice.109
  7.2 0.7 copy.103.tail_ref
  7.9 32.8 %gather_rows.1 = (bf16[384,576]{1,0:T(8,128)(2,1)}, f32[384,1]{1,0:T(8,128)}) custom-call(s32[384]{0:T(512)} %reshape.250.tok_s, s32[384,1]{1,0:T(8,128)} %broadcast_in_dim_reshape.9.tokv_ref, bf16[1,576]{1,0:T(2,128)(2,1)} %copy.103.tail_ref, bf16[576,122753]{1,0:T(8,128)(2,1)} %bitcast.1.emb_ref), custom_call_target="tpu_custom_call" | custom-call | flops 7247757312 | bytes 56623104 | tf_op jit(solution)/shard_map/gather_rows/pallas_call | solution.py:86
  40.8 1.2 reduce.4
  42.6 8.7 %psum.21 = f32[4,96]{1,0:T(4,128)S(1)} all-reduce(f32[4,96]{1,0:T(4,128)S(1)} %gather_fusion.2), channel_id=1, replica_groups=mesh['dp'=1,'y'=2,'x'=4] {'x'}, use_global_device_ids=true, to_apply=%region_0.1 | all-reduce | flops 384 | bytes 3072 | tf_op jit(solution)/shard_map/psum | solution.py:331
  52.0 2.0 convolution_convert_fusion.1
  54.1 1.0 convolution_convert_fusion
  55.4 1.0 convolution_convert_fusion.2
  56.6 1.2 slice.168
  58.3 2.4 collective-permute-done
  60.7 1.6 add_convert_fusion
  62.4 1.1 copy-done.2
  63.4 0.9 slice.170
  66.1 15.2 %collective-permute-done.1 = bf16[96,3456]{1,0:T(8,128)(2,1)} collective-permute-done((bf16[96,3456]{1,0:T(8,128)(2,1)}, bf16[96,3456]{1,0:T(8,128)(2,1)}, u32[]{:S(2)}, u32[]{:S(2)}) %collective-permute-start.1) | collective-permute-done | bytes 663584 | tf_op jit(solution)/shard_map/ppermute | solution.py:306
  81.3 1.2 fusion.69
  82.7 0.7 slice.181.vr_ref
  83.6 1.2 fusion.43
  84.8 23.8 %attend_quarter.1 = (f32[96,1152]{1,0:T(8,128)}, bf16[128,1152,128]{2,1,0:T(8,128)(2,1)}, bf16[128,1152,128]{2,1,0:T(8,128)(2,1)}) custom-call(s32[1]{0:T(128)} %bitcast.2.qi, s32[128]{0:T(128)} %len_s.7, f32[96,1152]{1,0:T(8,128)} %get-tuple-element.51.q_ref, bf16[96,1152]{1,0:T(8,128)(2,1)} %get-tuple-element.50.kr_ref, bf16[96,1152]{1,0:T(8,128)(2,1)} %slice.181.vr_ref, ...), custom_call_target="tpu_custom_call" | custom-call | flops 2415919104 | bytes 37748736 | tf_op jit(solution)/shard_map/attend_quarter/pallas_call | solution.py:162
  108.6 1.1 convert_element_type.181
  111.1 0.9 broadcast_in_dim_reshape.21.pb_ref
  112.8 0.9 broadcast_in_dim_reshape.20.pa_ref
  115.2 1.3 collective-permute-done.2
  117.1 1.3 collective-permute-done.3
  118.4 2.3 convolution_convert_fusion.4
  120.7 1.5 collective-permute-start.4
  122.2 0.7 pad_add_fusion.off_s
  122.9 6.4 %collective-permute-done.14 = bf16[96,2304]{1,0:T(8,128)(2,1)S(1)} collective-permute-done((bf16[96,2304]{1,0:T(8,128)(2,1)S(1)}, bf16[96,2304]{1,0:T(8,128)(2,1)S(1)}, u32[]{:S(2)}, u32[]{:S(2)}) %collective-permute-start.14) | collective-permute-done | bytes 442400 | tf_op jit(solution)/shard_map/ppermute | solution.py:306
  129.3 1.0 pad_maximum_fusion.3
  130.3 3.7 %collective-permute-done.4 = bf16[384,576]{1,0:T(8,128)(2,1)S(1)} collective-permute-done((bf16[384,576]{1,0:T(8,128)(2,1)S(1)}, bf16[384,576]{1,0:T(8,128)(2,1)S(1)}, u32[]{:S(2)}, u32[]{:S(2)}) %collective-permute-start.4) | collective-permute-done | bytes 442400 | tf_op jit(solution)/shard_map/ppermute | solution.py:376
  134.9 6.0 %psum.22 = f32[4,96]{1,0:T(4,128)S(1)} all-reduce(f32[4,96]{1,0:T(4,128)S(1)} %gather_fusion.6), channel_id=1, replica_groups=mesh['dp'=1,'y'=2,'x'=4] {'x'}, use_global_device_ids=true, to_apply=%region_5.6 | all-reduce | flops 384 | bytes 3072 | tf_op jit(solution)/shard_map/psum | solution.py:331
  141.6 2.0 convolution_convert_fusion.3.x_ref
  143.6 17.0 %up_experts.3 = bf16[2,896,1344]{2,1,0:T(8,128)(2,1)} custom-call(s32[9]{0:T(128)} %pad_add_fusion.off_s, bf16[896,576]{1,0:T(8,128)(2,1)} %convolution_convert_fusion.3.x_ref, bf16[8,576,2880]{2,1,0:T(8,128)(2,1)} %a_ref.3, bf16[8,576,2880]{2,1,0:T(8,128)(2,1)} %l_ref.3), custom_call_target="tpu_custom_call" | custom-call | flops 6341787648 | bytes 24772608 | tf_op jit(solution)/shard_map/up_experts/pallas_call | solution.py:242
  160.6 2.2 slice-done.1
  162.8 1.7 constant_dynamic-slice_fusion.1
  164.5 1.5 copy.120
  166.0 17.7 %up_experts.2 = bf16[2,896,1536]{2,1,0:T(8,128)(2,1)} custom-call(s32[9]{0:T(128)} %pad_add_fusion.off_s, bf16[896,576]{1,0:T(8,128)(2,1)} %convolution_convert_fusion.3.x_ref, bf16[8,576,2880]{2,1,0:T(8,128)(2,1)} %a_ref.3, bf16[8,576,2880]{2,1,0:T(8,128)(2,1)} %l_ref.3), custom_call_target="tpu_custom_call" | custom-call | flops 7247757312 | bytes 28311552 | tf_op jit(solution)/shard_map/up_experts/pallas_call | solution.py:242
  183.7 2.3 slice-done
  186.3 1.6 copy.119
  188.4 0.8 fusion.72
  189.2 18.1 %copy_quarter.3 = (bf16[128,1152,128]{2,1,0:T(8,128)(2,1)}, bf16[128,1152,128]{2,1,0:T(8,128)(2,1)}) custom-call(s32[1]{0:T(128)} %bitcast.50.qi, s32[128]{0:T(128)} %len_s.7, bf16[96,1152]{1,0:T(8,128)(2,1)} %get-tuple-element.63.kr_ref, bf16[96,1152]{1,0:T(8,128)(2,1)} %get-tuple-element.62.vr_ref, ...), custom_call_target="tpu_custom_call", output_to_operand_aliasing={{0}: (6, {}), {1}: (7, {})} | custom-call | flops 2415919104 | bytes 37748736 | tf_op jit(solution)/shard_map/copy_quarter/pallas_call | solution.py:199
  208.3 10.5 %psum.23 = f32[4,96,8]{1,2,0:T(8,128)S(1)} all-reduce(f32[4,96,8]{1,2,0:T(8,128)S(1)} %gather_fusion.8), channel_id=1, replica_groups=mesh['dp'=1,'y'=2,'x'=4] {'x'}, use_global_device_ids=true, to_apply=%region_6.7 | all-reduce | flops 3072 | bytes 24576 | tf_op jit(solution)/shard_map/psum | solution.py:385
  219.7 2.8 fusion.4
  222.6 1.3 collective-permute-start.10
  223.8 2.3 fusion.3
  226.2 0.8 collective-permute-start.6
  227.2 22.1 %collective-permute-done.10 = bf16[2,192,1344]{2,1,0:T(8,128)(2,1)S(1)} collective-permute-done((bf16[2,192,1344]{2,1,0:T(8,128)(2,1)S(1)}, bf16[2,192,1344]{2,1,0:T(8,128)(2,1)S(1)}, u32[]{:S(2)}, u32[]{:S(2)}) %collective-permute-start.10) | collective-permute-done | bytes 1032224 | tf_op jit(solution)/shard_map/ppermute | solution.py:306
  249.9 1.3 collective-permute-start.11
  251.2 23.4 %collective-permute-done.6 = bf16[2,192,1536]{2,1,0:T(8,128)(2,1)S(1)} collective-permute-done((bf16[2,192,1536]{2,1,0:T(8,128)(2,1)S(1)}, bf16[2,192,1536]{2,1,0:T(8,128)(2,1)S(1)}, u32[]{:S(2)}, u32[]{:S(2)}) %collective-permute-start.6) | collective-permute-done | bytes 1179680 | tf_op jit(solution)/shard_map/ppermute | solution.py:306
  275.3 1.3 collective-permute-start.7
  276.6 9.6 %collective-permute-done.11 = bf16[192,1344]{1,0:T(8,128)(2,1)S(1)} collective-permute-done((bf16[192,1344]{1,0:T(8,128)(2,1)S(1)}, bf16[192,1344]{1,0:T(8,128)(2,1)S(1)}, u32[]{:S(2)}, u32[]{:S(2)}) %collective-permute-start.11) | collective-permute-done | bytes 516128 | tf_op jit(solution)/shard_map/ppermute | solution.py:306
  286.7 10.2 %collective-permute-done.7 = bf16[192,1536]{1,0:T(8,128)(2,1)S(1)} collective-permute-done((bf16[192,1536]{1,0:T(8,128)(2,1)S(1)}, bf16[192,1536]{1,0:T(8,128)(2,1)S(1)}, u32[]{:S(2)}, u32[]{:S(2)}) %collective-permute-start.7) | collective-permute-done | bytes 589856 | tf_op jit(solution)/shard_map/ppermute | solution.py:306
  297.5 1.2 slice_bitcast_fusion
  298.7 0.9 fusion.73
  300.7 2.7 fusion.2.u_ref
  303.4 21.2 %down_experts.1 = bf16[384,576]{1,0:T(8,128)(2,1)} custom-call(s32[9]{0:T(128)} %pad_add_fusion.off_s, bf16[896,2880]{1,0:T(8,128)(2,1)} %fusion.2.u_ref, bf16[8,576,2880]{2,1,0:T(8,128)(2,1)} %bitcast.142, s32[384,1]{1,0:T(8,128)} %broadcast_in_dim_reshape.20.pa_ref, s32[384,1]{1,0:T(8,128)} %broadcast_in_dim_reshape.21.pb_ref), custom_call_target="tpu_custom_call" | custom-call | flops 6794772480 | bytes 26542080 | tf_op jit(solution)/shard_map/down_experts/pallas_call | solution.py:282
  324.5 1.6 collective-permute-start.13
  326.2 18.0 %copy_quarter.4 = (bf16[128,1152,128]{2,1,0:T(8,128)(2,1)}, bf16[128,1152,128]{2,1,0:T(8,128)(2,1)}) custom-call(s32[1]{0:T(128)} %bitcast.48.qi, s32[128]{0:T(128)} %len_s.7, bf16[96,1152]{1,0:T(8,128)(2,1)} %get-tuple-element.65.kr_ref, bf16[96,1152]{1,0:T(8,128)(2,1)} %get-tuple-element.64.vr_ref, ...), custom_call_target="tpu_custom_call", output_to_operand_aliasing={{0}: (6, {}), {1}: (7, {})} | custom-call | flops 2415919104 | bytes 37748736 | tf_op jit(solution)/shard_map/copy_quarter/pallas_call | solution.py:199
  344.2 18.1 %copy_quarter.5 = (bf16[128,1152,128]{2,1,0:T(8,128)(2,1)}, bf16[128,1152,128]{2,1,0:T(8,128)(2,1)}) custom-call(s32[1]{0:T(128)} %bitcast.42.qi, s32[128]{0:T(128)} %len_s.7, bf16[96,1152]{1,0:T(8,128)(2,1)} %get-tuple-element.72.kr_ref, bf16[96,1152]{1,0:T(8,128)(2,1)} %get-tuple-element.73.vr_ref, ...), custom_call_target="tpu_custom_call", output_to_operand_aliasing={{0}: (6, {}), {1}: (7, {})} | custom-call | flops 2415919104 | bytes 37748736 | tf_op jit(solution)/shard_map/copy_quarter/pallas_call | solution.py:199
  363.2 1.0 copy.100
  (137 shorter events, 18.8 us)
Async XLA Ops:
  0.6 51.4 %copy-start = (bf16[576,1152]{1,0:T(8,128)(2,1)S(1)}, bf16[576,1152]{1,0:T(8,128)(2,1)}, u32[]{:S(2)}) copy-start(bf16[576,1152]{1,0:T(8,128)(2,1)} %param.25) | copy-start | bytes 3981316
  40.7 13.3 %copy-start.7 = (bf16[384,576]{1,0:T(8,128)(2,1)S(1)}, bf16[384,576]{1,0:T(8,128)(2,1)}, u32[]{:S(2)}) copy-start(bf16[384,576]{1,0:T(8,128)(2,1)} %get-tuple-element.14) | copy-start | bytes 1327108
  40.7 13.3 %copy-start.12 = (bf16[576,1152]{1,0:T(8,128)(2,1)S(1)}, bf16[576,1152]{1,0:T(8,128)(2,1)}, u32[]{:S(2)}) copy-start(bf16[576,1152]{1,0:T(8,128)(2,1)} %param.26) | copy-start | bytes 3981316
  54.0 1.3 copy-start.13
  56.6 1.2 copy-start.10
  56.6 1.3 copy-start.9
  57.7 3.0 collective-permute-start
  62.4 1.1 copy-start.2
  64.3 17.0 %collective-permute-start.1 = (bf16[96,3456]{1,0:T(8,128)(2,1)}, bf16[96,3456]{1,0:T(8,128)(2,1)}, u32[]{:S(2)}, u32[]{:S(2)}) collective-permute-start(bf16[96,3456]{1,0:T(8,128)(2,1)} %slice.170), channel_id=1, source_target_pairs={{0,2},{2,0},{1,3},{3,1},{4,6},{6,4},{5,7},{7,5}} | collective-permute-start | bytes 1990664 | tf_op jit(solution)/shard_map/ppermute | solution.py:306
  65.1 16.2 %copy-start.3 = (bf16[192,3456]{1,0:T(8,128)(2,1)S(1)}, bf16[192,3456]{1,0:T(8,128)(2,1)}, u32[]{:S(2)}) copy-start(bf16[192,3456]{1,0:T(8,128)(2,1)} %copy-done.2) | copy-start | bytes 3981316
  84.8 28.9 %copy-start.11 = (bf16[576]{0:T(1024)(128)(2,1)S(1)}, bf16[576]{0:T(1024)(128)(2,1)}, u32[]{:S(2)}) copy-start(bf16[576]{0:T(1024)(128)(2,1)} %param.28) | copy-start | bytes 3460
  108.6 8.0 %copy-start.4 = (bf16[96,1152]{1,0:T(8,128)(2,1)S(1)}, bf16[96,1152]{1,0:T(8,128)(2,1)}, u32[]{:S(2)}) copy-start(bf16[96,1152]{1,0:T(8,128)(2,1)} %slice.181.vr_ref) | copy-start | bytes 663556
  108.6 8.0 %copy-start.5 = (bf16[96,1152]{1,0:T(8,128)(2,1)S(1)}, bf16[96,1152]{1,0:T(8,128)(2,1)}, u32[]{:S(2)}) copy-start(bf16[96,1152]{1,0:T(8,128)(2,1)} %get-tuple-element.50.kr_ref) | copy-start | bytes 663556
  109.7 6.8 %collective-permute-start.2 = (bf16[96,1152]{1,0:T(8,128)(2,1)S(1)}, bf16[96,1152]{1,0:T(8,128)(2,1)S(1)}, u32[]{:S(2)}, u32[]{:S(2)}) collective-permute-start(bf16[96,1152]{1,0:T(8,128)(2,1)S(1)} %convert_element_type.181), channel_id=1, source_target_pairs={{0,2},{2,0},{1,3},{3,1},{4,6},{6,4},{5,7},{7,5}} | collective-permute-start | bytes 663560 | tf_op jit(solution)/shard_map/ppermute | solution.py:306
  116.6 1.8 collective-permute-start.3
  116.7 12.6 %collective-permute-start.14 = (bf16[96,2304]{1,0:T(8,128)(2,1)S(1)}, bf16[96,2304]{1,0:T(8,128)(2,1)S(1)}, u32[]{:S(2)}, u32[]{:S(2)}) collective-permute-start(bf16[96,2304]{1,0:T(8,128)(2,1)S(1)} %get-tuple-element.69), channel_id=1, source_target_pairs={{0,2},{2,0},{1,3},{3,1},{4,6},{6,4},{5,7},{7,5}} | collective-permute-start | bytes 1327112 | tf_op jit(solution)/shard_map/ppermute | solution.py:306
  120.7 13.3 %copy-start.8 = (bf16[384,576]{1,0:T(8,128)(2,1)S(1)}, bf16[384,576]{1,0:T(8,128)(2,1)}, u32[]{:S(2)}) copy-start(bf16[384,576]{1,0:T(8,128)(2,1)} %get-tuple-element.14) | copy-start | bytes 1327108
  120.7 13.3 %collective-permute-start.4 = (bf16[384,576]{1,0:T(8,128)(2,1)S(1)}, bf16[384,576]{1,0:T(8,128)(2,1)S(1)}, u32[]{:S(2)}, u32[]{:S(2)}) collective-permute-start(bf16[384,576]{1,0:T(8,128)(2,1)S(1)} %convolution_convert_fusion.4), channel_id=1, source_target_pairs={{0,4},{4,0},{1,5},{5,1},{2,6},{6,2},{3,7},{7,3}} | collective-permute-start | bytes 1327112 | tf_op jit(solution)/shard_map/ppermute | solution.py:376
  130.3 167.2 %collective-permute-start.15 = (bf16[2,96,2304]{2,1,0:T(8,128)(2,1)}, bf16[2,96,2304]{2,1,0:T(8,128)(2,1)}, u32[]{:S(2)}, u32[]{:S(2)}) collective-permute-start(bf16[2,96,2304]{2,1,0:T(8,128)(2,1)} %pad_maximum_fusion.3), channel_id=1, source_target_pairs={{0,1},{1,0},{2,3},{3,2},{4,5},{5,4},{6,7},{7,6}} | collective-permute-start | bytes 2654216 | tf_op jit(solution)/shard_map/ppermute | solution.py:303
  160.6 2.2 slice-start.1
  166.0 53.7 %collective-permute-start.9 = (bf16[2,2,192,1344]{3,2,0,1:T(8,128)(2,1)}, bf16[2,2,192,1344]{3,2,0,1:T(8,128)(2,1)}, u32[]{:S(2)}, u32[]{:S(2)}) collective-permute-start(bf16[2,2,192,1344]{3,2,0,1:T(8,128)(2,1)} %bitcast.126), channel_id=1, source_target_pairs={{0,1},{1,0},{2,3},{3,2},{4,5},{5,4},{6,7},{7,6}} | collective-permute-start | bytes 6193160 | tf_op jit(solution)/shard_map/ppermute | solution.py:303
  183.7 2.3 slice-start
  187.9 36.0 %collective-permute-start.5 = (bf16[2,2,192,1536]{3,2,0,1:T(8,128)(2,1)}, bf16[2,2,192,1536]{3,2,0,1:T(8,128)(2,1)}, u32[]{:S(2)}, u32[]{:S(2)}) collective-permute-start(bf16[2,2,192,1536]{3,2,0,1:T(8,128)(2,1)} %bitcast.125), channel_id=1, source_target_pairs={{0,1},{1,0},{2,3},{3,2},{4,5},{5,4},{6,7},{7,6}} | collective-permute-start | bytes 7077896 | tf_op jit(solution)/shard_map/ppermute | solution.py:303
  189.2 18.1 %copy-start.14 = (bf16[576,8]{0,1:T(8,128)(2,1)S(1)}, bf16[576,8]{0,1:T(8,128)(2,1)}, u32[]{:S(2)}) copy-start(bf16[576,8]{0,1:T(8,128)(2,1)} %param.29) | copy-start | bytes 27652
  222.6 26.8 %collective-permute-start.10 = (bf16[2,192,1344]{2,1,0:T(8,128)(2,1)S(1)}, bf16[2,192,1344]{2,1,0:T(8,128)(2,1)S(1)}, u32[]{:S(2)}, u32[]{:S(2)}) collective-permute-start(bf16[2,192,1344]{2,1,0:T(8,128)(2,1)S(1)} %dynamic-slice_bitcast_fusion.1), channel_id=1, source_target_pairs={{0,2},{2,0},{1,3},{3,1},{4,6},{6,4},{5,7},{7,5}} | collective-permute-start | bytes 3096584 | tf_op jit(solution)/shard_map/ppermute | solution.py:306
  226.2 48.4 %collective-permute-start.6 = (bf16[2,192,1536]{2,1,0:T(8,128)(2,1)S(1)}, bf16[2,192,1536]{2,1,0:T(8,128)(2,1)S(1)}, u32[]{:S(2)}, u32[]{:S(2)}) collective-permute-start(bf16[2,192,1536]{2,1,0:T(8,128)(2,1)S(1)} %dynamic-slice_bitcast_fusion), channel_id=1, source_target_pairs={{0,2},{2,0},{1,3},{3,1},{4,6},{6,4},{5,7},{7,5}} | collective-permute-start | bytes 3538952 | tf_op jit(solution)/shard_map/ppermute | solution.py:306
  249.9 36.3 %collective-permute-start.11 = (bf16[192,1344]{1,0:T(8,128)(2,1)S(1)}, bf16[192,1344]{1,0:T(8,128)(2,1)S(1)}, u32[]{:S(2)}, u32[]{:S(2)}) collective-permute-start(bf16[192,1344]{1,0:T(8,128)(2,1)S(1)} %fusion.21), channel_id=1, source_target_pairs={{0,2},{2,0},{1,3},{3,1},{4,6},{6,4},{5,7},{7,5}} | collective-permute-start | bytes 1548296 | tf_op jit(solution)/shard_map/ppermute | solution.py:306
  275.3 21.6 %collective-permute-start.7 = (bf16[192,1536]{1,0:T(8,128)(2,1)S(1)}, bf16[192,1536]{1,0:T(8,128)(2,1)S(1)}, u32[]{:S(2)}, u32[]{:S(2)}) collective-permute-start(bf16[192,1536]{1,0:T(8,128)(2,1)S(1)} %fusion.11), channel_id=1, source_target_pairs={{0,2},{2,0},{1,3},{3,1},{4,6},{6,4},{5,7},{7,5}} | collective-permute-start | bytes 1769480 | tf_op jit(solution)/shard_map/ppermute | solution.py:306
  286.7 12.9 %collective-permute-start.12 = (bf16[2,192,1344]{2,1,0:T(8,128)(2,1)S(1)}, bf16[2,192,1344]{2,1,0:T(8,128)(2,1)S(1)}, u32[]{:S(2)}, u32[]{:S(2)}) collective-permute-start(bf16[2,192,1344]{2,1,0:T(8,128)(2,1)S(1)} %fusion.41), channel_id=1, source_target_pairs={{0,1},{1,0},{2,3},{3,2},{4,5},{5,4},{6,7},{7,6}} | collective-permute-start | bytes 3096584 | tf_op jit(solution)/shard_map/ppermute | solution.py:303
  297.4 2.9 collective-permute-start.8
  324.5 37.8 %collective-permute-start.13 = (bf16[384,576]{1,0:T(8,128)(2,1)}, bf16[384,576]{1,0:T(8,128)(2,1)S(1)}, u32[]{:S(2)}, u32[]{:S(2)}) collective-permute-start(bf16[384,576]{1,0:T(8,128)(2,1)} %down_experts.1), channel_id=1, source_target_pairs={{0,4},{4,0},{1,5},{5,1},{2,6},{6,2},{3,7},{7,3}} | collective-permute-start | bytes 1327112 | tf_op jit(solution)/shard_map/ppermute | solution.py:419
  344.2 18.1 %copy-start.6 = (bf16[384,576]{1,0:T(8,128)(2,1)S(1)}, bf16[384,576]{1,0:T(8,128)(2,1)}, u32[]{:S(2)}) copy-start(bf16[384,576]{1,0:T(8,128)(2,1)} %down_experts.1) | copy-start | bytes 1327108
  362.3 1.9 copy-start.1

commit v2 on v1

v2 whole, which is shorter than its diff:
```python
import jax
import jax.numpy as jnp
from jax import lax
from jax.experimental import pallas as pl
from jax.experimental.pallas import tpu as pltpu
from jax.sharding import PartitionSpec as P

EPS = 1e-5
ROPE_BASE = 1.0e6
LANES = 128
GROUP = 8
SLOTS = 4
TILE = 128
BLOCK = 256
ORDER = (0, 2, 1, 3)
VMEM_BYTES = 60 * 1024 * 1024
CORE_PERM = [(0, 1), (1, 0), (2, 3), (3, 2)]
CHIP_PERM = [(0, 2), (2, 0), (1, 3), (3, 1)]
F32 = jnp.float32
BF16 = jnp.bfloat16


def params(**kw):
    return pltpu.CompilerParams(vmem_limit_bytes=VMEM_BYTES, **kw)


def gather_rows(tokens, emb_table):
    n_tok = tokens.shape[0]
    vocab, width = emb_table.shape
    last_tile = vocab // LANES - 1
    tail_at = (last_tile + 1) * LANES
    n_tail = vocab - tail_at
    n_groups = n_tok // GROUP
    per_chunk = LANES // GROUP
    n_chunks = (n_tok + LANES - 1) // LANES

    def kernel(tok_s, tokv_ref, tail_ref, emb_ref, out_ref, sq_ref, buf, acc, sems):
        def copy(g, i):
            tile = jnp.minimum(tok_s[g * GROUP + i] // LANES, last_tile)
            slot = lax.rem(g, SLOTS)
            return pltpu.make_async_copy(
                emb_ref.at[:, pl.ds(pl.multiple_of(tile * LANES, LANES), LANES)],
                buf.at[slot, :, pl.ds(i * LANES, LANES)], sems.at[slot, i])

        def start(g):
            for i in range(GROUP):
                copy(g, i).start()

        for g in range(SLOTS - 1):
            start(g)
        lane_id = lax.broadcasted_iota(jnp.int32, (LANES, LANES), 0)
        col_id = lax.broadcasted_iota(jnp.int32, (LANES, LANES), 1)

        def step(g, carry):
            @pl.when(g + SLOTS - 1 < n_groups)
            def _():
                start(g + SLOTS - 1)

            for i in range(GROUP):
                copy(g, i).wait()
            slot = lax.rem(g, SLOTS)
            chunk = g // per_chunk
            base = lax.rem(g, per_chunk) * GROUP
            picks = []
            for i in range(GROUP):
                tok = tok_s[g * GROUP + i]
                lane = jnp.where(tok < tail_at, lax.rem(tok, LANES), -1)
                picks.append(((lane_id == lane) & (col_id == base + i)).astype(F32).astype(BF16))
            pick = jnp.concatenate(picks, axis=0)
            for m in range(2):
                ds = pl.ds(m * (width // 2), width // 2)
                part = jnp.dot(buf[slot, ds, :], pick, preferred_element_type=F32)
                acc[chunk, ds, :] = jnp.where(base == 0, part, acc[chunk, ds, :] + part)
            return carry

        lax.fori_loop(0, n_groups, step, 0)
        for c in range(n_chunks):
            size = min(LANES, n_tok - c * LANES)
            rows = jnp.transpose(acc[c])[:size]
            tok_col = tokv_ref[pl.ds(c * LANES, size), :]
            for k in range(n_tail):
                rows = jnp.where(tok_col == tail_at + k, tail_ref[pl.ds(k, 1), :].astype(F32), rows)
            out_ref[pl.ds(c * LANES, size), :] = rows.astype(BF16)
            sq_ref[pl.ds(c * LANES, size), :] = jnp.sum(rows * rows, axis=1, keepdims=True)

    return pl.pallas_call(
        kernel,
        out_shape=(jax.ShapeDtypeStruct((n_tok, width), BF16), jax.ShapeDtypeStruct((n_tok, 1), F32)),
        grid_spec=pltpu.PrefetchScalarGridSpec(
            num_scalar_prefetch=1, grid=(),
            in_specs=[pl.BlockSpec(memory_space=pltpu.VMEM), pl.BlockSpec(memory_space=pltpu.VMEM), pl.BlockSpec(memory_space=pl.ANY)],
            out_specs=[pl.BlockSpec(memory_space=pltpu.VMEM)] * 2,
            scratch_shapes=[pltpu.VMEM((SLOTS, width, GROUP * LANES), BF16), pltpu.VMEM((n_chunks, width, LANES), F32), pltpu.SemaphoreType.DMA((SLOTS, GROUP))]),
        compiler_params=params(),
        cost_estimate=pl.CostEstimate(flops=2 * n_tok * width * LANES * LANES, bytes_accessed=n_tok * width * LANES * 2, transcendentals=0),
        name="gather_rows",
    )(tokens, tokens[:, None], emb_table[tail_at:], emb_table.T)


def column_scratch(rows_ref, out_ref):
    rows = rows_ref[...].astype(F32)
    pad = jnp.zeros((LANES - rows.shape[0], rows.shape[1]), F32)
    out_ref[...] = jnp.transpose(jnp.concatenate([rows, pad], axis=0)).astype(BF16)


def slot_masks(pos, row_local, per_q, steps, slots):
    col = lax.broadcasted_iota(jnp.int32, (LANES, slots), 0)
    slot = lax.broadcasted_iota(jnp.int32, (LANES, slots), 1)
    t = col // per_q
    pick = ((lax.rem(col, per_q) == row_local) & (slot == pos + t) & (t < steps)).astype(F32).astype(BF16)
    lane = lax.broadcasted_iota(jnp.int32, (16, slots), 1)
    keep = ((lane < pos) | (lane >= pos + steps)).astype(F32).astype(BF16)
    return pick, keep[:1]


def put_pair(blocks, columns, picks, keeps):
    slots = blocks[0].shape[1]
    new = jnp.dot(columns, jnp.concatenate(picks, axis=1), preferred_element_type=F32).astype(BF16)
    return [b * k + new[:, i * slots:(i + 1) * slots] for i, (b, k) in enumerate(zip(blocks, keeps))]


def cache_specs(k_cache, n_grid, step_b, skip=0):
    _, kv_width, slots = k_cache.shape
    return pl.BlockSpec((step_b, kv_width, slots), lambda g, qi, ln: (qi[0] * n_grid + skip + g, 0, 0))


def attend_quarter(quarter, lengths, q_rows, k_rows, v_rows, k_cache, v_cache, heads, steps):
    _, kv_width, slots = k_cache.shape
    per_q = q_rows.shape[0] // steps
    head = kv_width // heads
    h_pad = (heads + 7) // 8 * 8
    step_b = 4
    n_grid = per_q // step_b

    def kernel(qi, len_s, q_ref, kr_ref, vr_ref, kc_ref, vc_ref, o_ref, ko_ref, vo_ref, k_cols, v_cols):
        g = pl.program_id(0)

        @pl.when(g == 0)
        def _():
            column_scratch(kr_ref, k_cols)
            column_scratch(vr_ref, v_cols)

        row_h = lax.broadcasted_iota(jnp.int32, (h_pad, kv_width), 0)
        col_h = lax.broadcasted_iota(jnp.int32, (h_pad, kv_width), 1) // head
        diag = row_h == col_h
        srow_t = lax.broadcasted_iota(jnp.int32, (steps * h_pad, slots), 0) // h_pad
        scol = lax.broadcasted_iota(jnp.int32, (steps * h_pad, slots), 1)
        bls = [g * step_b + i for i in range(step_b)]
        poss = [len_s[qi[0] * per_q + bl] for bl in bls]
        picks, keeps = zip(*[slot_masks(pos, bl, per_q, steps, slots) for pos, bl in zip(poss, bls)])
        for i in range(0, step_b, 2):
            for src, cols, dst in ((kc_ref, k_cols, ko_ref), (vc_ref, v_cols, vo_ref)):
                for j, blk in enumerate(put_pair([src[i], src[i + 1]], cols[...], picks[i:i + 2], keeps[i:i + 2])):
                    dst[i + j] = blk
        scores, oks = [], []
        for i, (pos, bl) in enumerate(zip(poss, bls)):
            wide = jnp.concatenate([jnp.where(diag, q_ref[pl.ds(t * per_q + bl, 1), :], 0.0) for t in range(steps)], axis=0).astype(BF16)
            scores.append(jnp.dot(wide, ko_ref[i], preferred_element_type=F32) * head ** -0.5)
            oks.append((scol <= pos + srow_t).astype(F32))
        ok = jnp.concatenate(oks, axis=0) > 0.5
        s = jnp.where(ok, jnp.concatenate(scores, axis=0), -1.0e30)
        e = jnp.where(ok, jnp.exp(s - jnp.max(s, axis=1, keepdims=True)), 0.0)
        scale = 1.0 / jnp.sum(e, axis=1, keepdims=True)
        e = e.astype(BF16)
        n_row = steps * h_pad
        for i, bl in enumerate(bls):
            mine = slice(i * n_row, (i + 1) * n_row)
            mix = lax.dot_general(e[mine], vo_ref[i], (((1,), (1,)), ((), ())), preferred_element_type=F32) * scale[mine]
            for t in range(steps):
                piece = jnp.where(diag, mix[t * h_pad:(t + 1) * h_pad], 0.0)
                o_ref[pl.ds(t * per_q + bl, 1), :] = jnp.sum(piece, axis=0, keepdims=True)

    cache_in = cache_specs(k_cache, n_grid, step_b)
    whole = lambda a: pl.BlockSpec(a.shape, lambda g, qi, ln: (0, 0))
    return pl.pallas_call(
        kernel,
        out_shape=(jax.ShapeDtypeStruct(q_rows.shape, F32), jax.ShapeDtypeStruct(k_cache.shape, BF16), jax.ShapeDtypeStruct(v_cache.shape, BF16)),
        grid_spec=pltpu.PrefetchScalarGridSpec(
            num_scalar_prefetch=2, grid=(n_grid,),
            in_specs=[whole(q_rows), whole(k_rows), whole(v_rows), cache_in, cache_in],
            out_specs=[pl.BlockSpec(q_rows.shape, lambda g, qi, ln: (0, 0)), cache_in, cache_in],
            scratch_shapes=[pltpu.VMEM((kv_width, LANES), BF16)] * 2),
        compiler_params=params(),
        cost_estimate=pl.CostEstimate(flops=4 * per_q * kv_width * LANES * LANES, bytes_accessed=8 * per_q * kv_width * slots, transcendentals=0),
        name="attend_quarter",
    )(quarter, lengths, q_rows, k_rows, v_rows, k_cache, v_cache)


def copy_part(quarter, lengths, k_rows, v_rows, k_cache, v_cache, k_out, v_out, steps, part, n_parts, step_b):
    _, kv_width, slots = k_cache.shape
    per_q = k_rows.shape[0] // steps
    n_all = per_q // step_b
    n_grid = n_all // n_parts
    skip = part * n_grid

    def kernel(qi, len_s, kr_ref, vr_ref, kc_ref, vc_ref, ka_ref, va_ref, ko_ref, vo_ref, k_cols, v_cols):
        g = pl.program_id(0)

        @pl.when(g == 0)
        def _():
            column_scratch(kr_ref, k_cols)
            column_scratch(vr_ref, v_cols)

        for i in range(0, step_b, 2):
            bls = [(g + skip) * step_b + i + j for j in range(2)]
            poss = [len_s[qi[0] * per_q + bl] for bl in bls]
            picks, keeps = zip(*[slot_masks(pos, bl, per_q, steps, slots) for pos, bl in zip(poss, bls)])
            for src, cols, dst in ((kc_ref, k_cols, ko_ref), (vc_ref, v_cols, vo_ref)):
                for j, blk in enumerate(put_pair([src[i], src[i + 1]], cols[...], picks, keeps)):
                    dst[i + j] = blk

    cache_in = cache_specs(k_cache, n_all, step_b, skip)
    whole = lambda a: pl.BlockSpec(a.shape, lambda g, qi, ln: (0, 0))
    anyspec = pl.BlockSpec(memory_space=pl.ANY)
    return pl.pallas_call(
        kernel,
        out_shape=(jax.ShapeDtypeStruct(k_cache.shape, BF16), jax.ShapeDtypeStruct(v_cache.shape, BF16)),
        grid_spec=pltpu.PrefetchScalarGridSpec(
            num_scalar_prefetch=2, grid=(n_grid,),
            in_specs=[whole(k_rows), whole(v_rows), cache_in, cache_in, anyspec, anyspec],
            out_specs=[cache_in, cache_in],
            scratch_shapes=[pltpu.VMEM((kv_width, LANES), BF16)] * 2),
        input_output_aliases={6: 0, 7: 1},
        compiler_params=params(),
        cost_estimate=pl.CostEstimate(flops=4 * per_q // n_parts * kv_width * LANES * LANES, bytes_accessed=12 * per_q // n_parts * kv_width * slots, transcendentals=0),
        name="copy_part",
    )(quarter, lengths, k_rows, v_rows, k_cache, v_cache, k_out, v_out)


def expert_tiles(off_s, e, n_rows, body):
    lo, hi = off_s[e], off_s[e + 1]
    first = lo // 16 * 16
    n_tiles = jnp.where(hi > lo, (hi - first + TILE - 1) // TILE, 0)

    def step(i, carry):
        start = first + i * TILE
        at = pl.multiple_of(jnp.minimum(start, n_rows - TILE), 16)
        row = at + lax.broadcasted_iota(jnp.int32, (TILE, 1), 0)
        body(pl.ds(at, TILE), (row >= jnp.maximum(lo, start)) & (row < hi))
        return carry

    lax.fori_loop(0, n_tiles, step, 0)


def weight_specs(parts, per_quarter, blocks, depth):
    def spec(i, b):
        return pl.BlockSpec((1, depth, BLOCK), lambda e, rel, off: (e, 0, rel[i] * per_quarter + b))

    return [spec(i, b) for i in range(parts) for b in blocks]


def up_experts(rel, offsets, rows, w_act, w_lin, blocks, per_quarter):
    n_rows, depth = rows.shape
    experts, _, ff = w_act.shape
    parts, nb = rel.shape[0], len(blocks)
    n_w = parts * nb

    def kernel(rel_s, off_s, x_ref, *refs):
        a_refs, l_refs, (keep_ref, send_ref) = refs[:n_w], refs[n_w:2 * n_w], refs[2 * n_w:]
        e = pl.program_id(0)
        lane = lax.broadcasted_iota(jnp.int32, (1, BLOCK), 1)

        def body(ds, mine):
            x = x_ref[ds, :]
            for i in range(parts):
                for n, b in enumerate(blocks):
                    ok = mine & (lane + (rel_s[i] * per_quarter + b) * BLOCK < ff)
                    for k, w_refs in enumerate((a_refs, l_refs)):
                        out_ref = (keep_ref if i < 2 else send_ref).at[i % 2, k]
                        cols = pl.ds(n * BLOCK, BLOCK)
                        y = jnp.dot(x, w_refs[i * nb + n][0], preferred_element_type=F32)
                        out_ref[ds, cols] = jnp.where(ok, y, out_ref[ds, cols].astype(F32)).astype(BF16)

        @pl.when(e == 0)
        def _():
            keep_ref[...] = jnp.zeros_like(keep_ref)
            send_ref[...] = jnp.zeros_like(send_ref)

        expert_tiles(off_s, e, n_rows, body)

    shape = (2, 2, n_rows, nb * BLOCK)
    out = pl.BlockSpec(shape, lambda e, rel, off: (0, 0, 0, 0))
    cols = n_w * BLOCK
    return pl.pallas_call(
        kernel,
        out_shape=(jax.ShapeDtypeStruct(shape, BF16),) * 2,
        grid_spec=pltpu.PrefetchScalarGridSpec(
            num_scalar_prefetch=2, grid=(experts,),
            in_specs=[pl.BlockSpec(rows.shape, lambda e, rel, off: (0, 0))] + weight_specs(parts, per_quarter, blocks, depth) * 2,
            out_specs=[out, out]),
        compiler_params=params(),
        cost_estimate=pl.CostEstimate(flops=8 * TILE * experts * depth * cols, bytes_accessed=6 * experts * depth * cols, transcendentals=0),
        name="up_experts",
    )(rel, offsets, rows, *[w_act] * n_w, *[w_lin] * n_w)


def down_experts(rel, offsets, own, near, far, w_down_t, before, pos_a, pos_b, blocks, per_quarter, last):
    n_rows = own.shape[0]
    experts, width, ff = w_down_t.shape
    n_tok = pos_a.shape[0]
    parts, nb = rel.shape[0], len(blocks)
    n_w = parts * nb
    edge = ff - (ff - 1) // BLOCK * BLOCK
    has_edge = per_quarter - 1 in blocks

    def kernel(rel_s, off_s, own_ref, near_ref, far_ref, *refs):
        w_refs, refs = refs[:n_w], refs[n_w:]
        if before is not None:
            before_ref, refs = refs[0], refs[1:]
        if last:
            pa_ref, pb_ref, out_ref, acc = refs
        else:
            acc, = refs
        e = pl.program_id(0)

        @pl.when(e == 0)
        def _():
            acc[...] = jnp.zeros_like(acc) if before is None else before_ref[...]

        def body(ds, mine):
            def run(edge_part):
                total = acc[ds, :]
                for i in range(parts):
                    for n, b in enumerate(blocks):
                        cut = edge if i == edge_part and b == per_quarter - 1 else BLOCK
                        cols = pl.ds(n * BLOCK, cut)
                        u = (own_ref[ds, cols], near_ref[ds, cols], far_ref[0, ds, cols], far_ref[1, ds, cols])[i]
                        w = w_refs[i * nb + n][0, :, :cut]
                        total = total + lax.dot_general(u, w, (((1,), (1,)), ((), ())), preferred_element_type=F32)
                acc[ds, :] = jnp.where(mine, total, acc[ds, :])

            if has_edge:
                for i in range(parts):
                    @pl.when(rel_s[i] == parts - 1)
                    def _(i=i):
                        run(i)
            else:
                run(None)

        expert_tiles(off_s, e, n_rows, body)

        if last:
            @pl.when(e == experts - 1)
            def _():
                col = lax.broadcasted_iota(jnp.int32, (n_tok, n_rows), 1)
                pick = ((col == pa_ref[...]) | (col == pb_ref[...])).astype(F32).astype(BF16)
                y = acc[...]
                high = y.astype(BF16)
                low = (y - high.astype(F32)).astype(BF16)
                out_ref[...] = (jnp.dot(pick, high, preferred_element_type=F32) + jnp.dot(pick, low, preferred_element_type=F32)).astype(BF16)

    whole = lambda a: pl.BlockSpec(a.shape, lambda e, rel, off: (0,) * a.ndim)
    extra = ([] if before is None else [before]) + ([pos_a, pos_b] if last else [])
    acc_shape = (n_rows, width)
    if last:
        out_shape, scratch = jax.ShapeDtypeStruct((n_tok, width), BF16), [pltpu.VMEM(acc_shape, F32)]
    else:
        out_shape, scratch = jax.ShapeDtypeStruct(acc_shape, F32), []
    cols = n_w * BLOCK
    return pl.pallas_call(
        kernel,
        out_shape=out_shape,
        grid_spec=pltpu.PrefetchScalarGridSpec(
            num_scalar_prefetch=2, grid=(experts,),
            in_specs=[whole(own), whole(near), whole(far)] + weight_specs(parts, per_quarter, blocks, width) + [whole(a) for a in extra],
            out_specs=pl.BlockSpec(out_shape.shape, lambda e, rel, off: (0, 0)),
            scratch_shapes=scratch),
        compiler_params=params(),
        cost_estimate=pl.CostEstimate(flops=4 * TILE * experts * cols * width, bytes_accessed=4 * experts * cols * width, transcendentals=0),
        name="down_experts",
    )(rel, offsets, own, near, far, *[w_down_t] * n_w, *extra)


def share_rows(rows, sums):
    n_x, n_y = 4, 2
    peers = [(d, e) for d in range(n_x) for e in range(n_y) if d or e]

    def kernel(rows_ref, sums_ref, rows_out, sums_out, send_sems, recv_sems):
        xi, yi = lax.axis_index('x'), lax.axis_index('y')

        def peer(d, e):
            return {'x': lax.bitwise_xor(xi, d), 'y': lax.bitwise_xor(yi, e)}

        barrier = pltpu.get_barrier_semaphore()
        for d, e in peers:
            pl.semaphore_signal(barrier, inc=1, device_id=peer(d, e), device_id_type=pl.DeviceIdType.MESH)
        pl.semaphore_wait(barrier, len(peers))
        copies = [pltpu.make_async_remote_copy(
            src_ref=rows_ref, dst_ref=rows_out.at[yi], send_sem=send_sems.at[0], recv_sem=recv_sems.at[0],
            device_id=peer(0, 1), device_id_type=pl.DeviceIdType.MESH)]
        copies += [pltpu.make_async_remote_copy(
            src_ref=sums_ref, dst_ref=sums_out.at[d, yi], send_sem=send_sems.at[k + 1], recv_sem=recv_sems.at[k + 1],
            device_id=peer(d, e), device_id_type=pl.DeviceIdType.MESH) for k, (d, e) in enumerate(peers)]
        for c in copies:
            c.start()
        rows_out[yi] = rows_ref[...]
        sums_out[0, yi] = sums_ref[...]
        for c in copies:
            c.wait()

    return pl.pallas_call(
        kernel,
        out_shape=(jax.ShapeDtypeStruct((n_y,) + rows.shape, rows.dtype), jax.ShapeDtypeStruct((n_x, n_y) + sums.shape, sums.dtype)),
        in_specs=[pl.BlockSpec(memory_space=pltpu.VMEM)] * 2,
        out_specs=[pl.BlockSpec(memory_space=pltpu.VMEM)] * 2,
        scratch_shapes=[pltpu.SemaphoreType.DMA((len(peers) + 1,))] * 2,
        compiler_params=pltpu.CompilerParams(collective_id=0, has_side_effects=True),
        cost_estimate=pl.CostEstimate(flops=0, bytes_accessed=16_000_000, transcendentals=0),
        name="share_rows",
    )(rows, sums)


def share_small(values, call_id):
    n_dev = 4

    def kernel(v_ref, out_ref, send_sems, recv_sems):
        xi = lax.axis_index('x')
        barrier = pltpu.get_barrier_semaphore()
        for d in range(1, n_dev):
            pl.semaphore_signal(barrier, inc=1, device_id={'x': lax.bitwise_xor(xi, d)}, device_id_type=pl.DeviceIdType.MESH)
        pl.semaphore_wait(barrier, n_dev - 1)
        copies = []
        for d in range(1, n_dev):
            copies.append(pltpu.make_async_remote_copy(
                src_ref=v_ref, dst_ref=out_ref.at[d], send_sem=send_sems.at[d - 1], recv_sem=recv_sems.at[d - 1],
                device_id={'x': lax.bitwise_xor(xi, d)}, device_id_type=pl.DeviceIdType.MESH))
            copies[-1].start()
        out_ref[0] = v_ref[...]
        for c in copies:
            c.wait()

    return pl.pallas_call(
        kernel,
        out_shape=jax.ShapeDtypeStruct((n_dev,) + values.shape, values.dtype),
        in_specs=[pl.BlockSpec(memory_space=pltpu.VMEM)],
        out_specs=pl.BlockSpec(memory_space=pltpu.VMEM),
        scratch_shapes=[pltpu.SemaphoreType.DMA((n_dev - 1,))] * 2,
        compiler_params=pltpu.CompilerParams(collective_id=call_id, has_side_effects=True),
        cost_estimate=pl.CostEstimate(flops=0, bytes_accessed=8_000_000, transcendentals=0),
        name="share_small",
    )(values)


def solution(mesh):
    x_count = mesh.shape['x']
    cache_spec = P('dp', None, 'y', None)
    in_specs = (P(None, 'dp'), P('dp'), P(None, 'dp', None), P(None, 'x'), cache_spec, cache_spec, P('x'), P('x', 'y'), P('x', 'y'), P('x', 'y'), P('y', 'x'), P('x'), P('x', None), P(None, 'x', 'y'), P(None, 'x', 'y'), P(None, 'y', 'x'))
    out_specs = (P(None, 'dp', 'x'), cache_spec, cache_spec)

    def over_core(v):
        return lax.ppermute(v, 'x', CORE_PERM)

    def over_chip(v):
        return lax.ppermute(v, 'x', CHIP_PERM)

    def layer_steps(tokens, lengths, choices, emb_table, k_cache, v_cache, g_attn, w_q, w_k, w_v, w_o, g_ffn, w_router, w_act, w_lin, w_down):
        steps, n_batch = tokens.shape
        heads, head = k_cache.shape[2], k_cache.shape[3]
        kv_width = heads * head
        width = emb_table.shape[1]
        width_full = width * x_count
        experts, _, ff = w_act.shape
        n_tok = steps * n_batch
        per_q = n_batch // x_count
        q_rows_n = steps * per_q
        xi = lax.axis_index('x')
        order = jnp.array(ORDER, jnp.int32)
        rel = lax.bitwise_xor(order, xi)
        back = order[lax.bitwise_xor(jnp.arange(x_count, dtype=jnp.int32), xi)]

        def to_rel(a):
            a = a.reshape((steps, x_count, per_q) + a.shape[2:])
            return jnp.moveaxis(a, 1, 0)[rel].reshape((n_tok,) + a.shape[3:])

        def shared(v, call_id):
            r = v.shape[0]
            v = jnp.pad(v, ((0, -r % 8), (0, 0)))
            got = share_small(jnp.moveaxis(v.reshape(-1, x_count, q_rows_n), 1, 0), call_id)
            rows = [[got[d, ORDER[ORDER[i] ^ d], :r] for i in range(x_count)] for d in range(x_count)]
            return jnp.stack([jnp.concatenate(one, axis=1) for one in rows])

        yi = lax.axis_index('y')
        y_rows = n_tok // 2
        my_tokens = lax.dynamic_slice(to_rel(tokens), (yi * y_rows,), (y_rows,))
        my_rows, my_sq = gather_rows(my_tokens, emb_table)
        both_rows, each_sq = share_rows(my_rows, jnp.pad(my_sq.reshape(2, 1, q_rows_n), ((0, 0), (0, 7), (0, 0))))
        x_in = both_rows.reshape(n_tok, width)
        found = [[ORDER[ORDER[i] ^ d] for d in range(x_count)] for i in range(x_count)]
        total_sq = jnp.stack([sum(each_sq[d, j // 2, j % 2, 0] for d, j in enumerate(js)) for js in found]).reshape(n_tok, 1)
        h = (x_in.astype(F32) * lax.rsqrt(total_sq / width_full + EPS) * g_attn.astype(F32)).astype(BF16)
        part = jnp.concatenate([jnp.dot(h, w, preferred_element_type=F32) for w in (w_q, w_k, w_v)], axis=1).astype(BF16)

        choices, lengths_r, part = lax.optimization_barrier((choices, lengths, part))
        flat = choices.reshape(n_tok * 2)
        hot = (flat[:, None] == jnp.arange(experts)[None, :])
        lower = (lax.broadcasted_iota(jnp.int32, (2 * n_tok, 2 * n_tok), 0) > lax.broadcasted_iota(jnp.int32, (2 * n_tok, 2 * n_tok), 1)).astype(BF16)
        before = jnp.dot(lower, hot.astype(BF16), preferred_element_type=F32).astype(jnp.int32)
        counts = jnp.sum(hot.astype(jnp.int32), axis=0)
        first = jnp.sum(jnp.where(jnp.arange(experts)[:, None] > jnp.arange(experts)[None, :], counts[None, :], 0), axis=1)
        offsets = jnp.concatenate([first, jnp.full((1,), 2 * n_tok, jnp.int32)])
        place = jnp.sum(jnp.where(hot, before + first[None, :], 0), axis=1).reshape(steps, n_batch, 2)
        pos_a = to_rel(place[:, :, 0])
        pos_b = to_rel(place[:, :, 1])
        choice_a = to_rel(choices[:, :, 0])
        choice_b = to_rel(choices[:, :, 1])

        half = n_tok // 2
        got = over_core(part[half:])
        part = (part[:half].astype(F32) + got.astype(F32)).astype(BF16)
        got = over_chip(part[q_rows_n:])
        proj = (part[:q_rows_n].astype(F32) + got.astype(F32)).astype(BF16).astype(F32)
        len_q = lax.dynamic_slice(lengths_r, (xi * per_q,), (per_q,))
        positions = (len_q[None, :] + jnp.arange(steps)[:, None]).reshape(q_rows_n).astype(F32)
        inv_freq = ROPE_BASE ** (-(jnp.arange(head // 2, dtype=F32) * 2.0 / head))
        angles = jnp.tile(positions[:, None] * inv_freq[None, :], (1, 2 * heads))
        cosine, sine = jnp.cos(angles), jnp.sin(angles)
        low_half = (jnp.arange(kv_width) % head < head // 2)[None, :]

        def rotate(v):
            other = jnp.where(low_half, -jnp.roll(v, -(head // 2), axis=1), jnp.roll(v, head // 2, axis=1))
            return (v * cosine + other * sine).astype(BF16)

        queries = rotate(proj[:, :kv_width]).astype(F32)
        kv_new = jnp.concatenate([rotate(proj[:, kv_width:2 * kv_width]), proj[:, 2 * kv_width:].astype(BF16)], axis=1)
        k_view = k_cache.transpose(0, 2, 3, 1).reshape(n_batch, kv_width, -1)
        v_view = v_cache.transpose(0, 2, 3, 1).reshape(n_batch, kv_width, -1)
        mixed, k_out, v_out = attend_quarter(xi[None], lengths, queries, kv_new[:, :kv_width], kv_new[:, kv_width:], k_view, v_view, heads, steps)
        mixed = mixed.astype(BF16)
        mixed2 = jnp.concatenate([mixed, over_chip(mixed)], axis=0)
        mixed4 = jnp.concatenate([mixed2, over_core(mixed2)], axis=0)
        attn = jnp.dot(mixed4, w_o, preferred_element_type=F32).astype(BF16)

        kv_pair = jnp.stack([kv_new, over_chip(kv_new)])
        kv_far = over_core(kv_pair)

        def write(caches, rows, idx, part, n_parts, step_b):
            return copy_part(lax.bitwise_xor(xi, idx)[None], lengths, rows[:, :kv_width], rows[:, kv_width:], k_view, v_view, *caches, steps, part, n_parts, step_b)

        def add_over_y(v):
            got = lax.ppermute(v, 'y', [(0, 1), (1, 0)])
            return v.astype(F32) + got.astype(F32)

        caches = write((k_out, v_out), kv_pair[1], 2, 0, 2, 4)
        attn_sum = add_over_y(attn)
        x_mid = (x_in.astype(F32) + attn_sum).astype(BF16)

        x_mid32 = x_mid.astype(F32)
        sq_mid = jnp.sum(x_mid32 * x_mid32, axis=1)
        local_scale = lax.rsqrt(sq_mid / width + EPS)
        h_local = (x_mid32 * local_scale[:, None] * g_ffn.astype(F32)).astype(BF16)
        r_part = lax.dot_general(w_router, h_local, (((0,), (1,)), ((), ())), preferred_element_type=F32)
        got = shared(jnp.concatenate([r_part, sq_mid[None, :]], axis=0), 1)
        sq_each = got[:, experts]
        full_scale = lax.rsqrt(jnp.sum(sq_each, axis=0) / width_full + EPS)
        logits = jnp.sum(got[:, :experts] * (full_scale[None, :] / lax.rsqrt(sq_each / width + EPS))[:, None, :], axis=0)
        h2 = (x_mid32 * full_scale[:, None] * g_ffn.astype(F32)).astype(BF16)
        eid = jnp.arange(experts)[:, None]
        pair = jnp.stack([jnp.sum(jnp.where(choice[None, :] == eid, logits, 0.0), axis=0) for choice in (choice_a, choice_b)])
        gates = jax.nn.softmax(pair, axis=0)
        n_pair = 2 * n_tok
        row_id = jnp.arange(n_pair)[:, None]
        at_a, at_b = pos_a[None, :] == row_id, pos_b[None, :] == row_id
        coef = jnp.sum(jnp.where(at_a, gates[0][None, :], 0.0) + jnp.where(at_b, gates[1][None, :], 0.0), axis=1, keepdims=True)
        sorted_h = jnp.dot((at_a | at_b).astype(BF16), h2, preferred_element_type=F32).astype(BF16)

        per_quarter = (ff + x_count * BLOCK - 1) // (x_count * BLOCK)
        first_blocks, last_blocks = list(range(per_quarter - 1)), [per_quarter - 1]
        w_down_t = w_down.transpose(0, 2, 1)

        def up(blocks):
            keep, send = up_experts(rel, offsets, sorted_h, w_act, w_lin, blocks, per_quarter)
            got = over_core(send)
            mine = (keep[0].astype(F32) + got[0].astype(F32)).astype(BF16)
            return mine, (keep[1].astype(F32) + got[1].astype(F32)).astype(BF16)

        def activate(mine, got):
            act, lin = (v for v in (mine.astype(F32) + got.astype(F32)).astype(BF16).astype(F32))
            unit = (coef * jax.nn.silu(act) * lin).astype(BF16)
            near = over_chip(unit)
            return unit, near, over_core(jnp.stack([unit, near]))

        def down(unit, before, blocks, last):
            return down_experts(rel, offsets, *unit, w_down_t, before, pos_a[:, None], pos_b[:, None], blocks, per_quarter, last)

        mine0, next0 = up(first_blocks)
        got0 = over_chip(next0)
        mine1, next1 = up(last_blocks)
        got1 = over_chip(next1)
        unit0 = activate(mine0, got0)
        caches = write(caches, kv_far[0], 1, 0, 1, 8)
        caches = write(caches, kv_far[1], 3, 0, 1, 8)
        unit1 = activate(mine1, got1)
        moe = down(unit0, None, first_blocks, False)
        moe = down(unit1, moe, last_blocks, True)
        k_out, v_out = write(caches, kv_pair[1], 2, 1, 2, 4)
        moe_sum = add_over_y(moe)
        out = (x_mid32 + moe_sum).astype(BF16)
        out = jnp.moveaxis(out.reshape(x_count, steps, per_q, width)[back], 0, 1).reshape(steps, n_batch, width)

        def to_cache(v):
            return v.reshape(n_batch, heads, head, -1).transpose(0, 3, 1, 2)

        return out, to_cache(k_out), to_cache(v_out)

    return jax.shard_map(layer_steps, mesh=mesh, in_specs=in_specs, out_specs=out_specs, check_vma=False)
```

time: 366 us -> 344 us (0.940)
  blocking collectives: 25.2 us -> 0 us
  local copies, waits for them, and re-layouts: 35 us -> 26.3 us
  Pallas kernels: 167 us -> 174 us
  waiting for transfers between devices: 96 us -> 101 us
    pallas_call x6 -> x10, Pallas kernels: 110 us -> 136 us  [the longest x4 51 us: copy_part(): pl.pallas_call(kernel, out_shape=(jax.ShapeDtypeStruct(k_cache.shape, BF1...]
    psum x3 -> x0, blocking collectives: 25.2 us -> none  [the longest x2 14.7 us: norm(): total = lax.psum(sq_abs, 'x')[rel].reshape(n_tok, 1)]
    pallas_call x1, Pallas kernels: 32.8 us -> 17.5 us  [gather_rows(): pl.pallas_call(kernel, out_shape=(jax.ShapeDtypeStruct((n_tok, width), BF...]
    ppermute x2, waiting for transfers between devices: 3.66 us -> 8.82 us  [add_over_y(): got = lax.ppermute(v, 'y', [(0, 1), (1, 0)])]
    dynamic_slice x5 -> x2, local copies, waits for them, and re-layouts: 5.14 us -> 0.15 us  [the longest x1 0.08 us: layer_steps(): my_tokens = lax.dynamic_slice(to_rel(tokens), (yi * y_rows,), (y_rows,))]
    slice x12 -> x8, local copies, waits for them, and re-layouts: 9.33 us -> 4.82 us  [the longest x2 1.78 us: write(): rows[:, kv_width:]]
    pallas_call x1, Pallas kernels: 23.8 us -> 19.9 us  [attend_quarter(): pl.pallas_call(kernel, out_shape=(jax.ShapeDtypeStruct(q_rows.shape, F32)...]
    convert_element_type x13 -> x16, other arithmetic: 11.1 us -> 15 us  [the longest x2 4.62 us: up(): return (mine, (keep[1].astype(F32) + got[1].astype(F32)).astype(BF16))]
  transfers between devices with their start and end apart: 16 -> 16, of which waited for: 11 -> 10; matrix products, arithmetic and copies ran while one was open for 9% -> 7% of each run, Pallas kernels for 24% -> 24%
where the time goes in v2:
time: 344 us; the launch traced here: 342 us
  Pallas kernels  174 us (51%)
  waiting for transfers between devices  101 us (29%)
  local copies, waits for them, and re-layouts  26.3 us (8%)
  other arithmetic  24 us (7%)
  starting transfers between devices  8.71 us (3%)
  matrix products  7.12 us (2%)
    ppermute x7, waiting for transfers between devices, over_chip(): return lax.ppermute(v, 'x', CHIP_PERM)  87.4 us
    pallas_call x4, Pallas kernels, copy_part(): pl.pallas_call(kernel, out_shape=(jax.ShapeDtypeStruct(k_cache.shape, BF1...  51 us
    pallas_call x2, Pallas kernels, up_experts(): pl.pallas_call(kernel, out_shape=(jax.ShapeDtypeStruct(shape, BF16),) * 2...  36.7 us
    pallas_call x2, Pallas kernels, down_experts(): pl.pallas_call(kernel, out_shape=out_shape, grid_spec=pltpu.PrefetchScala...  29.5 us
    pallas_call x1, Pallas kernels, attend_quarter(): pl.pallas_call(kernel, out_shape=(jax.ShapeDtypeStruct(q_rows.shape, F32)...  19.9 us
    pallas_call x1, Pallas kernels, gather_rows(): pl.pallas_call(kernel, out_shape=(jax.ShapeDtypeStruct((n_tok, width), BF...  17.5 us
    pallas_call x1, Pallas kernels, share_rows(): pl.pallas_call(kernel, out_shape=(jax.ShapeDtypeStruct((n_y,) + rows.shap...  13.6 us
    ppermute x2, waiting for transfers between devices, add_over_y(): got = lax.ppermute(v, 'y', [(0, 1), (1, 0)])  8.82 us
  transfers between devices with their start and end apart: 16, of which 10 were waited for; matrix products, arithmetic and copies ran while one was open for 7% of the time, Pallas kernels for 24%

profile of v2, /device:TPU:0, one launch (start us, length us, event | category | flops | bytes accessed | tf_op | source)
XLA Modules:
  0.0 342.3 jit_solution(18262685440955284433)
XLA Ops:
  0.7 1.4 broadcast_xor_fusion
  2.0 0.7 convert_element_type.202
  2.7 0.8 reshape.380
  4.2 0.8 copy.72.tokv_ref
  5.0 0.9 slice.231
  5.9 0.7 copy.93.tail_ref
  6.6 17.5 %gather_rows.1 = (bf16[192,576]{1,0:T(8,128)(2,1)}, f32[192,1]{1,0:T(8,128)}) custom-call(s32[192]{0:T(256)} %copy-done.30, s32[192,1]{1,0:T(8,128)} %copy.72.tokv_ref, bf16[1,576]{1,0:T(2,128)(2,1)} %copy.93.tail_ref, bf16[576,122753]{1,0:T(8,128)(2,1)} %bitcast.2.emb_ref), custom_call_target="tpu_custom_call" | custom-call | flops 3623878656 | bytes 28311552 | tf_op jit(solution)/shard_map/gather_rows/pallas_call | solution.py:86
  24.1 1.0 reduce.3
  25.8 13.6 %share_rows.1 = (bf16[2,192,576]{2,1,0:T(8,128)(2,1)}, f32[4,2,2,8,96]{4,3,2,1,0:T(8,128)}) custom-call(bf16[192,576]{1,0:T(8,128)(2,1)} %get-tuple-element.25.rows_ref, f32[2,8,96]{2,1,0:T(8,128)} %pad.8.sums_ref), custom_call_target="tpu_custom_call" | custom-call | bytes 16000000 | tf_op jit(solution)/shard_map/share_rows/pallas_call | solution.py:401
  39.4 0.8 add_bitcast_fusion.3
  40.3 1.2 fusion.18
  41.6 0.9 convolution_convert_fusion
  42.9 0.9 convolution_convert_fusion.1
  44.2 0.9 convolution_convert_fusion.2
  45.3 1.2 slice.249
  46.7 3.2 collective-permute-done
  49.9 1.6 add_convert_fusion.2
  51.5 1.1 copy-done.3
  52.6 0.9 slice.318
  54.9 15.8 %collective-permute-done.1 = bf16[96,3456]{1,0:T(8,128)(2,1)S(1)} collective-permute-done((bf16[96,3456]{1,0:T(8,128)(2,1)}, bf16[96,3456]{1,0:T(8,128)(2,1)S(1)}, u32[]{:S(2)}, u32[]{:S(2)}) %collective-permute-start.1) | collective-permute-done | bytes 663584 | tf_op jit(solution)/shard_map/ppermute | solution.py:454
  70.9 0.7 slice.329.vr_ref
  71.8 1.2 fusion.48
  73.0 19.9 %attend_quarter.1 = (f32[96,1152]{1,0:T(8,128)}, bf16[128,1152,128]{2,1,0:T(8,128)(2,1)}, bf16[128,1152,128]{2,1,0:T(8,128)(2,1)}) custom-call(s32[1]{0:T(128)} %bitcast.5.qi, s32[128]{0:T(128)} %len_s.9, f32[96,1152]{1,0:T(8,128)} %get-tuple-element.71.q_ref, bf16[96,1152]{1,0:T(8,128)(2,1)} %get-tuple-element.70.kr_ref, bf16[96,1152]{1,0:T(8,128)(2,1)} %slice.329.vr_ref, ...), custom_call_target="tpu_custom_call" | custom-call | flops 2415919104 | bytes 37748736 | tf_op jit(solution)/shard_map/attend_quarter/pallas_call | solution.py:175
  92.9 1.1 convert_element_type.216
  94.6 6.1 %collective-permute-done.2 = bf16[96,1152]{1,0:T(8,128)(2,1)S(1)} collective-permute-done((bf16[96,1152]{1,0:T(8,128)(2,1)S(1)}, bf16[96,1152]{1,0:T(8,128)(2,1)S(1)}, u32[]{:S(2)}, u32[]{:S(2)}) %collective-permute-start.2) | collective-permute-done | bytes 221216 | tf_op jit(solution)/shard_map/ppermute | solution.py:454
  101.2 1.5 collective-permute-done.3
  102.7 1.9 convolution_convert_fusion.4
  104.7 1.5 collective-permute-start.4
  109.1 8.8 %collective-permute-done.4 = bf16[384,576]{1,0:T(8,128)(2,1)S(1)} collective-permute-done((bf16[384,576]{1,0:T(8,128)(2,1)S(1)}, bf16[384,576]{1,0:T(8,128)(2,1)S(1)}, u32[]{:S(2)}, u32[]{:S(2)}) %collective-permute-start.4) | collective-permute-done | bytes 442400 | tf_op jit(solution)/shard_map/ppermute | solution.py:540
  118.8 0.6 copy.101
  119.4 5.5 %share_small.1 = f32[4,4,16,96]{3,2,1,0:T(8,128)} custom-call(f32[4,16,96]{2,1,0:T(8,128)} %bitcast.212), custom_call_target="tpu_custom_call" | custom-call | bytes 8000000 | tf_op jit(solution)/shard_map/share_small/pallas_call | solution.py:432
  124.9 0.9 slice_bitcast_fusion.17
  127.2 1.8 convolution_convert_fusion.3.x_ref
  129.0 22.5 %up_experts.3 = (bf16[2,2,768,512]{3,2,1,0:T(8,128)(2,1)}, bf16[2,2,768,512]{3,2,1,0:T(8,128)(2,1)}) custom-call(s32[4]{0:T(128)} %get-tuple-element.112.rel_s, s32[9]{0:T(128)} %pad_add_fusion.off_s, bf16[768,576]{1,0:T(8,128)(2,1)} %convolution_convert_fusion.3.x_ref, bf16[8,576,2880]{2,1,0:T(8,128)(2,1)} %refs_7_.3, bf16[8,576,2880]{2,1,0:T(8,128)(2,1)} %refs_7_.3, ...), custom_call_target="tpu_custom_call" | custom-call | flops 9663676416 | bytes 56623104 | tf_op jit(solution)/shard_map/up_experts/pallas_call | solution.py:284
  151.7 0.9 broadcast_in_dim_reshape.14.refs_6_
  152.5 0.9 broadcast_in_dim_reshape.6.refs_5_
  153.4 0.6 gather_fusion.5
  156.9 9.7 %collective-permute-done.14 = bf16[96,2304]{1,0:T(8,128)(2,1)S(1)} collective-permute-done((bf16[96,2304]{1,0:T(8,128)(2,1)S(1)}, bf16[96,2304]{1,0:T(8,128)(2,1)S(1)}, u32[]{:S(2)}, u32[]{:S(2)}) %collective-permute-start.14) | collective-permute-done | bytes 442400 | tf_op jit(solution)/shard_map/ppermute | solution.py:454
  166.6 1.0 pad_maximum_fusion.2
  167.6 0.8 fusion.77
  168.4 14.2 %up_experts.2 = (bf16[2,2,768,256]{3,2,1,0:T(8,128)(2,1)}, bf16[2,2,768,256]{3,2,1,0:T(8,128)(2,1)}) custom-call(s32[4]{0:T(128)} %get-tuple-element.112.rel_s, s32[9]{0:T(128)} %pad_add_fusion.off_s, bf16[768,576]{1,0:T(8,128)(2,1)} %convolution_convert_fusion.3.x_ref, bf16[8,576,2880]{2,1,0:T(8,128)(2,1)} %refs_7_.3, bf16[8,576,2880]{2,1,0:T(8,128)(2,1)} %refs_7_.3, ...), custom_call_target="tpu_custom_call" | custom-call | flops 4831838208 | bytes 28311552 | tf_op jit(solution)/shard_map/up_experts/pallas_call | solution.py:284
  183.2 3.1 fusion.3
  186.8 9.9 %copy_part.4 = (bf16[128,1152,128]{2,1,0:T(8,128)(2,1)}, bf16[128,1152,128]{2,1,0:T(8,128)(2,1)}) custom-call(s32[1]{0:T(128)} %bitcast.60.qi, s32[128]{0:T(128)} %len_s.9, bf16[96,1152]{1,0:T(8,128)(2,1)} %get-tuple-element.89.kr_ref, bf16[96,1152]{1,0:T(8,128)(2,1)} %get-tuple-element.88.vr_ref, ...), custom_call_target="tpu_custom_call", output_to_operand_aliasing={{0}: (6, {}), {1}: (7, {})} | custom-call | flops 1207959552 | bytes 28311552 | tf_op jit(solution)/shard_map/copy_part/pallas_call | solution.py:215
  197.3 1.6 fusion.32
  198.9 1.5 collective-permute-start.6
  200.4 23.4 %collective-permute-done.10 = bf16[2,768,512]{2,1,0:T(8,128)(2,1)} collective-permute-done((bf16[2,768,512]{2,1,0:T(8,128)(2,1)}, bf16[2,768,512]{2,1,0:T(8,128)(2,1)}, u32[]{:S(2)}, u32[]{:S(2)}) %collective-permute-start.10) | collective-permute-done | bytes 1572896 | tf_op jit(solution)/shard_map/ppermute | solution.py:454
  223.8 2.5 fusion.4
  227.4 13.2 %collective-permute-done.6 = bf16[2,768,256]{2,1,0:T(8,128)(2,1)S(1)} collective-permute-done((bf16[2,768,256]{2,1,0:T(8,128)(2,1)S(1)}, bf16[2,768,256]{2,1,0:T(8,128)(2,1)S(1)}, u32[]{:S(2)}, u32[]{:S(2)}) %collective-permute-start.6) | collective-permute-done | bytes 786464 | tf_op jit(solution)/shard_map/ppermute | solution.py:454
  240.6 1.4 fusion.33
  243.3 14.1 %collective-permute-done.11.near_ref = bf16[768,512]{1,0:T(8,128)(2,1)S(1)} collective-permute-done((bf16[768,512]{1,0:T(8,128)(2,1)S(1)}, bf16[768,512]{1,0:T(8,128)(2,1)S(1)}, u32[]{:S(2)}, u32[]{:S(2)}) %collective-permute-start.11) | collective-permute-done | bytes 786464 | tf_op jit(solution)/shard_map/ppermute | solution.py:454
  257.6 0.7 copy-done.6
  258.3 1.2 slice_bitcast_fusion
  259.8 5.1 %collective-permute-done.7.near_ref = bf16[768,256]{1,0:T(8,128)(2,1)S(1)} collective-permute-done((bf16[768,256]{1,0:T(8,128)(2,1)S(1)}, bf16[768,256]{1,0:T(8,128)(2,1)S(1)}, u32[]{:S(2)}, u32[]{:S(2)}) %collective-permute-start.7) | collective-permute-done | bytes 393248 | tf_op jit(solution)/shard_map/ppermute | solution.py:454
  265.0 1.0 fusion.75
  266.0 1.1 copy-done.14
  267.2 16.5 %down_experts.2.refs_4_ = f32[768,576]{1,0:T(8,128)} custom-call(s32[4]{0:T(128)} %get-tuple-element.112.rel_s, s32[9]{0:T(128)} %pad_add_fusion.off_s, bf16[768,512]{1,0:T(8,128)(2,1)} %copy-done.5, bf16[768,512]{1,0:T(8,128)(2,1)} %copy-done.6, bf16[2,768,512]{2,1,0:T(8,128)(2,1)} %copy-done.14, bf16[8,576,2880]{2,1,0:T(8,128)(2,1)} %bitcast.180, ...), custom_call_target="tpu_custom_call" | custom-call | flops 4831838208 | bytes 37748736 | tf_op jit(solution)/shard_map/down_experts/pallas_call | solution.py:360
  283.7 0.9 copy-done.18
  284.6 13.0 %down_experts.3 = bf16[384,576]{1,0:T(8,128)(2,1)} custom-call(s32[4]{0:T(128)} %get-tuple-element.112.rel_s, s32[9]{0:T(128)} %pad_add_fusion.off_s, bf16[768,256]{1,0:T(8,128)(2,1)} %copy-done.17, bf16[768,256]{1,0:T(8,128)(2,1)} %copy-done.16, bf16[2,768,256]{2,1,0:T(8,128)(2,1)} %copy-done.18, bf16[8,576,2880]{2,1,0:T(8,128)(2,1)} %bitcast.188, ...), custom_call_target="tpu_custom_call" | custom-call | flops 2415919104 | bytes 18874368 | tf_op jit(solution)/shard_map/down_experts/pallas_call | solution.py:360
  297.6 1.5 collective-permute-start.13
  299.0 15.7 %copy_part.5 = (bf16[128,1152,128]{2,1,0:T(8,128)(2,1)}, bf16[128,1152,128]{2,1,0:T(8,128)(2,1)}) custom-call(s32[1]{0:T(128)} %bitcast.67.qi, s32[128]{0:T(128)} %len_s.9, bf16[96,1152]{1,0:T(8,128)(2,1)} %get-tuple-element.83.kr_ref, bf16[96,1152]{1,0:T(8,128)(2,1)} %get-tuple-element.82.vr_ref, ...), custom_call_target="tpu_custom_call", output_to_operand_aliasing={{0}: (6, {}), {1}: (7, {})} | custom-call | flops 2415919104 | bytes 56623104 | tf_op jit(solution)/shard_map/copy_part/pallas_call | solution.py:215
  314.7 15.5 %copy_part.6 = (bf16[128,1152,128]{2,1,0:T(8,128)(2,1)}, bf16[128,1152,128]{2,1,0:T(8,128)(2,1)}) custom-call(s32[1]{0:T(128)} %bitcast.63.qi, s32[128]{0:T(128)} %len_s.9, bf16[96,1152]{1,0:T(8,128)(2,1)} %get-tuple-element.118.kr_ref, bf16[96,1152]{1,0:T(8,128)(2,1)} %get-tuple-element.119.vr_ref, ...), custom_call_target="tpu_custom_call", output_to_operand_aliasing={{0}: (6, {}), {1}: (7, {})} | custom-call | flops 2415919104 | bytes 56623104 | tf_op jit(solution)/shard_map/copy_part/pallas_call | solution.py:215
  330.2 9.9 %copy_part.7 = (bf16[128,1152,128]{2,1,0:T(8,128)(2,1)}, bf16[128,1152,128]{2,1,0:T(8,128)(2,1)}) custom-call(s32[1]{0:T(128)} %bitcast.60.qi, s32[128]{0:T(128)} %len_s.9, bf16[96,1152]{1,0:T(8,128)(2,1)} %get-tuple-element.89.kr_ref, bf16[96,1152]{1,0:T(8,128)(2,1)} %get-tuple-element.88.vr_ref, ...), custom_call_target="tpu_custom_call", output_to_operand_aliasing={{0}: (6, {}), {1}: (7, {})} | custom-call | flops 1207959552 | bytes 28311552 | tf_op jit(solution)/shard_map/copy_part/pallas_call | solution.py:215
  340.4 0.9 gather_fusion.6
  341.3 1.0 copy.89
  (184 shorter events, 18.3 us)
Async XLA Ops:
  0.6 40.9 %copy-start = (bf16[576,1152]{1,0:T(8,128)(2,1)S(1)}, bf16[576,1152]{1,0:T(8,128)(2,1)}, u32[]{:S(2)}) copy-start(bf16[576,1152]{1,0:T(8,128)(2,1)} %param.26) | copy-start | bytes 3981316
  4.2 2.4 copy-start.30
  41.6 1.3 copy-start.38
  42.9 1.3 copy-start.39
  45.3 1.3 copy-start.28
  46.5 3.4 collective-permute-start
  51.5 1.1 copy-start.3
  53.5 17.2 %collective-permute-start.1 = (bf16[96,3456]{1,0:T(8,128)(2,1)}, bf16[96,3456]{1,0:T(8,128)(2,1)S(1)}, u32[]{:S(2)}, u32[]{:S(2)}) collective-permute-start(bf16[96,3456]{1,0:T(8,128)(2,1)} %slice.318), channel_id=1, source_target_pairs={{0,2},{2,0},{1,3},{3,1},{4,6},{6,4},{5,7},{7,5}} | collective-permute-start | bytes 1990664 | tf_op jit(solution)/shard_map/ppermute | solution.py:454
  54.2 16.4 %copy-start.4 = (bf16[192,3456]{1,0:T(8,128)(2,1)S(1)}, bf16[192,3456]{1,0:T(8,128)(2,1)}, u32[]{:S(2)}) copy-start(bf16[192,3456]{1,0:T(8,128)(2,1)} %copy-done.3) | copy-start | bytes 3981316
  73.0 27.8 %copy-start.37 = (bf16[576]{0:T(1024)(128)(2,1)S(1)}, bf16[576]{0:T(1024)(128)(2,1)}, u32[]{:S(2)}) copy-start(bf16[576]{0:T(1024)(128)(2,1)} %param.28) | copy-start | bytes 3460
  73.0 27.8 %copy-start.29 = (s32[3,128,2]{1,2,0:T(2,128)S(1)}, s32[3,128,2]{1,2,0:T(2,128)}, u32[]{:S(2)}) copy-start(s32[3,128,2]{1,2,0:T(2,128)} %param.19) | copy-start | bytes 9220
  92.9 9.8 %copy-start.40 = (bf16[1152,576]{0,1:T(8,128)(2,1)S(1)}, bf16[1152,576]{0,1:T(8,128)(2,1)}, u32[]{:S(2)}) copy-start(bf16[1152,576]{0,1:T(8,128)(2,1)} %param.27) | copy-start | bytes 3981316
  94.1 6.6 %collective-permute-start.2 = (bf16[96,1152]{1,0:T(8,128)(2,1)S(1)}, bf16[96,1152]{1,0:T(8,128)(2,1)S(1)}, u32[]{:S(2)}, u32[]{:S(2)}) collective-permute-start(bf16[96,1152]{1,0:T(8,128)(2,1)S(1)} %convert_element_type.216), channel_id=1, source_target_pairs={{0,2},{2,0},{1,3},{3,1},{4,6},{6,4},{5,7},{7,5}} | collective-permute-start | bytes 663560 | tf_op jit(solution)/shard_map/ppermute | solution.py:454
  100.8 1.9 collective-permute-start.3
  104.7 13.3 %copy-start.11 = (bf16[2,192,576]{2,1,0:T(8,128)(2,1)S(1)}, bf16[2,192,576]{2,1,0:T(8,128)(2,1)}, u32[]{:S(2)}) copy-start(bf16[2,192,576]{2,1,0:T(8,128)(2,1)} %get-tuple-element.27) | copy-start | bytes 1327108
  104.7 13.3 %collective-permute-start.4 = (bf16[384,576]{1,0:T(8,128)(2,1)S(1)}, bf16[384,576]{1,0:T(8,128)(2,1)S(1)}, u32[]{:S(2)}, u32[]{:S(2)}) collective-permute-start(bf16[384,576]{1,0:T(8,128)(2,1)S(1)} %convolution_convert_fusion.4), channel_id=1, source_target_pairs={{0,4},{4,0},{1,5},{5,1},{2,6},{6,2},{3,7},{7,3}} | collective-permute-start | bytes 1327112 | tf_op jit(solution)/shard_map/ppermute | solution.py:540
  106.3 12.0 %copy-start.41 = (bf16[576,8]{0,1:T(8,128)(2,1)S(1)}, bf16[576,8]{0,1:T(8,128)(2,1)}, u32[]{:S(2)}) copy-start(bf16[576,8]{0,1:T(8,128)(2,1)} %param.29) | copy-start | bytes 27652
  107.8 19.3 %copy-start.33 = (s32[384]{0:T(512)}, s32[384]{0:T(512)S(1)}, u32[]{:S(2)}) copy-start(s32[384]{0:T(512)S(1)} %eq.81) | copy-start | bytes 4612
  108.6 18.6 %copy-start.35 = (s32[384]{0:T(512)}, s32[384]{0:T(512)S(1)}, u32[]{:S(2)}) copy-start(s32[384]{0:T(512)S(1)} %eq.93) | copy-start | bytes 4612
  118.3 10.7 %copy-start.12 = (bf16[384,576]{1,0:T(8,128)(2,1)}, bf16[384,576]{1,0:T(8,128)(2,1)S(1)}, u32[]{:S(2)}) copy-start(bf16[384,576]{1,0:T(8,128)(2,1)S(1)} %get-tuple-element.67) | copy-start | bytes 1327108
  125.9 0.6 copy-start.19
  125.9 1.2 copy-start.21
  126.0 1.1 copy-start.23
  126.0 1.1 copy-start.25
  127.1 24.3 %copy-start.31 = (f32[384]{0:T(512)}, f32[384]{0:T(512)S(1)}, u32[]{:S(2)}) copy-start(f32[384]{0:T(512)S(1)} %add_rsqrt_fusion) | copy-start | bytes 4612
  128.9 24.5 %copy-start.2 = (s32[4]{0:T(128)S(1)}, s32[4]{0:T(128)}, u32[]{:S(2)}) copy-start(s32[4]{0:T(128)} %constant.79.clone) | copy-start | bytes 52
  129.0 25.1 %copy-start.8 = (bf16[96,1152]{1,0:T(8,128)(2,1)S(1)}, bf16[96,1152]{1,0:T(8,128)(2,1)}, u32[]{:S(2)}) copy-start(bf16[96,1152]{1,0:T(8,128)(2,1)} %slice.329.vr_ref) | copy-start | bytes 663556
  129.0 25.1 %copy-start.9 = (bf16[96,1152]{1,0:T(8,128)(2,1)S(1)}, bf16[96,1152]{1,0:T(8,128)(2,1)}, u32[]{:S(2)}) copy-start(bf16[96,1152]{1,0:T(8,128)(2,1)} %get-tuple-element.70.kr_ref) | copy-start | bytes 663556
  151.5 31.7 %collective-permute-start.9 = (bf16[2,2,768,512]{3,2,1,0:T(8,128)(2,1)}, bf16[2,2,768,512]{3,2,1,0:T(8,128)(2,1)}, u32[]{:S(2)}, u32[]{:S(2)}) collective-permute-start(bf16[2,2,768,512]{3,2,1,0:T(8,128)(2,1)} %get-tuple-element.36), channel_id=1, source_target_pairs={{0,1},{1,0},{2,3},{3,2},{4,5},{5,4},{6,7},{7,6}} | collective-permute-start | bytes 9437192 | tf_op jit(solution)/shard_map/ppermute | solution.py:451
  154.2 12.4 %collective-permute-start.14 = (bf16[96,2304]{1,0:T(8,128)(2,1)S(1)}, bf16[96,2304]{1,0:T(8,128)(2,1)S(1)}, u32[]{:S(2)}, u32[]{:S(2)}) collective-permute-start(bf16[96,2304]{1,0:T(8,128)(2,1)S(1)} %get-tuple-element.87), channel_id=1, source_target_pairs={{0,2},{2,0},{1,3},{3,1},{4,6},{6,4},{5,7},{7,5}} | collective-permute-start | bytes 1327112 | tf_op jit(solution)/shard_map/ppermute | solution.py:454
  167.6 90.7 %collective-permute-start.15 = (bf16[2,96,2304]{2,1,0:T(8,128)(2,1)}, bf16[2,96,2304]{2,1,0:T(8,128)(2,1)}, u32[]{:S(2)}, u32[]{:S(2)}) collective-permute-start(bf16[2,96,2304]{2,1,0:T(8,128)(2,1)} %pad_maximum_fusion.2), channel_id=1, source_target_pairs={{0,1},{1,0},{2,3},{3,2},{4,5},{5,4},{6,7},{7,6}} | collective-permute-start | bytes 2654216 | tf_op jit(solution)/shard_map/ppermute | solution.py:451
  168.4 14.8 %copy-start.7 = (bf16[2,2,768,512]{3,2,1,0:T(8,128)(2,1)S(1)}, bf16[2,2,768,512]{3,2,1,0:T(8,128)(2,1)}, u32[]{:S(2)}) copy-start(bf16[2,2,768,512]{3,2,1,0:T(8,128)(2,1)} %get-tuple-element.35) | copy-start | bytes 9437188
  182.6 14.7 %collective-permute-start.5 = (bf16[2,2,768,256]{3,2,1,0:T(8,128)(2,1)}, bf16[2,2,768,256]{3,2,1,0:T(8,128)(2,1)}, u32[]{:S(2)}, u32[]{:S(2)}) collective-permute-start(bf16[2,2,768,256]{3,2,1,0:T(8,128)(2,1)} %get-tuple-element.34), channel_id=1, source_target_pairs={{0,1},{1,0},{2,3},{3,2},{4,5},{5,4},{6,7},{7,6}} | collective-permute-start | bytes 4718600 | tf_op jit(solution)/shard_map/ppermute | solution.py:451
  186.3 37.6 %collective-permute-start.10 = (bf16[2,768,512]{2,1,0:T(8,128)(2,1)}, bf16[2,768,512]{2,1,0:T(8,128)(2,1)}, u32[]{:S(2)}, u32[]{:S(2)}) collective-permute-start(bf16[2,768,512]{2,1,0:T(8,128)(2,1)} %fusion.3), channel_id=1, source_target_pairs={{0,2},{2,0},{1,3},{3,1},{4,6},{6,4},{5,7},{7,5}} | collective-permute-start | bytes 4718600 | tf_op jit(solution)/shard_map/ppermute | solution.py:454
  186.8 10.0 %copy-start.27 = (f32[4,1,384]{2,1,0:T(1,128)S(1)}, f32[4,1,384]{2,1,0:T(1,128)}, u32[]{:S(2)}) copy-start(f32[4,1,384]{2,1,0:T(1,128)} %get-tuple-element.65) | copy-start | bytes 18436
  186.8 10.0 %copy-start.32 = (f32[384]{0:T(512)S(1)}, f32[384]{0:T(512)}, u32[]{:S(2)}) copy-start(f32[384]{0:T(512)} %copy-done.31) | copy-start | bytes 4612
  186.8 10.0 %copy-start.20 = (f32[1,9,384]{2,1,0:T(8,128)S(1)}, f32[1,9,384]{2,1,0:T(8,128)}, u32[]{:S(2)}) copy-start(f32[1,9,384]{2,1,0:T(8,128)} %copy-done.19) | copy-start | bytes 41476
  186.8 10.0 %copy-start.22 = (f32[1,9,384]{2,1,0:T(8,128)S(1)}, f32[1,9,384]{2,1,0:T(8,128)}, u32[]{:S(2)}) copy-start(f32[1,9,384]{2,1,0:T(8,128)} %copy-done.21) | copy-start | bytes 41476
  186.8 10.0 %copy-start.24 = (f32[1,9,384]{2,1,0:T(8,128)S(1)}, f32[1,9,384]{2,1,0:T(8,128)}, u32[]{:S(2)}) copy-start(f32[1,9,384]{2,1,0:T(8,128)} %copy-done.23) | copy-start | bytes 41476
  186.8 10.0 %copy-start.26 = (f32[1,9,384]{2,1,0:T(8,128)S(1)}, f32[1,9,384]{2,1,0:T(8,128)}, u32[]{:S(2)}) copy-start(f32[1,9,384]{2,1,0:T(8,128)} %copy-done.25) | copy-start | bytes 41476
  186.8 10.2 %copy-start.34 = (s32[384]{0:T(512)S(1)}, s32[384]{0:T(512)}, u32[]{:S(2)}) copy-start(s32[384]{0:T(512)} %copy-done.33) | copy-start | bytes 4612
  186.8 10.2 %copy-start.36 = (s32[384]{0:T(512)S(1)}, s32[384]{0:T(512)}, u32[]{:S(2)}) copy-start(s32[384]{0:T(512)} %copy-done.35) | copy-start | bytes 4612
  198.9 41.7 %collective-permute-start.6 = (bf16[2,768,256]{2,1,0:T(8,128)(2,1)S(1)}, bf16[2,768,256]{2,1,0:T(8,128)(2,1)S(1)}, u32[]{:S(2)}, u32[]{:S(2)}) collective-permute-start(bf16[2,768,256]{2,1,0:T(8,128)(2,1)S(1)} %fusion.32), channel_id=1, source_target_pairs={{0,2},{2,0},{1,3},{3,1},{4,6},{6,4},{5,7},{7,5}} | collective-permute-start | bytes 2359304 | tf_op jit(solution)/shard_map/ppermute | solution.py:454
  226.4 14.2 %copy-start.15 = (bf16[2,2,768,256]{3,2,1,0:T(8,128)(2,1)S(1)}, bf16[2,2,768,256]{3,2,1,0:T(8,128)(2,1)}, u32[]{:S(2)}) copy-start(bf16[2,2,768,256]{3,2,1,0:T(8,128)(2,1)} %get-tuple-element.33) | copy-start | bytes 4718596
  226.9 15.2 %copy-start.5 = (bf16[768,512]{1,0:T(8,128)(2,1)}, bf16[768,512]{1,0:T(8,128)(2,1)S(1)}, u32[]{:S(2)}) copy-start(bf16[768,512]{1,0:T(8,128)(2,1)S(1)} %fusion.6.own_ref) | copy-start | bytes 2359300
  226.9 30.6 %collective-permute-start.11 = (bf16[768,512]{1,0:T(8,128)(2,1)S(1)}, bf16[768,512]{1,0:T(8,128)(2,1)S(1)}, u32[]{:S(2)}, u32[]{:S(2)}) collective-permute-start(bf16[768,512]{1,0:T(8,128)(2,1)S(1)} %fusion.6.own_ref), channel_id=1, source_target_pairs={{0,2},{2,0},{1,3},{3,1},{4,6},{6,4},{5,7},{7,5}} | collective-permute-start | bytes 2359304 | tf_op jit(solution)/shard_map/ppermute | solution.py:454
  242.3 1.0 copy-start.17
  242.3 22.6 %collective-permute-start.7 = (bf16[768,256]{1,0:T(8,128)(2,1)S(1)}, bf16[768,256]{1,0:T(8,128)(2,1)S(1)}, u32[]{:S(2)}, u32[]{:S(2)}) collective-permute-start(bf16[768,256]{1,0:T(8,128)(2,1)S(1)} %fusion.34.own_ref), channel_id=1, source_target_pairs={{0,2},{2,0},{1,3},{3,1},{4,6},{6,4},{5,7},{7,5}} | collective-permute-start | bytes 1179656 | tf_op jit(solution)/shard_map/ppermute | solution.py:454
  257.4 0.9 copy-start.6
  258.3 7.7 %collective-permute-start.12 = (bf16[2,768,512]{2,1,0:T(8,128)(2,1)S(1)}, bf16[2,768,512]{2,1,0:T(8,128)(2,1)S(1)}, u32[]{:S(2)}, u32[]{:S(2)}) collective-permute-start(bf16[2,768,512]{2,1,0:T(8,128)(2,1)S(1)} %pad_maximum_fusion.1), channel_id=1, source_target_pairs={{0,1},{1,0},{2,3},{3,2},{4,5},{5,4},{6,7},{7,6}} | collective-permute-start | bytes 4718600 | tf_op jit(solution)/shard_map/ppermute | solution.py:451
  264.9 1.1 copy-start.16
  265.0 18.7 %collective-permute-start.8 = (bf16[2,768,256]{2,1,0:T(8,128)(2,1)S(1)}, bf16[2,768,256]{2,1,0:T(8,128)(2,1)S(1)}, u32[]{:S(2)}, u32[]{:S(2)}) collective-permute-start(bf16[2,768,256]{2,1,0:T(8,128)(2,1)S(1)} %pad_maximum_fusion.3), channel_id=1, source_target_pairs={{0,1},{1,0},{2,3},{3,2},{4,5},{5,4},{6,7},{7,6}} | collective-permute-start | bytes 2359304 | tf_op jit(solution)/shard_map/ppermute | solution.py:451
  266.0 1.1 copy-start.14
  283.7 0.9 copy-start.18
  297.6 42.6 %collective-permute-start.13 = (bf16[384,576]{1,0:T(8,128)(2,1)}, bf16[384,576]{1,0:T(8,128)(2,1)S(1)}, u32[]{:S(2)}, u32[]{:S(2)}) collective-permute-start(bf16[384,576]{1,0:T(8,128)(2,1)} %down_experts.3), channel_id=1, source_target_pairs={{0,4},{4,0},{1,5},{5,1},{2,6},{6,2},{3,7},{7,3}} | collective-permute-start | bytes 1327112 | tf_op jit(solution)/shard_map/ppermute | solution.py:540
  330.2 9.9 %copy-start.10 = (bf16[384,576]{1,0:T(8,128)(2,1)S(1)}, bf16[384,576]{1,0:T(8,128)(2,1)}, u32[]{:S(2)}) copy-start(bf16[384,576]{1,0:T(8,128)(2,1)} %down_experts.3) | copy-start | bytes 1327108
  330.2 9.9 %copy-start.13 = (bf16[384,576]{1,0:T(8,128)(2,1)S(1)}, bf16[384,576]{1,0:T(8,128)(2,1)}, u32[]{:S(2)}) copy-start(bf16[384,576]{1,0:T(8,128)(2,1)} %copy-done.12) | copy-start | bytes 1327108
  340.2 2.1 copy-start.1

commit v3 on v2

--- a/solution.py
+++ b/solution.py
@@ -24,27 +24,47 @@
     return pltpu.CompilerParams(vmem_limit_bytes=VMEM_BYTES, **kw)
 
 
-def gather_rows(tokens, emb_table):
-    n_tok = tokens.shape[0]
+def gather_rows(where, tokens, emb_table, n_tok, per_q, x_count):
+    steps, n_batch = tokens.shape
     vocab, width = emb_table.shape
     last_tile = vocab // LANES - 1
     tail_at = (last_tile + 1) * LANES
-    n_tail = vocab - tail_at
+    block_rows = steps * per_q
+    n_block = n_tok // block_rows
     n_groups = n_tok // GROUP
     per_chunk = LANES // GROUP
     n_chunks = (n_tok + LANES - 1) // LANES
 
-    def kernel(tok_s, tokv_ref, tail_ref, emb_ref, out_ref, sq_ref, buf, acc, sems):
-        def copy(g, i):
-            tile = jnp.minimum(tok_s[g * GROUP + i] // LANES, last_tile)
+    def kernel(where_s, tok_s, tail_ref, emb_ref, out_ref, sq_ref, buf, acc, mine_s, sems):
+        for k in range(n_block):
+            quarter = lax.bitwise_xor(where_s[0], ORDER[k])
+            for y in range(1, x_count // n_block):
+                quarter = jnp.where(where_s[1] == y, lax.bitwise_xor(where_s[0], ORDER[y * n_block + k]), quarter)
+            for t in range(steps):
+                def note(bl, carry, k=k, t=t, quarter=quarter):
+                    mine_s[k * block_rows + t * per_q + bl] = tok_s[t * n_batch + quarter * per_q + bl]
+                    return carry
+
+                lax.fori_loop(0, per_q, note, 0)
+
+        def copy(g, i, tail=False):
+            tile = jnp.minimum(mine_s[g * GROUP + i] // LANES, last_tile)
             slot = lax.rem(g, SLOTS)
             return pltpu.make_async_copy(
-                emb_ref.at[:, pl.ds(pl.multiple_of(tile * LANES, LANES), LANES)],
+                tail_ref if tail else emb_ref.at[:, pl.ds(pl.multiple_of(tile * LANES, LANES), LANES)],
                 buf.at[slot, :, pl.ds(i * LANES, LANES)], sems.at[slot, i])
 
         def start(g):
             for i in range(GROUP):
-                copy(g, i).start()
+                in_tail = mine_s[g * GROUP + i] >= tail_at
+
+                @pl.when(in_tail)
+                def _():
+                    copy(g, i, True).start()
+
+                @pl.when(jnp.logical_not(in_tail))
+                def _():
+                    copy(g, i).start()
 
         for g in range(SLOTS - 1):
             start(g)
@@ -63,8 +83,7 @@
             base = lax.rem(g, per_chunk) * GROUP
             picks = []
             for i in range(GROUP):
-                tok = tok_s[g * GROUP + i]
-                lane = jnp.where(tok < tail_at, lax.rem(tok, LANES), -1)
+                lane = lax.rem(mine_s[g * GROUP + i], LANES)
                 picks.append(((lane_id == lane) & (col_id == base + i)).astype(F32).astype(BF16))
             pick = jnp.concatenate(picks, axis=0)
             for m in range(2):
@@ -77,9 +96,6 @@
         for c in range(n_chunks):
             size = min(LANES, n_tok - c * LANES)
             rows = jnp.transpose(acc[c])[:size]
-            tok_col = tokv_ref[pl.ds(c * LANES, size), :]
-            for k in range(n_tail):
-                rows = jnp.where(tok_col == tail_at + k, tail_ref[pl.ds(k, 1), :].astype(F32), rows)
             out_ref[pl.ds(c * LANES, size), :] = rows.astype(BF16)
             sq_ref[pl.ds(c * LANES, size), :] = jnp.sum(rows * rows, axis=1, keepdims=True)
 
@@ -87,14 +103,14 @@
         kernel,
         out_shape=(jax.ShapeDtypeStruct((n_tok, width), BF16), jax.ShapeDtypeStruct((n_tok, 1), F32)),
         grid_spec=pltpu.PrefetchScalarGridSpec(
-            num_scalar_prefetch=1, grid=(),
-            in_specs=[pl.BlockSpec(memory_space=pltpu.VMEM), pl.BlockSpec(memory_space=pltpu.VMEM), pl.BlockSpec(memory_space=pl.ANY)],
+            num_scalar_prefetch=2, grid=(),
+            in_specs=[pl.BlockSpec(memory_space=pl.ANY)] * 2,
             out_specs=[pl.BlockSpec(memory_space=pltpu.VMEM)] * 2,
-            scratch_shapes=[pltpu.VMEM((SLOTS, width, GROUP * LANES), BF16), pltpu.VMEM((n_chunks, width, LANES), F32), pltpu.SemaphoreType.DMA((SLOTS, GROUP))]),
+            scratch_shapes=[pltpu.VMEM((SLOTS, width, GROUP * LANES), BF16), pltpu.VMEM((n_chunks, width, LANES), F32), pltpu.SMEM((n_tok,), jnp.int32), pltpu.SemaphoreType.DMA((SLOTS, GROUP))]),
         compiler_params=params(),
         cost_estimate=pl.CostEstimate(flops=2 * n_tok * width * LANES * LANES, bytes_accessed=n_tok * width * LANES * 2, transcendentals=0),
         name="gather_rows",
-    )(tokens, tokens[:, None], emb_table[tail_at:], emb_table.T)
+    )(where, tokens.reshape(-1), jnp.pad(emb_table[tail_at:].T, ((0, 0), (0, LANES - (vocab - tail_at)))), emb_table.T)
 
 
 def column_scratch(rows_ref, out_ref):
@@ -124,7 +140,7 @@
     return pl.BlockSpec((step_b, kv_width, slots), lambda g, qi, ln: (qi[0] * n_grid + skip + g, 0, 0))
 
 
-def attend_quarter(quarter, lengths, q_rows, k_rows, v_rows, k_cache, v_cache, heads, steps):
+def attend_part(quarter, lengths, q_rows, k_rows, v_rows, k_cache, v_cache, caches, heads, steps, part, n_parts):
     _, kv_width, slots = k_cache.shape
     per_q = q_rows.shape[0] // steps
     head = kv_width // heads
@@ -132,7 +148,8 @@
     step_b = 4
     n_grid = per_q // step_b
 
-    def kernel(qi, len_s, q_ref, kr_ref, vr_ref, kc_ref, vc_ref, o_ref, ko_ref, vo_ref, k_cols, v_cols):
+    def kernel(qi, len_s, q_ref, kr_ref, vr_ref, kc_ref, vc_ref, *refs):
+        o_ref, ko_ref, vo_ref, k_cols, v_cols = refs[-5:]
         g = pl.program_id(0)
 
         @pl.when(g == 0)
@@ -146,7 +163,7 @@
         srow_t = lax.broadcasted_iota(jnp.int32, (steps * h_pad, slots), 0) // h_pad
         scol = lax.broadcasted_iota(jnp.int32, (steps * h_pad, slots), 1)
         bls = [g * step_b + i for i in range(step_b)]
-        poss = [len_s[qi[0] * per_q + bl] for bl in bls]
+        poss = [len_s[(qi[0] * n_parts + part) * per_q + bl] for bl in bls]
         picks, keeps = zip(*[slot_masks(pos, bl, per_q, steps, slots) for pos, bl in zip(poss, bls)])
         for i in range(0, step_b, 2):
             for src, cols, dst in ((kc_ref, k_cols, ko_ref), (vc_ref, v_cols, vo_ref)):
@@ -170,20 +187,22 @@
                 piece = jnp.where(diag, mix[t * h_pad:(t + 1) * h_pad], 0.0)
                 o_ref[pl.ds(t * per_q + bl, 1), :] = jnp.sum(piece, axis=0, keepdims=True)
 
-    cache_in = cache_specs(k_cache, n_grid, step_b)
+    cache_in = cache_specs(k_cache, n_grid * n_parts, step_b, part * n_grid)
+    anyspec = [pl.BlockSpec(memory_space=pl.ANY)] * len(caches)
     whole = lambda a: pl.BlockSpec(a.shape, lambda g, qi, ln: (0, 0))
     return pl.pallas_call(
         kernel,
         out_shape=(jax.ShapeDtypeStruct(q_rows.shape, F32), jax.ShapeDtypeStruct(k_cache.shape, BF16), jax.ShapeDtypeStruct(v_cache.shape, BF16)),
         grid_spec=pltpu.PrefetchScalarGridSpec(
             num_scalar_prefetch=2, grid=(n_grid,),
-            in_specs=[whole(q_rows), whole(k_rows), whole(v_rows), cache_in, cache_in],
+            in_specs=[whole(q_rows), whole(k_rows), whole(v_rows), cache_in, cache_in] + anyspec,
             out_specs=[pl.BlockSpec(q_rows.shape, lambda g, qi, ln: (0, 0)), cache_in, cache_in],
             scratch_shapes=[pltpu.VMEM((kv_width, LANES), BF16)] * 2),
+        input_output_aliases={7: 1, 8: 2} if caches else {},
         compiler_params=params(),
         cost_estimate=pl.CostEstimate(flops=4 * per_q * kv_width * LANES * LANES, bytes_accessed=8 * per_q * kv_width * slots, transcendentals=0),
-        name="attend_quarter",
-    )(quarter, lengths, q_rows, k_rows, v_rows, k_cache, v_cache)
+        name="attend_part",
+    )(quarter, lengths, q_rows, k_rows, v_rows, k_cache, v_cache, *caches)
 
 
 def copy_part(quarter, lengths, k_rows, v_rows, k_cache, v_cache, k_out, v_out, steps, part, n_parts, step_b):
@@ -254,6 +273,7 @@
     experts, _, ff = w_act.shape
     parts, nb = rel.shape[0], len(blocks)
     n_w = parts * nb
+    ragged = [b for b in blocks if ((parts - 1) * per_quarter + b + 1) * BLOCK > ff]
 
     def kernel(rel_s, off_s, x_ref, *refs):
         a_refs, l_refs, (keep_ref, send_ref) = refs[:n_w], refs[n_w:2 * n_w], refs[2 * n_w:]
@@ -264,18 +284,18 @@
             x = x_ref[ds, :]
             for i in range(parts):
                 for n, b in enumerate(blocks):
-                    ok = mine & (lane + (rel_s[i] * per_quarter + b) * BLOCK < ff)
+                    ok = mine & (lane + (rel_s[i] * per_quarter + b) * BLOCK < ff) if b in ragged else mine
                     for k, w_refs in enumerate((a_refs, l_refs)):
                         out_ref = (keep_ref if i < 2 else send_ref).at[i % 2, k]
                         cols = pl.ds(n * BLOCK, BLOCK)
                         y = jnp.dot(x, w_refs[i * nb + n][0], preferred_element_type=F32)
                         out_ref[ds, cols] = jnp.where(ok, y, out_ref[ds, cols].astype(F32)).astype(BF16)
 
-        @pl.when(e == 0)
-        def _():
-            keep_ref[...] = jnp.zeros_like(keep_ref)
-            send_ref[...] = jnp.zeros_like(send_ref)
-
+        if any(b in ragged for b in blocks):
+            @pl.when(e == 0)
+            def _():
+                keep_ref[...] = jnp.zeros_like(keep_ref)
+                send_ref[...] = jnp.zeros_like(send_ref)
         expert_tiles(off_s, e, n_rows, body)
 
     shape = (2, 2, n_rows, nb * BLOCK)
@@ -463,6 +483,8 @@
         n_tok = steps * n_batch
         per_q = n_batch // x_count
         q_rows_n = steps * per_q
+        n_group = 2
+        g_rows = q_rows_n // n_group
         xi = lax.axis_index('x')
         order = jnp.array(ORDER, jnp.int32)
         rel = lax.bitwise_xor(order, xi)
@@ -481,8 +503,7 @@
 
         yi = lax.axis_index('y')
         y_rows = n_tok // 2
-        my_tokens = lax.dynamic_slice(to_rel(tokens), (yi * y_rows,), (y_rows,))
-        my_rows, my_sq = gather_rows(my_tokens, emb_table)
+        my_rows, my_sq = gather_rows(jnp.stack([xi, yi]), tokens, emb_table, y_rows, per_q, x_count)
         both_rows, each_sq = share_rows(my_rows, jnp.pad(my_sq.reshape(2, 1, q_rows_n), ((0, 0), (0, 7), (0, 0))))
         x_in = both_rows.reshape(n_tok, width)
         found = [[ORDER[ORDER[i] ^ d] for d in range(x_count)] for i in range(x_count)]
@@ -504,11 +525,6 @@
         choice_a = to_rel(choices[:, :, 0])
         choice_b = to_rel(choices[:, :, 1])
 
-        half = n_tok // 2
-        got = over_core(part[half:])
-        part = (part[:half].astype(F32) + got.astype(F32)).astype(BF16)
-        got = over_chip(part[q_rows_n:])
-        proj = (part[:q_rows_n].astype(F32) + got.astype(F32)).astype(BF16).astype(F32)
         len_q = lax.dynamic_slice(lengths_r, (xi * per_q,), (per_q,))
         positions = (len_q[None, :] + jnp.arange(steps)[:, None]).reshape(q_rows_n).astype(F32)
         inv_freq = ROPE_BASE ** (-(jnp.arange(head // 2, dtype=F32) * 2.0 / head))
@@ -516,19 +532,39 @@
         cosine, sine = jnp.cos(angles), jnp.sin(angles)
         low_half = (jnp.arange(kv_width) % head < head // 2)[None, :]
 
-        def rotate(v):
+        def rotate(v, cosine, sine):
             other = jnp.where(low_half, -jnp.roll(v, -(head // 2), axis=1), jnp.roll(v, head // 2, axis=1))
             return (v * cosine + other * sine).astype(BF16)
 
-        queries = rotate(proj[:, :kv_width]).astype(F32)
-        kv_new = jnp.concatenate([rotate(proj[:, kv_width:2 * kv_width]), proj[:, 2 * kv_width:].astype(BF16)], axis=1)
+        def grouped(a):
+            return a.reshape(a.shape[0] // per_q, n_group, per_q // n_group, -1)
+
+        cosine, sine = grouped(cosine), grouped(sine)
+        part = part.reshape(x_count, steps, n_group, per_q // n_group, -1)
+        firsts = []
+        for g in range(n_group):
+            one = part[:, :, g].reshape(x_count, g_rows, -1)
+            got = over_core(one[2:])
+            mine, away = ((one[i].astype(F32) + got[i].astype(F32)).astype(BF16) for i in range(2))
+            firsts.append((mine, over_chip(away)))
         k_view = k_cache.transpose(0, 2, 3, 1).reshape(n_batch, kv_width, -1)
         v_view = v_cache.transpose(0, 2, 3, 1).reshape(n_batch, kv_width, -1)
-        mixed, k_out, v_out = attend_quarter(xi[None], lengths, queries, kv_new[:, :kv_width], kv_new[:, kv_width:], k_view, v_view, heads, steps)
-        mixed = mixed.astype(BF16)
-        mixed2 = jnp.concatenate([mixed, over_chip(mixed)], axis=0)
-        mixed4 = jnp.concatenate([mixed2, over_core(mixed2)], axis=0)
-        attn = jnp.dot(mixed4, w_o, preferred_element_type=F32).astype(BF16)
+        caches, kv_groups, mixed_groups = (), [], []
+        for g, (mine, got) in enumerate(firsts):
+            proj = (mine.astype(F32) + got.astype(F32)).astype(BF16).astype(F32)
+            cos_g, sin_g = cosine[:, g].reshape(g_rows, -1), sine[:, g].reshape(g_rows, -1)
+            queries = rotate(proj[:, :kv_width], cos_g, sin_g).astype(F32)
+            keys = rotate(proj[:, kv_width:2 * kv_width], cos_g, sin_g)
+            vals = proj[:, 2 * kv_width:].astype(BF16)
+            mixed, *caches = attend_part(xi[None], lengths, queries, keys, vals, k_view, v_view, caches, heads, steps, g, n_group)
+            kv_groups.append(jnp.concatenate([keys, vals], axis=1).reshape(steps, per_q // n_group, -1))
+            mixed = mixed.astype(BF16)
+            mixed_groups.append(jnp.stack([mixed, over_chip(mixed)]))
+        attn_groups = []
+        for mixed2 in mixed_groups:
+            mixed4 = jnp.concatenate([mixed2, over_core(mixed2)], axis=0).reshape(x_count * g_rows, -1)
+            attn_groups.append(jnp.dot(mixed4, w_o, preferred_element_type=F32).astype(BF16))
+        kv_new = jnp.stack(kv_groups, axis=1).reshape(q_rows_n, -1)
 
         kv_pair = jnp.stack([kv_new, over_chip(kv_new)])
         kv_far = over_core(kv_pair)
@@ -540,8 +576,7 @@
             got = lax.ppermute(v, 'y', [(0, 1), (1, 0)])
             return v.astype(F32) + got.astype(F32)
 
-        caches = write((k_out, v_out), kv_pair[1], 2, 0, 2, 4)
-        attn_sum = add_over_y(attn)
+        attn_sum = jnp.stack([add_over_y(v).reshape(x_count, steps, per_q // n_group, width) for v in attn_groups], axis=2).reshape(n_tok, width)
         x_mid = (x_in.astype(F32) + attn_sum).astype(BF16)
 
         x_mid32 = x_mid.astype(F32)
@@ -589,6 +624,7 @@
         unit0 = activate(mine0, got0)
         caches = write(caches, kv_far[0], 1, 0, 1, 8)
         caches = write(caches, kv_far[1], 3, 0, 1, 8)
+        caches = write(caches, kv_pair[1], 2, 0, 2, 4)
         unit1 = activate(mine1, got1)
         moe = down(unit0, None, first_blocks, False)
         moe = down(unit1, moe, last_blocks, True)

time: 344 us -> 358 us (1.041)
  waiting for transfers between devices: 101 us -> 109 us
  starting transfers between devices: 8.71 us -> 12.9 us
    ppermute x7 -> x9, waiting for transfers between devices: 87.4 us -> 97.9 us  [over_chip(): return lax.ppermute(v, 'x', CHIP_PERM)]
    ppermute x7 -> x9, waiting for transfers between devices: 4.69 us -> 0.3 us  [over_core(): return lax.ppermute(v, 'x', CORE_PERM)]
    ppermute x7 -> x9, starting transfers between devices: 4.81 us -> 8.16 us  [over_chip(): return lax.ppermute(v, 'x', CHIP_PERM)]
    pallas_call x1 -> x2, Pallas kernels: 19.9 us -> 22.7 us  [attend_part(): pl.pallas_call(kernel, out_shape=(jax.ShapeDtypeStruct(q_rows.shape, F32)...]
    ppermute x2 -> x3, waiting for transfers between devices: 8.82 us -> 10.5 us  [add_over_y(): got = lax.ppermute(v, 'y', [(0, 1), (1, 0)])]
  transfers between devices with their start and end apart: 16 -> 21, of which waited for: 10 -> 12; matrix products, arithmetic and copies ran while one was open for 7% -> 8% of each run, Pallas kernels for 24% -> 23%
where the time goes in v3:
time: 358 us; the launch traced here: 357 us
  Pallas kernels  177 us (49%)
  waiting for transfers between devices  109 us (30%)
  other arithmetic  25.1 us (7%)
  local copies, waits for them, and re-layouts  24.9 us (7%)
  starting transfers between devices  12.9 us (4%)
  matrix products  6.48 us (2%)
    ppermute x9, waiting for transfers between devices, over_chip(): return lax.ppermute(v, 'x', CHIP_PERM)  97.9 us
    pallas_call x4, Pallas kernels, copy_part(): pl.pallas_call(kernel, out_shape=(jax.ShapeDtypeStruct(k_cache.shape, BF1...  50.9 us
    pallas_call x2, Pallas kernels, up_experts(): pl.pallas_call(kernel, out_shape=(jax.ShapeDtypeStruct(shape, BF16),) * 2...  36.2 us
    pallas_call x2, Pallas kernels, down_experts(): pl.pallas_call(kernel, out_shape=out_shape, grid_spec=pltpu.PrefetchScala...  29.5 us
    pallas_call x2, Pallas kernels, attend_part(): pl.pallas_call(kernel, out_shape=(jax.ShapeDtypeStruct(q_rows.shape, F32)...  22.7 us
    pallas_call x1, Pallas kernels, gather_rows(): pl.pallas_call(kernel, out_shape=(jax.ShapeDtypeStruct((n_tok, width), BF...  18.3 us
    pallas_call x1, Pallas kernels, share_rows(): pl.pallas_call(kernel, out_shape=(jax.ShapeDtypeStruct((n_y,) + rows.shap...  13.6 us
    ppermute x3, waiting for transfers between devices, add_over_y(): got = lax.ppermute(v, 'y', [(0, 1), (1, 0)])  10.5 us
  transfers between devices with their start and end apart: 21, of which 12 were waited for; matrix products, arithmetic and copies ran while one was open for 8% of the time, Pallas kernels for 23%

profile of v3, /device:TPU:0, one launch (start us, length us, event | category | flops | bytes accessed | tf_op | source)
XLA Modules:
  0.0 356.6 jit_solution(3726520053055151662)
XLA Ops:
  0.7 1.0 slice_bitcast_fusion.6
  3.0 18.3 %gather_rows.1 = (bf16[192,576]{1,0:T(8,128)(2,1)}, f32[192,1]{1,0:T(8,128)}) custom-call(s32[2]{0:T(128)} %pad_add_fusion.where_s, s32[384]{0:T(512)} %bitcast.333, bf16[576,128]{1,0:T(8,128)(2,1)} %pad.12.tail_ref, bf16[576,122753]{1,0:T(8,128)(2,1)} %bitcast.4.emb_ref), custom_call_target="tpu_custom_call" | custom-call | flops 3623878656 | bytes 28311552 | tf_op jit(solution)/shard_map/gather_rows/pallas_call | solution.py:102
  21.4 1.0 reduce.5
  23.1 13.6 %share_rows.1 = (bf16[2,192,576]{2,1,0:T(8,128)(2,1)}, f32[4,2,2,8,96]{4,3,2,1,0:T(8,128)}) custom-call(bf16[192,576]{1,0:T(8,128)(2,1)} %get-tuple-element.28.rows_ref, f32[2,8,96]{2,1,0:T(8,128)} %pad.13.sums_ref), custom_call_target="tpu_custom_call" | custom-call | bytes 16000000 | tf_op jit(solution)/shard_map/share_rows/pallas_call | solution.py:421
  36.7 0.8 add_bitcast_fusion.3
  37.6 1.2 fusion.25
  38.8 0.9 convolution_convert_fusion
  40.1 0.9 convolution_convert_fusion.1
  41.5 0.9 convolution_convert_fusion.2
  42.6 1.1 fusion.80
  44.2 0.9 fusion.79
  51.0 1.1 fusion.34
  52.6 1.1 fusion.36
  53.7 1.5 collective-permute-start.1
  55.2 7.5 %collective-permute-done.6 = bf16[48,3456]{1,0:T(8,128)(2,1)S(1)} collective-permute-done((bf16[48,3456]{1,0:T(8,128)(2,1)S(1)}, bf16[48,3456]{1,0:T(8,128)(2,1)S(1)}, u32[]{:S(2)}, u32[]{:S(2)}) %collective-permute-start.6) | collective-permute-done | bytes 331808 | tf_op jit(solution)/shard_map/ppermute | solution.py:474
  62.8 1.1 fusion.78
  64.8 4.3 %collective-permute-done.1 = bf16[48,3456]{1,0:T(8,128)(2,1)S(1)} collective-permute-done((bf16[48,3456]{1,0:T(8,128)(2,1)S(1)}, bf16[48,3456]{1,0:T(8,128)(2,1)S(1)}, u32[]{:S(2)}, u32[]{:S(2)}) %collective-permute-start.1) | collective-permute-done | bytes 331808 | tf_op jit(solution)/shard_map/ppermute | solution.py:474
  69.0 1.1 fusion.77
  71.0 0.9 fusion.51
  71.9 11.3 %attend_part.2 = (f32[48,1152]{1,0:T(8,128)}, bf16[128,1152,128]{2,1,0:T(8,128)(2,1)}, bf16[128,1152,128]{2,1,0:T(8,128)(2,1)}) custom-call(s32[1]{0:T(128)} %bitcast.qi, s32[128]{0:T(128)} %len_s.11, f32[48,1152]{1,0:T(8,128)} %get-tuple-element.83.q_ref, bf16[48,1152]{1,0:T(8,128)(2,1)} %get-tuple-element.82.kr_ref, bf16[48,1152]{1,0:T(8,128)(2,1)} %slice.445.vr_ref, ...), custom_call_target="tpu_custom_call" | custom-call | flops 1207959552 | bytes 18874368 | tf_op jit(solution)/shard_map/attend_part/pallas_call | solution.py:193
  83.2 0.9 fusion.47
  84.2 11.4 %attend_part.3 = (f32[48,1152]{1,0:T(8,128)}, bf16[128,1152,128]{2,1,0:T(8,128)(2,1)}, bf16[128,1152,128]{2,1,0:T(8,128)(2,1)}) custom-call(s32[1]{0:T(128)} %bitcast.qi, s32[128]{0:T(128)} %len_s.11, f32[48,1152]{1,0:T(8,128)} %get-tuple-element.85.q_ref, bf16[48,1152]{1,0:T(8,128)(2,1)} %get-tuple-element.84.kr_ref, ...), custom_call_target="tpu_custom_call", output_to_operand_aliasing={{1}: (7, {}), {2}: (8, {})} | custom-call | flops 1207959552 | bytes 18874368 | tf_op jit(solution)/shard_map/attend_part/pallas_call | solution.py:193
  95.6 1.1 convert_element_type.343
  96.7 1.0 convert_bitcast_fusion.1
  98.2 1.5 collective-permute-start.2
  99.7 3.3 collective-permute-done.7
  103.1 1.1 collective-permute-done.2
  105.3 1.5 collective-permute-start.9
  108.1 6.1 %collective-permute-done.9 = bf16[192,576]{1,0:T(8,128)(2,1)S(1)} collective-permute-done((bf16[192,576]{1,0:T(8,128)(2,1)S(1)}, bf16[192,576]{1,0:T(8,128)(2,1)S(1)}, u32[]{:S(2)}, u32[]{:S(2)}) %collective-permute-start.9) | collective-permute-done | bytes 221216 | tf_op jit(solution)/shard_map/ppermute | solution.py:576
  114.2 4.5 %collective-permute-done.4 = bf16[192,576]{1,0:T(8,128)(2,1)S(1)} collective-permute-done((bf16[192,576]{1,0:T(8,128)(2,1)S(1)}, bf16[192,576]{1,0:T(8,128)(2,1)S(1)}, u32[]{:S(2)}, u32[]{:S(2)}) %collective-permute-start.4) | collective-permute-done | bytes 221216 | tf_op jit(solution)/shard_map/ppermute | solution.py:576
  120.6 5.5 %share_small.1 = f32[4,4,16,96]{3,2,1,0:T(8,128)} custom-call(f32[4,16,96]{2,1,0:T(8,128)} %bitcast.326), custom_call_target="tpu_custom_call" | custom-call | bytes 8000000 | tf_op jit(solution)/shard_map/share_small/pallas_call | solution.py:452
  126.1 0.9 slice_bitcast_fusion.22
  128.4 1.8 convolution_convert_fusion.3.x_ref
  130.2 21.9 %up_experts.3 = (bf16[2,2,768,512]{3,2,1,0:T(8,128)(2,1)}, bf16[2,2,768,512]{3,2,1,0:T(8,128)(2,1)}) custom-call(s32[4]{0:T(128)} %get-tuple-element.137.rel_s, s32[9]{0:T(128)} %pad_add_fusion.1.off_s, bf16[768,576]{1,0:T(8,128)(2,1)} %convolution_convert_fusion.3.x_ref, bf16[8,576,2880]{2,1,0:T(8,128)(2,1)} %refs_7_.3, bf16[8,576,2880]{2,1,0:T(8,128)(2,1)} %refs_7_.3, ...), custom_call_target="tpu_custom_call" | custom-call | flops 9663676416 | bytes 56623104 | tf_op jit(solution)/shard_map/up_experts/pallas_call | solution.py:304
  152.3 0.9 broadcast_in_dim_reshape.6.refs_5_
  153.2 0.9 broadcast_in_dim_reshape.14.refs_6_
  154.2 0.7 gather_fusion.2
  155.1 0.7 gather_fusion.1
  157.9 10.5 %collective-permute-done.19 = bf16[96,2304]{1,0:T(8,128)(2,1)S(1)} collective-permute-done((bf16[96,2304]{1,0:T(8,128)(2,1)S(1)}, bf16[96,2304]{1,0:T(8,128)(2,1)S(1)}, u32[]{:S(2)}, u32[]{:S(2)}) %collective-permute-start.19) | collective-permute-done | bytes 442400 | tf_op jit(solution)/shard_map/ppermute | solution.py:474
  168.4 1.0 pad_maximum_fusion.3
  169.4 14.3 %up_experts.2 = (bf16[2,2,768,256]{3,2,1,0:T(8,128)(2,1)}, bf16[2,2,768,256]{3,2,1,0:T(8,128)(2,1)}) custom-call(s32[4]{0:T(128)} %get-tuple-element.137.rel_s, s32[9]{0:T(128)} %pad_add_fusion.1.off_s, bf16[768,576]{1,0:T(8,128)(2,1)} %convolution_convert_fusion.3.x_ref, bf16[8,576,2880]{2,1,0:T(8,128)(2,1)} %refs_7_.3, bf16[8,576,2880]{2,1,0:T(8,128)(2,1)} %refs_7_.3, ...), custom_call_target="tpu_custom_call" | custom-call | flops 4831838208 | bytes 28311552 | tf_op jit(solution)/shard_map/up_experts/pallas_call | solution.py:304
  184.2 2.0 fusion.3
  186.8 0.8 fusion.83
  188.4 1.4 collective-permute-start.11
  189.9 33.6 %collective-permute-done.15 = bf16[2,768,512]{2,1,0:T(8,128)(2,1)S(1)} collective-permute-done((bf16[2,768,512]{2,1,0:T(8,128)(2,1)S(1)}, bf16[2,768,512]{2,1,0:T(8,128)(2,1)S(1)}, u32[]{:S(2)}, u32[]{:S(2)}) %collective-permute-start.15) | collective-permute-done | bytes 1572896 | tf_op jit(solution)/shard_map/ppermute | solution.py:474
  223.5 2.0 fusion.4
  226.6 1.2 slice_bitcast_fusion
  227.8 12.5 %collective-permute-done.11 = bf16[2,768,256]{2,1,0:T(8,128)(2,1)S(1)} collective-permute-done((bf16[2,768,256]{2,1,0:T(8,128)(2,1)S(1)}, bf16[2,768,256]{2,1,0:T(8,128)(2,1)S(1)}, u32[]{:S(2)}, u32[]{:S(2)}) %collective-permute-start.11) | collective-permute-done | bytes 786464 | tf_op jit(solution)/shard_map/ppermute | solution.py:474
  241.0 15.3 %collective-permute-done.16.near_ref = bf16[768,512]{1,0:T(8,128)(2,1)S(1)} collective-permute-done((bf16[768,512]{1,0:T(8,128)(2,1)S(1)}, bf16[768,512]{1,0:T(8,128)(2,1)S(1)}, u32[]{:S(2)}, u32[]{:S(2)}) %collective-permute-start.16) | collective-permute-done | bytes 786464 | tf_op jit(solution)/shard_map/ppermute | solution.py:474
  256.3 1.4 pad_maximum_fusion.1
  258.7 0.8 fusion.82
  259.7 9.8 %collective-permute-done.12.near_ref = bf16[768,256]{1,0:T(8,128)(2,1)S(1)} collective-permute-done((bf16[768,256]{1,0:T(8,128)(2,1)S(1)}, bf16[768,256]{1,0:T(8,128)(2,1)S(1)}, u32[]{:S(2)}, u32[]{:S(2)}) %collective-permute-start.12) | collective-permute-done | bytes 393248 | tf_op jit(solution)/shard_map/ppermute | solution.py:474
  269.7 0.8 fusion.81
  270.5 15.7 %copy_part.4 = (bf16[128,1152,128]{2,1,0:T(8,128)(2,1)}, bf16[128,1152,128]{2,1,0:T(8,128)(2,1)}) custom-call(s32[1]{0:T(128)} %bitcast.97.qi, s32[128]{0:T(128)} %len_s.11, bf16[96,1152]{1,0:T(8,128)(2,1)} %get-tuple-element.89.kr_ref, bf16[96,1152]{1,0:T(8,128)(2,1)} %get-tuple-element.88.vr_ref, ...), custom_call_target="tpu_custom_call", output_to_operand_aliasing={{0}: (6, {}), {1}: (7, {})} | custom-call | flops 2415919104 | bytes 56623104 | tf_op jit(solution)/shard_map/copy_part/pallas_call | solution.py:234
  286.2 1.2 copy-done.12
  287.4 16.5 %down_experts.2.refs_4_ = f32[768,576]{1,0:T(8,128)} custom-call(s32[4]{0:T(128)} %get-tuple-element.137.rel_s, s32[9]{0:T(128)} %pad_add_fusion.1.off_s, bf16[768,512]{1,0:T(8,128)(2,1)} %copy-done.6, bf16[768,512]{1,0:T(8,128)(2,1)} %copy-done.7, bf16[2,768,512]{2,1,0:T(8,128)(2,1)} %copy-done.12, bf16[8,576,2880]{2,1,0:T(8,128)(2,1)} %bitcast.279, ...), custom_call_target="tpu_custom_call" | custom-call | flops 4831838208 | bytes 37748736 | tf_op jit(solution)/shard_map/down_experts/pallas_call | solution.py:380
  303.9 0.9 copy-done.23
  304.8 13.0 %down_experts.3 = bf16[384,576]{1,0:T(8,128)(2,1)} custom-call(s32[4]{0:T(128)} %get-tuple-element.137.rel_s, s32[9]{0:T(128)} %pad_add_fusion.1.off_s, bf16[768,256]{1,0:T(8,128)(2,1)} %copy-done.15, bf16[768,256]{1,0:T(8,128)(2,1)} %copy-done.14, bf16[2,768,256]{2,1,0:T(8,128)(2,1)} %copy-done.23, bf16[8,576,2880]{2,1,0:T(8,128)(2,1)} %bitcast.287, ...), custom_call_target="tpu_custom_call" | custom-call | flops 2415919104 | bytes 18874368 | tf_op jit(solution)/shard_map/down_experts/pallas_call | solution.py:380
  317.8 1.5 collective-permute-start.18
  319.3 15.5 %copy_part.5 = (bf16[128,1152,128]{2,1,0:T(8,128)(2,1)}, bf16[128,1152,128]{2,1,0:T(8,128)(2,1)}) custom-call(s32[1]{0:T(128)} %bitcast.93.qi, s32[128]{0:T(128)} %len_s.11, bf16[96,1152]{1,0:T(8,128)(2,1)} %get-tuple-element.91.kr_ref, bf16[96,1152]{1,0:T(8,128)(2,1)} %get-tuple-element.90.vr_ref, ...), custom_call_target="tpu_custom_call", output_to_operand_aliasing={{0}: (6, {}), {1}: (7, {})} | custom-call | flops 2415919104 | bytes 56623104 | tf_op jit(solution)/shard_map/copy_part/pallas_call | solution.py:234
  334.7 9.8 %copy_part.6 = (bf16[128,1152,128]{2,1,0:T(8,128)(2,1)}, bf16[128,1152,128]{2,1,0:T(8,128)(2,1)}) custom-call(s32[1]{0:T(128)} %bitcast.87.qi, s32[128]{0:T(128)} %len_s.11, bf16[96,1152]{1,0:T(8,128)(2,1)} %get-tuple-element.93.kr_ref, bf16[96,1152]{1,0:T(8,128)(2,1)} %get-tuple-element.92.vr_ref, ...), custom_call_target="tpu_custom_call", output_to_operand_aliasing={{0}: (6, {}), {1}: (7, {})} | custom-call | flops 1207959552 | bytes 28311552 | tf_op jit(solution)/shard_map/copy_part/pallas_call | solution.py:234
  344.5 9.9 %copy_part.7 = (bf16[128,1152,128]{2,1,0:T(8,128)(2,1)}, bf16[128,1152,128]{2,1,0:T(8,128)(2,1)}) custom-call(s32[1]{0:T(128)} %bitcast.87.qi, s32[128]{0:T(128)} %len_s.11, bf16[96,1152]{1,0:T(8,128)(2,1)} %get-tuple-element.93.kr_ref, bf16[96,1152]{1,0:T(8,128)(2,1)} %get-tuple-element.92.vr_ref, ...), custom_call_target="tpu_custom_call", output_to_operand_aliasing={{0}: (6, {}), {1}: (7, {})} | custom-call | flops 1207959552 | bytes 28311552 | tf_op jit(solution)/shard_map/copy_part/pallas_call | solution.py:234
  354.6 0.9 gather_fusion.5
  355.6 1.0 copy.106
  (234 shorter events, 25.6 us)
Async XLA Ops:
  0.6 38.2 %copy-start = (bf16[576,1152]{1,0:T(8,128)(2,1)S(1)}, bf16[576,1152]{1,0:T(8,128)(2,1)}, u32[]{:S(2)}) copy-start(bf16[576,1152]{1,0:T(8,128)(2,1)} %param.26) | copy-start | bytes 3981316
  3.0 19.4 %copy-start.47 = (bf16[576]{0:T(1024)(128)(2,1)S(1)}, bf16[576]{0:T(1024)(128)(2,1)}, u32[]{:S(2)}) copy-start(bf16[576]{0:T(1024)(128)(2,1)} %param.23) | copy-start | bytes 3460
  43.7 1.5 copy-start.37
  43.7 1.6 copy-start.2
  43.7 2.2 copy-start.38
  43.7 7.3 %collective-permute-start.5 = (bf16[2,48,3456]{2,1,0:T(8,128)(2,1)}, bf16[2,48,3456]{2,1,0:T(8,128)(2,1)}, u32[]{:S(2)}, u32[]{:S(2)}) collective-permute-start(bf16[2,48,3456]{2,1,0:T(8,128)(2,1)} %bitcast.29), channel_id=1, source_target_pairs={{0,1},{1,0},{2,3},{3,2},{4,5},{5,4},{6,7},{7,6}} | collective-permute-start | bytes 1990664 | tf_op jit(solution)/shard_map/ppermute | solution.py:471
  43.8 8.8 %collective-permute-start = (bf16[2,48,3456]{2,1,0:T(8,128)(2,1)}, bf16[2,48,3456]{2,1,0:T(8,128)(2,1)}, u32[]{:S(2)}, u32[]{:S(2)}) collective-permute-start(bf16[2,48,3456]{2,1,0:T(8,128)(2,1)} %bitcast.13), channel_id=1, source_target_pairs={{0,1},{1,0},{2,3},{3,2},{4,5},{5,4},{6,7},{7,6}} | collective-permute-start | bytes 1990664 | tf_op jit(solution)/shard_map/ppermute | solution.py:471
  47.3 2.9 copy-start.40
  48.9 2.0 copy-start.48
  50.0 3.7 %copy-start.32 = (s32[4,3,32]{2,1,0:T(4,128)}, s32[4,3,32]{2,1,0:T(4,128)S(1)}, u32[]{:S(2)}) copy-start(s32[4,3,32]{2,1,0:T(4,128)S(1)} %gather_fusion.3) | copy-start | bytes 4612
  50.1 78.2 %copy-start.43 = (s32[384]{0:T(512)}, s32[384]{0:T(512)S(1)}, u32[]{:S(2)}) copy-start(s32[384]{0:T(512)S(1)} %eq.93) | copy-start | bytes 4612
  50.8 2.9 copy-start.34
  50.9 77.5 %copy-start.45 = (s32[384]{0:T(512)}, s32[384]{0:T(512)S(1)}, u32[]{:S(2)}) copy-start(s32[384]{0:T(512)S(1)} %eq.81) | copy-start | bytes 4612
  50.9 11.9 %copy-start.17 = (bf16[1,3,1,16,3456]{4,3,2,1,0:T(8,128)(2,1)S(1)}, bf16[1,3,1,16,3456]{4,3,2,1,0:T(8,128)(2,1)}, u32[]{:S(2)}) copy-start(bf16[1,3,1,16,3456]{4,3,2,1,0:T(8,128)(2,1)} %get-tuple-element.77) | copy-start | bytes 995332
  52.1 10.7 %collective-permute-start.6 = (bf16[48,3456]{1,0:T(8,128)(2,1)S(1)}, bf16[48,3456]{1,0:T(8,128)(2,1)S(1)}, u32[]{:S(2)}, u32[]{:S(2)}) collective-permute-start(bf16[48,3456]{1,0:T(8,128)(2,1)S(1)} %fusion.34), channel_id=1, source_target_pairs={{0,2},{2,0},{1,3},{3,1},{4,6},{6,4},{5,7},{7,5}} | collective-permute-start | bytes 995336 | tf_op jit(solution)/shard_map/ppermute | solution.py:474
  53.7 15.3 %collective-permute-start.1 = (bf16[48,3456]{1,0:T(8,128)(2,1)S(1)}, bf16[48,3456]{1,0:T(8,128)(2,1)S(1)}, u32[]{:S(2)}, u32[]{:S(2)}) collective-permute-start(bf16[48,3456]{1,0:T(8,128)(2,1)S(1)} %fusion.36), channel_id=1, source_target_pairs={{0,2},{2,0},{1,3},{3,1},{4,6},{6,4},{5,7},{7,5}} | collective-permute-start | bytes 995336 | tf_op jit(solution)/shard_map/ppermute | solution.py:474
  63.9 5.1 %copy-start.16 = (bf16[1,3,1,16,3456]{4,3,2,1,0:T(8,128)(2,1)S(1)}, bf16[1,3,1,16,3456]{4,3,2,1,0:T(8,128)(2,1)}, u32[]{:S(2)}) copy-start(bf16[1,3,1,16,3456]{4,3,2,1,0:T(8,128)(2,1)} %get-tuple-element.76) | copy-start | bytes 995332
  84.2 14.0 %copy-start.22 = (f32[48,1152]{1,0:T(8,128)S(1)}, f32[48,1152]{1,0:T(8,128)}, u32[]{:S(2)}) copy-start(f32[48,1152]{1,0:T(8,128)} %get-tuple-element.34) | copy-start | bytes 663556
  95.6 9.0 %copy-start.4 = (bf16[1152,576]{0,1:T(8,128)(2,1)S(1)}, bf16[1152,576]{0,1:T(8,128)(2,1)}, u32[]{:S(2)}) copy-start(bf16[1152,576]{0,1:T(8,128)(2,1)} %param.27) | copy-start | bytes 3981316
  97.6 5.4 %collective-permute-start.7 = (bf16[48,1152]{1,0:T(8,128)(2,1)S(1)}, bf16[48,1152]{1,0:T(8,128)(2,1)S(1)}, u32[]{:S(2)}, u32[]{:S(2)}) collective-permute-start(bf16[48,1152]{1,0:T(8,128)(2,1)S(1)} %convert_element_type.343), channel_id=1, source_target_pairs={{0,2},{2,0},{1,3},{3,1},{4,6},{6,4},{5,7},{7,5}} | collective-permute-start | bytes 331784 | tf_op jit(solution)/shard_map/ppermute | solution.py:474
  98.2 6.0 %collective-permute-start.2 = (bf16[48,1152]{1,0:T(8,128)(2,1)S(1)}, bf16[48,1152]{1,0:T(8,128)(2,1)S(1)}, u32[]{:S(2)}, u32[]{:S(2)}) collective-permute-start(bf16[48,1152]{1,0:T(8,128)(2,1)S(1)} %convert_element_type.322), channel_id=1, source_target_pairs={{0,2},{2,0},{1,3},{3,1},{4,6},{6,4},{5,7},{7,5}} | collective-permute-start | bytes 331784 | tf_op jit(solution)/shard_map/ppermute | solution.py:474
  103.1 1.5 collective-permute-start.8
  104.3 2.5 collective-permute-start.3
  105.3 8.8 %collective-permute-start.9 = (bf16[192,576]{1,0:T(8,128)(2,1)S(1)}, bf16[192,576]{1,0:T(8,128)(2,1)S(1)}, u32[]{:S(2)}, u32[]{:S(2)}) collective-permute-start(bf16[192,576]{1,0:T(8,128)(2,1)S(1)} %convolution_convert_fusion.4), channel_id=1, source_target_pairs={{0,4},{4,0},{1,5},{5,1},{2,6},{6,2},{3,7},{7,3}} | collective-permute-start | bytes 663560 | tf_op jit(solution)/shard_map/ppermute | solution.py:576
  107.5 11.2 %collective-permute-start.4 = (bf16[192,576]{1,0:T(8,128)(2,1)S(1)}, bf16[192,576]{1,0:T(8,128)(2,1)S(1)}, u32[]{:S(2)}, u32[]{:S(2)}) collective-permute-start(bf16[192,576]{1,0:T(8,128)(2,1)S(1)} %convolution_convert_fusion.5), channel_id=1, source_target_pairs={{0,4},{4,0},{1,5},{5,1},{2,6},{6,2},{3,7},{7,3}} | collective-permute-start | bytes 663560 | tf_op jit(solution)/shard_map/ppermute | solution.py:576
  114.2 4.6 %copy-start.5 = (bf16[2,192,576]{2,1,0:T(8,128)(2,1)S(1)}, bf16[2,192,576]{2,1,0:T(8,128)(2,1)}, u32[]{:S(2)}) copy-start(bf16[2,192,576]{2,1,0:T(8,128)(2,1)} %get-tuple-element.30) | copy-start | bytes 1327108
  119.0 9.4 %copy-start.10 = (bf16[384,576]{1,0:T(8,128)(2,1)}, bf16[384,576]{1,0:T(8,128)(2,1)S(1)}, u32[]{:S(2)}) copy-start(bf16[384,576]{1,0:T(8,128)(2,1)S(1)} %fusion.22) | copy-start | bytes 1327108
  128.4 1.8 copy-start.41
  130.2 22.1 %copy-start.35 = (s32[4,3,32]{2,1,0:T(4,128)S(1)}, s32[4,3,32]{2,1,0:T(4,128)}, u32[]{:S(2)}) copy-start(s32[4,3,32]{2,1,0:T(4,128)} %copy-done.34) | copy-start | bytes 4612
  130.2 23.0 %copy-start.33 = (s32[4,3,32]{2,1,0:T(4,128)S(1)}, s32[4,3,32]{2,1,0:T(4,128)}, u32[]{:S(2)}) copy-start(s32[4,3,32]{2,1,0:T(4,128)} %copy-done.32) | copy-start | bytes 4612
  130.2 23.9 %copy-start.39 = (s32[3,128,2]{1,2,0:T(2,128)S(1)}, s32[3,128,2]{1,2,0:T(2,128)}, u32[]{:S(2)}) copy-start(s32[3,128,2]{1,2,0:T(2,128)} %param.19) | copy-start | bytes 9220
  130.2 25.7 %copy-start.18 = (bf16[48,1152]{1,0:T(8,128)(2,1)S(1)}, bf16[48,1152]{1,0:T(8,128)(2,1)}, u32[]{:S(2)}) copy-start(bf16[48,1152]{1,0:T(8,128)(2,1)} %slice.463.vr_ref) | copy-start | bytes 331780
  130.2 25.7 %copy-start.19 = (bf16[48,1152]{1,0:T(8,128)(2,1)S(1)}, bf16[48,1152]{1,0:T(8,128)(2,1)}, u32[]{:S(2)}) copy-start(bf16[48,1152]{1,0:T(8,128)(2,1)} %get-tuple-element.84.kr_ref) | copy-start | bytes 331780
  130.2 25.7 %copy-start.20 = (bf16[48,1152]{1,0:T(8,128)(2,1)S(1)}, bf16[48,1152]{1,0:T(8,128)(2,1)}, u32[]{:S(2)}) copy-start(bf16[48,1152]{1,0:T(8,128)(2,1)} %slice.445.vr_ref) | copy-start | bytes 331780
  130.2 25.7 %copy-start.21 = (bf16[48,1152]{1,0:T(8,128)(2,1)S(1)}, bf16[48,1152]{1,0:T(8,128)(2,1)}, u32[]{:S(2)}) copy-start(bf16[48,1152]{1,0:T(8,128)(2,1)} %get-tuple-element.82.kr_ref) | copy-start | bytes 331780
  152.1 4.5 %copy-start.3 = (s32[4]{0:T(128)S(1)}, s32[4]{0:T(128)}, u32[]{:S(2)}) copy-start(s32[4]{0:T(128)} %constant.77.clone) | copy-start | bytes 52
  152.1 32.0 %collective-permute-start.14 = (bf16[2,2,768,512]{3,2,1,0:T(8,128)(2,1)}, bf16[2,2,768,512]{3,2,1,0:T(8,128)(2,1)}, u32[]{:S(2)}, u32[]{:S(2)}) collective-permute-start(bf16[2,2,768,512]{3,2,1,0:T(8,128)(2,1)} %get-tuple-element.42), channel_id=1, source_target_pairs={{0,1},{1,0},{2,3},{3,2},{4,5},{5,4},{6,7},{7,6}} | collective-permute-start | bytes 9437192 | tf_op jit(solution)/shard_map/ppermute | solution.py:471
  156.0 12.4 %collective-permute-start.19 = (bf16[96,2304]{1,0:T(8,128)(2,1)S(1)}, bf16[96,2304]{1,0:T(8,128)(2,1)S(1)}, u32[]{:S(2)}, u32[]{:S(2)}) collective-permute-start(bf16[96,2304]{1,0:T(8,128)(2,1)S(1)} %bitcast.315), channel_id=1, source_target_pairs={{0,2},{2,0},{1,3},{3,1},{4,6},{6,4},{5,7},{7,5}} | collective-permute-start | bytes 1327112 | tf_op jit(solution)/shard_map/ppermute | solution.py:474
  169.4 14.7 %copy-start.8 = (bf16[2,2,768,512]{3,2,1,0:T(8,128)(2,1)S(1)}, bf16[2,2,768,512]{3,2,1,0:T(8,128)(2,1)}, u32[]{:S(2)}) copy-start(bf16[2,2,768,512]{3,2,1,0:T(8,128)(2,1)} %get-tuple-element.41) | copy-start | bytes 9437188
  169.4 57.2 %collective-permute-start.20 = (bf16[2,96,2304]{2,1,0:T(8,128)(2,1)}, bf16[2,96,2304]{2,1,0:T(8,128)(2,1)}, u32[]{:S(2)}, u32[]{:S(2)}) collective-permute-start(bf16[2,96,2304]{2,1,0:T(8,128)(2,1)} %pad_maximum_fusion.3), channel_id=1, source_target_pairs={{0,1},{1,0},{2,3},{3,2},{4,5},{5,4},{6,7},{7,6}} | collective-permute-start | bytes 2654216 | tf_op jit(solution)/shard_map/ppermute | solution.py:471
  183.7 4.5 %collective-permute-start.10 = (bf16[2,2,768,256]{3,2,1,0:T(8,128)(2,1)}, bf16[2,2,768,256]{3,2,1,0:T(8,128)(2,1)S(1)}, u32[]{:S(2)}, u32[]{:S(2)}) collective-permute-start(bf16[2,2,768,256]{3,2,1,0:T(8,128)(2,1)} %get-tuple-element.40), channel_id=1, source_target_pairs={{0,1},{1,0},{2,3},{3,2},{4,5},{5,4},{6,7},{7,6}} | collective-permute-start | bytes 4718600 | tf_op jit(solution)/shard_map/ppermute | solution.py:471
  184.1 3.5 copy-start.36
  184.1 3.5 copy-start.42
  184.1 3.5 copy-start.25
  184.1 3.5 copy-start.27
  184.1 3.5 copy-start.29
  184.2 3.5 copy-start.31
  184.2 3.7 %copy-start.44 = (s32[384]{0:T(512)S(1)}, s32[384]{0:T(512)}, u32[]{:S(2)}) copy-start(s32[384]{0:T(512)} %copy-done.43) | copy-start | bytes 4612
  184.2 3.7 %copy-start.46 = (s32[384]{0:T(512)S(1)}, s32[384]{0:T(512)}, u32[]{:S(2)}) copy-start(s32[384]{0:T(512)} %copy-done.45) | copy-start | bytes 4612
  184.2 4.0 %copy-start.13 = (bf16[2,2,768,256]{3,2,1,0:T(8,128)(2,1)S(1)}, bf16[2,2,768,256]{3,2,1,0:T(8,128)(2,1)}, u32[]{:S(2)}) copy-start(bf16[2,2,768,256]{3,2,1,0:T(8,128)(2,1)} %get-tuple-element.39) | copy-start | bytes 4718596
  186.2 37.3 %collective-permute-start.15 = (bf16[2,768,512]{2,1,0:T(8,128)(2,1)S(1)}, bf16[2,768,512]{2,1,0:T(8,128)(2,1)S(1)}, u32[]{:S(2)}, u32[]{:S(2)}) collective-permute-start(bf16[2,768,512]{2,1,0:T(8,128)(2,1)S(1)} %fusion.3), channel_id=1, source_target_pairs={{0,2},{2,0},{1,3},{3,1},{4,6},{6,4},{5,7},{7,5}} | collective-permute-start | bytes 4718600 | tf_op jit(solution)/shard_map/ppermute | solution.py:474
  188.4 51.9 %collective-permute-start.11 = (bf16[2,768,256]{2,1,0:T(8,128)(2,1)S(1)}, bf16[2,768,256]{2,1,0:T(8,128)(2,1)S(1)}, u32[]{:S(2)}, u32[]{:S(2)}) collective-permute-start(bf16[2,768,256]{2,1,0:T(8,128)(2,1)S(1)} %fusion.27), channel_id=1, source_target_pairs={{0,2},{2,0},{1,3},{3,1},{4,6},{6,4},{5,7},{7,5}} | collective-permute-start | bytes 2359304 | tf_op jit(solution)/shard_map/ppermute | solution.py:474
  225.9 14.6 %copy-start.6 = (bf16[768,512]{1,0:T(8,128)(2,1)}, bf16[768,512]{1,0:T(8,128)(2,1)S(1)}, u32[]{:S(2)}) copy-start(bf16[768,512]{1,0:T(8,128)(2,1)S(1)} %fusion.6.own_ref) | copy-start | bytes 2359300
  226.0 30.3 %collective-permute-start.16 = (bf16[768,512]{1,0:T(8,128)(2,1)S(1)}, bf16[768,512]{1,0:T(8,128)(2,1)S(1)}, u32[]{:S(2)}, u32[]{:S(2)}) collective-permute-start(bf16[768,512]{1,0:T(8,128)(2,1)S(1)} %fusion.6.own_ref), channel_id=1, source_target_pairs={{0,2},{2,0},{1,3},{3,1},{4,6},{6,4},{5,7},{7,5}} | collective-permute-start | bytes 2359304 | tf_op jit(solution)/shard_map/ppermute | solution.py:474
  256.3 1.4 copy-start.7
  257.7 28.5 %collective-permute-start.17 = (bf16[2,768,512]{2,1,0:T(8,128)(2,1)}, bf16[2,768,512]{2,1,0:T(8,128)(2,1)S(1)}, u32[]{:S(2)}, u32[]{:S(2)}) collective-permute-start(bf16[2,768,512]{2,1,0:T(8,128)(2,1)} %pad_maximum_fusion.1), channel_id=1, source_target_pairs={{0,1},{1,0},{2,3},{3,2},{4,5},{5,4},{6,7},{7,6}} | collective-permute-start | bytes 4718600 | tf_op jit(solution)/shard_map/ppermute | solution.py:471
  258.0 11.6 %copy-start.15 = (bf16[768,256]{1,0:T(8,128)(2,1)}, bf16[768,256]{1,0:T(8,128)(2,1)S(1)}, u32[]{:S(2)}) copy-start(bf16[768,256]{1,0:T(8,128)(2,1)S(1)} %fusion.29.own_ref) | copy-start | bytes 1179652
  258.0 11.5 %collective-permute-start.12 = (bf16[768,256]{1,0:T(8,128)(2,1)S(1)}, bf16[768,256]{1,0:T(8,128)(2,1)S(1)}, u32[]{:S(2)}, u32[]{:S(2)}) collective-permute-start(bf16[768,256]{1,0:T(8,128)(2,1)S(1)} %fusion.29.own_ref), channel_id=1, source_target_pairs={{0,2},{2,0},{1,3},{3,1},{4,6},{6,4},{5,7},{7,5}} | collective-permute-start | bytes 1179656 | tf_op jit(solution)/shard_map/ppermute | solution.py:474
  269.5 16.7 %copy-start.14 = (bf16[768,256]{1,0:T(8,128)(2,1)}, bf16[768,256]{1,0:T(8,128)(2,1)S(1)}, u32[]{:S(2)}) copy-start(bf16[768,256]{1,0:T(8,128)(2,1)S(1)} %collective-permute-done.12.near_ref) | copy-start | bytes 1179652
  269.6 34.3 %collective-permute-start.13 = (bf16[2,768,256]{2,1,0:T(8,128)(2,1)S(1)}, bf16[2,768,256]{2,1,0:T(8,128)(2,1)S(1)}, u32[]{:S(2)}, u32[]{:S(2)}) collective-permute-start(bf16[2,768,256]{2,1,0:T(8,128)(2,1)S(1)} %pad_maximum_fusion.4), channel_id=1, source_target_pairs={{0,1},{1,0},{2,3},{3,2},{4,5},{5,4},{6,7},{7,6}} | collective-permute-start | bytes 2359304 | tf_op jit(solution)/shard_map/ppermute | solution.py:471
  317.8 36.6 %collective-permute-start.18 = (bf16[384,576]{1,0:T(8,128)(2,1)}, bf16[384,576]{1,0:T(8,128)(2,1)S(1)}, u32[]{:S(2)}, u32[]{:S(2)}) collective-permute-start(bf16[384,576]{1,0:T(8,128)(2,1)} %down_experts.3), channel_id=1, source_target_pairs={{0,4},{4,0},{1,5},{5,1},{2,6},{6,2},{3,7},{7,3}} | collective-permute-start | bytes 1327112 | tf_op jit(solution)/shard_map/ppermute | solution.py:576
  344.5 9.9 %copy-start.9 = (bf16[384,576]{1,0:T(8,128)(2,1)S(1)}, bf16[384,576]{1,0:T(8,128)(2,1)}, u32[]{:S(2)}) copy-start(bf16[384,576]{1,0:T(8,128)(2,1)} %down_experts.3) | copy-start | bytes 1327108
  344.5 9.9 %copy-start.11 = (bf16[384,576]{1,0:T(8,128)(2,1)S(1)}, bf16[384,576]{1,0:T(8,128)(2,1)}, u32[]{:S(2)}) copy-start(bf16[384,576]{1,0:T(8,128)(2,1)} %copy-done.10) | copy-start | bytes 1327108
  354.4 2.1 copy-start.1
  (9 other events, 8.8 us)
